TPU v7x, 32 devices: a whole 2x2x4 slice. The times are simulated.
32 devices in a mesh: fsdp: 8 (over z, y), seq: 4 (over x, core).
Axes of the slice: x: 2, y: 2, z: 4, core: 2. Of those that a mesh axis runs over, the one named last changes fastest.
Arguments:
- tokens: bfloat16 [8, 1024, 768], P('fsdp', 'seq'), may hold values from -6 to 6
- condition: bfloat16 [8, 768], P('fsdp'), may hold values from -6 to 6
- ada_weight: bfloat16 [2, 768, 4608], P(None, 'fsdp'), may hold values from -0.21875 to 0.21875
- ada_bias: bfloat16 [2, 4608], P(None, 'fsdp'), may hold values from -3 to 3
- qkv_weight: bfloat16 [2, 768, 2304], P(None, 'fsdp'), may hold values from -0.21875 to 0.21875
- qv_bias: bfloat16 [2, 1536], P(None, 'fsdp'), may hold values from -3 to 3
- out_weight: bfloat16 [2, 768, 768], P(None, 'fsdp'), may hold values from -1.25 to 1.25
- out_bias: bfloat16 [2, 768], P(None, 'fsdp'), may hold values from -3 to 3
- up_weight: bfloat16 [2, 768, 3072], P(None, 'fsdp'), may hold values from -0.21875 to 0.21875
- up_bias: bfloat16 [2, 3072], P(None, 'fsdp'), may hold values from -3 to 3
- down_weight: bfloat16 [2, 3072, 768], P(None, 'fsdp'), may hold values from -0.109375 to 0.109375
- down_bias: bfloat16 [2, 768], P(None, 'fsdp'), may hold values from -3 to 3
- cotangent: bfloat16 [8, 1024, 768], P('fsdp', 'seq'), may hold values from -6 to 6
Outputs:
- block_out: bfloat16 [8, 1024, 768], P('fsdp', 'seq')
- grad_tokens: float32 [8, 1024, 768], P('fsdp', 'seq')
- grad_condition: float32 [8, 768], P('fsdp')
- grad_ada_weight: float32 [2, 768, 4608], P(None, 'fsdp')
- grad_ada_bias: float32 [2, 4608], P(None, 'fsdp')
- grad_qkv_weight: float32 [2, 768, 2304], P(None, 'fsdp')
- grad_qv_bias: float32 [2, 1536], P(None, 'fsdp')
- grad_out_weight: float32 [2, 768, 768], P(None, 'fsdp')
- grad_out_bias: float32 [2, 768], P(None, 'fsdp')
- grad_up_weight: float32 [2, 768, 3072], P(None, 'fsdp')
- grad_up_bias: float32 [2, 3072], P(None, 'fsdp')
- grad_down_weight: float32 [2, 3072, 768], P(None, 'fsdp')
- grad_down_bias: float32 [2, 768], P(None, 'fsdp')
All inputs are finite; a program needn't handle non-finite values.
Results may differ from a plain program's by a relative error of at most 0.017.
The roundings to bfloat16 on the way count: a program that leaves them out, or rounds other values in their place, can miss the bound.
Values may be sent and summed in bfloat16 or wider, within the bound.
A program may use at most 256 MiB of HBM per device.

v0:
```python
import jax
import jax.numpy as jnp
from jax import lax
from jax.sharding import PartitionSpec as P

HEAD_DIM = 64


epsilon = 1e-06
highest = lax.Precision.HIGHEST


def normalize(values):
    centred = values - jnp.mean(values, axis=-1, keepdims=True)
    inverse = lax.rsqrt(jnp.mean(centred * centred, axis=-1, keepdims=True) + epsilon)
    return (centred * inverse, inverse)


def norm_back(gradient, normed, inverse):
    return inverse * (
        gradient
        - jnp.mean(gradient, axis=-1, keepdims=True)
        - normed * jnp.mean(gradient * normed, axis=-1, keepdims=True)
    )


def linear(values, matrix):
    return jnp.einsum("lsd,dn->lsn", values, matrix, preferred_element_type=jnp.float32)


def linear_back(gradient, matrix):
    return jnp.einsum("lsn,dn->lsd", gradient, matrix, preferred_element_type=jnp.float32)


def weight_grad(values, gradient):
    return jnp.einsum("lsd,lsn->dn", values, gradient, preferred_element_type=jnp.float32)


def column_sums(values):
    return jnp.sum(values, axis=(0, 1), dtype=jnp.float32)


def token_sums(values):
    return jnp.sum(values, axis=1)


def split_heads(rows):
    return rows.reshape(rows.shape[0], rows.shape[1] // HEAD_DIM, HEAD_DIM)


def attend_latent(operands):
    queries, key_rows, value_rows = [split_heads(member) for member in operands]
    scores = jnp.einsum(
        "qhd,khd->hqk", queries, key_rows, preferred_element_type=jnp.float32
    ) * HEAD_DIM ** (-0.5)
    logsum = jnp.log(jnp.sum(jnp.exp(scores), axis=-1, keepdims=True))
    probability = jnp.exp(scores - logsum).astype(jnp.bfloat16)
    output = jnp.einsum("hqk,khd->qhd", probability, value_rows, preferred_element_type=jnp.float32)
    return (output.reshape(output.shape[0], -1).astype(jnp.bfloat16), logsum)


def attend_back(operands):
    queries, key_rows, value_rows, logsum, out_grad = operands
    queries, key_rows, value_rows, out_grad = [
        split_heads(member) for member in (queries, key_rows, value_rows, out_grad)
    ]
    score_scale = HEAD_DIM ** (-0.5)
    scores = (
        jnp.einsum("qhd,khd->hqk", queries, key_rows, preferred_element_type=jnp.float32)
        * score_scale
    )
    probability = jnp.exp(scores - logsum)
    value_grad = jnp.einsum(
        "hqk,qhd->khd",
        probability.astype(jnp.bfloat16),
        out_grad,
        preferred_element_type=jnp.float32,
    )
    prob_grad = jnp.einsum("qhd,khd->hqk", out_grad, value_rows, preferred_element_type=jnp.float32)
    row_inner = jnp.sum(probability * prob_grad, axis=-1, keepdims=True)
    score_grad = (probability * (prob_grad - row_inner)).astype(jnp.bfloat16)
    query_grad = (
        jnp.einsum("hqk,khd->qhd", score_grad, key_rows, preferred_element_type=jnp.float32)
        * score_scale
    )
    key_grad = (
        jnp.einsum("hqk,qhd->khd", score_grad, queries, preferred_element_type=jnp.float32)
        * score_scale
    )
    return tuple(
        (
            member.reshape(member.shape[0], -1).astype(jnp.bfloat16)
            for member in (query_grad, key_grad, value_grad)
        )
    )


def fetch_layer(shards, layer_index):
    (
        ada_weight,
        ada_bias,
        qkv_weight,
        qv_bias,
        out_weight,
        out_bias,
        up_weight,
        up_bias,
        down_weight,
        down_bias,
    ) = shards
    return (
        lax.all_gather(ada_weight[layer_index], "fsdp", axis=0, tiled=True),
        lax.all_gather(ada_bias[layer_index], "fsdp", axis=0, tiled=True),
        lax.all_gather(qkv_weight[layer_index], "fsdp", axis=0, tiled=True),
        lax.all_gather(qv_bias[layer_index], "fsdp", axis=0, tiled=True),
        lax.all_gather(out_weight[layer_index], "fsdp", axis=0, tiled=True),
        lax.all_gather(out_bias[layer_index], "fsdp", axis=0, tiled=True),
        lax.all_gather(up_weight[layer_index], "fsdp", axis=0, tiled=True),
        lax.all_gather(up_bias[layer_index], "fsdp", axis=0, tiled=True),
        lax.all_gather(down_weight[layer_index], "fsdp", axis=0, tiled=True),
        lax.all_gather(down_bias[layer_index], "fsdp", axis=0, tiled=True),
    )


def fetch_again(shards, layer_index):
    (
        ada_weight,
        ada_bias,
        qkv_weight,
        qv_bias,
        out_weight,
        out_bias,
        up_weight,
        up_bias,
        down_weight,
        down_bias,
    ) = shards
    return (
        lax.all_gather(ada_weight[layer_index], "fsdp", axis=0, tiled=True),
        lax.all_gather(ada_bias[layer_index], "fsdp", axis=0, tiled=True),
        lax.all_gather(qkv_weight[layer_index], "fsdp", axis=0, tiled=True),
        lax.all_gather(qv_bias[layer_index], "fsdp", axis=0, tiled=True),
        lax.all_gather(out_weight[layer_index], "fsdp", axis=0, tiled=True),
        lax.all_gather(out_bias[layer_index], "fsdp", axis=0, tiled=True),
        lax.all_gather(up_weight[layer_index], "fsdp", axis=0, tiled=True),
        lax.all_gather(up_bias[layer_index], "fsdp", axis=0, tiled=True),
        lax.all_gather(down_weight[layer_index], "fsdp", axis=0, tiled=True),
        lax.all_gather(down_bias[layer_index], "fsdp", axis=0, tiled=True),
    )


def split_modulation(modulation):
    return [portion[:, None, :] for portion in jnp.split(modulation, 6, axis=-1)]


def forward_layer(hidden, scaled_cond, gathered):
    (
        ada_matrix,
        ada_offset,
        qkv_matrix,
        qv_offset,
        out_matrix,
        out_offset,
        up_matrix,
        up_offset,
        down_matrix,
        down_offset,
    ) = gathered
    model_width = out_matrix.shape[0]
    modulation = jnp.dot(
        scaled_cond, ada_matrix, preferred_element_type=jnp.float32
    ) + ada_offset.astype(jnp.float32)
    shift_attn, scale_attn, gate_attn, shift_mlp, scale_mlp, gate_mlp = split_modulation(modulation)
    normed_attn, inverse_attn = normalize(hidden)
    attn_in = (normed_attn * (1.0 + scale_attn) + shift_attn).astype(jnp.bfloat16)
    qkv_offset = jnp.concatenate(
        [qv_offset[:model_width], jnp.zeros((model_width,), jnp.bfloat16), qv_offset[model_width:]]
    ).astype(jnp.float32)
    projected = (linear(attn_in, qkv_matrix) + qkv_offset).astype(jnp.bfloat16)
    queries, key_rows, value_rows = jnp.split(projected, 3, axis=-1)
    head_query, head_key, head_value = (
        lax.all_to_all(queries, "seq", split_axis=2, concat_axis=1, tiled=True),
        lax.all_to_all(key_rows, "seq", split_axis=2, concat_axis=1, tiled=True),
        lax.all_to_all(value_rows, "seq", split_axis=2, concat_axis=1, tiled=True),
    )
    head_out, logsum = lax.map(attend_latent, (head_query, head_key, head_value))
    token_out = lax.all_to_all(head_out, "seq", split_axis=1, concat_axis=2, tiled=True)
    branch = linear(token_out, out_matrix) + out_offset.astype(jnp.float32)
    middle = hidden + gate_attn * branch
    normed_mlp, inverse_mlp = normalize(middle)
    mlp_in = (normed_mlp * (1.0 + scale_mlp) + shift_mlp).astype(jnp.bfloat16)
    upward = linear(mlp_in, up_matrix) + up_offset.astype(jnp.float32)
    activated = jax.nn.gelu(upward, approximate=True).astype(jnp.bfloat16)
    feed_out = linear(activated, down_matrix) + down_offset.astype(jnp.float32)
    result = middle + gate_mlp * feed_out
    saved_values = (
        modulation,
        normed_attn,
        inverse_attn,
        attn_in,
        head_query,
        head_key,
        head_value,
        logsum,
        token_out,
        branch,
        normed_mlp,
        inverse_mlp,
        mlp_in,
        upward,
        activated,
        feed_out,
    )
    return (result, saved_values)


def backward_layer(gradient, scaled_cond, gathered, saved_values):
    (
        ada_matrix,
        ada_offset,
        qkv_matrix,
        qv_offset,
        out_matrix,
        out_offset,
        up_matrix,
        up_offset,
        down_matrix,
        down_offset,
    ) = gathered
    (
        modulation,
        normed_attn,
        inverse_attn,
        attn_in,
        head_query,
        head_key,
        head_value,
        logsum,
        token_out,
        branch,
        normed_mlp,
        inverse_mlp,
        mlp_in,
        upward,
        activated,
        feed_out,
    ) = saved_values
    shift_attn, scale_attn, gate_attn, shift_mlp, scale_mlp, gate_mlp = split_modulation(modulation)
    feed_grad = (gate_mlp * gradient).astype(jnp.bfloat16)
    grad_gate_mlp = token_sums(gradient * feed_out)
    grad_down = weight_grad(activated, feed_grad)
    grad_down_offset = column_sums(feed_grad)
    act_grad = linear_back(feed_grad, down_matrix)
    unused_value, gelu_back = jax.vjp(lambda values: jax.nn.gelu(values, approximate=True), upward)
    up_grad = gelu_back(act_grad)[0].astype(jnp.bfloat16)
    grad_up = weight_grad(mlp_in, up_grad)
    grad_up_offset = column_sums(up_grad)
    mlp_in_grad = linear_back(up_grad, up_matrix)
    grad_scale_mlp = token_sums(mlp_in_grad * normed_mlp)
    grad_shift_mlp = token_sums(mlp_in_grad)
    middle_grad = gradient + norm_back(mlp_in_grad * (1.0 + scale_mlp), normed_mlp, inverse_mlp)
    branch_grad = (gate_attn * middle_grad).astype(jnp.bfloat16)
    grad_gate_attn = token_sums(middle_grad * branch)
    grad_out = weight_grad(token_out, branch_grad)
    grad_out_offset = column_sums(branch_grad)
    out_grad = linear_back(branch_grad, out_matrix).astype(jnp.bfloat16)
    head_grad = lax.all_to_all(out_grad, "seq", split_axis=2, concat_axis=1, tiled=True)
    query_grad, key_grad, value_grad = lax.map(
        attend_back, (head_query, head_key, head_value, logsum, head_grad)
    )
    token_query, token_key, token_value = (
        lax.all_to_all(query_grad, "seq", split_axis=1, concat_axis=2, tiled=True),
        lax.all_to_all(key_grad, "seq", split_axis=1, concat_axis=2, tiled=True),
        lax.all_to_all(value_grad, "seq", split_axis=1, concat_axis=2, tiled=True),
    )
    projected_grad = jnp.concatenate([token_query, token_key, token_value], axis=-1)
    grad_qkv = weight_grad(attn_in, projected_grad)
    grad_qv_offset = jnp.concatenate([column_sums(token_query), column_sums(token_value)])
    attn_in_grad = linear_back(projected_grad, qkv_matrix)
    grad_scale_attn = token_sums(attn_in_grad * normed_attn)
    grad_shift_attn = token_sums(attn_in_grad)
    hidden_grad = middle_grad + norm_back(
        attn_in_grad * (1.0 + scale_attn), normed_attn, inverse_attn
    )
    modulation_grad = jnp.concatenate(
        [
            grad_shift_attn,
            grad_scale_attn,
            grad_gate_attn,
            grad_shift_mlp,
            grad_scale_mlp,
            grad_gate_mlp,
        ],
        axis=-1,
    )
    grad_ada = jnp.dot(scaled_cond.astype(jnp.float32).T, modulation_grad, precision=highest)
    grad_ada_offset = jnp.sum(modulation_grad, axis=0)
    cond_grad = jnp.dot(
        modulation_grad, ada_matrix.T, precision=highest, preferred_element_type=jnp.float32
    )
    grads = (
        grad_ada,
        grad_ada_offset,
        grad_qkv,
        grad_qv_offset,
        grad_out,
        grad_out_offset,
        grad_up,
        grad_up_offset,
        grad_down,
        grad_down_offset,
    )
    return (hidden_grad, cond_grad, grads)


def reduce_rows(grads):
    first, second, third, fourth, fifth, sixth, seventh, eighth, ninth, tenth = grads
    return (
        lax.psum_scatter(
            first.astype(jnp.bfloat16), "fsdp", scatter_dimension=0, tiled=True
        ).astype(jnp.float32),
        lax.psum_scatter(
            second.astype(jnp.bfloat16), "fsdp", scatter_dimension=0, tiled=True
        ).astype(jnp.float32),
        lax.psum_scatter(
            third.astype(jnp.bfloat16), "fsdp", scatter_dimension=0, tiled=True
        ).astype(jnp.float32),
        lax.psum_scatter(
            fourth.astype(jnp.bfloat16), "fsdp", scatter_dimension=0, tiled=True
        ).astype(jnp.float32),
        lax.psum_scatter(
            fifth.astype(jnp.bfloat16), "fsdp", scatter_dimension=0, tiled=True
        ).astype(jnp.float32),
        lax.psum_scatter(
            sixth.astype(jnp.bfloat16), "fsdp", scatter_dimension=0, tiled=True
        ).astype(jnp.float32),
        lax.psum_scatter(
            seventh.astype(jnp.bfloat16), "fsdp", scatter_dimension=0, tiled=True
        ).astype(jnp.float32),
        lax.psum_scatter(
            eighth.astype(jnp.bfloat16), "fsdp", scatter_dimension=0, tiled=True
        ).astype(jnp.float32),
        lax.psum_scatter(
            ninth.astype(jnp.bfloat16), "fsdp", scatter_dimension=0, tiled=True
        ).astype(jnp.float32),
        lax.psum_scatter(
            tenth.astype(jnp.bfloat16), "fsdp", scatter_dimension=0, tiled=True
        ).astype(jnp.float32),
    )


def per_device(
    tokens,
    condition,
    ada_weight,
    ada_bias,
    qkv_weight,
    qv_bias,
    out_weight,
    out_bias,
    up_weight,
    up_bias,
    down_weight,
    down_bias,
    cotangent,
):
    shards = (
        ada_weight,
        ada_bias,
        qkv_weight,
        qv_bias,
        out_weight,
        out_bias,
        up_weight,
        up_bias,
        down_weight,
        down_bias,
    )
    layers = ada_weight.shape[0]
    cond_float = condition.astype(jnp.float32)
    scaled_cond = jax.nn.silu(cond_float).astype(jnp.bfloat16)
    hidden = tokens.astype(jnp.float32)
    gathered_list = []
    saved_list = []
    for layer_index in range(layers):
        gathered = fetch_layer(shards, layer_index)
        hidden, saved_values = forward_layer(hidden, scaled_cond, gathered)
        gathered_list.append(gathered)
        saved_list.append(saved_values)
    block_out = hidden.astype(jnp.bfloat16)
    gradient = cotangent.astype(jnp.float32)
    cond_partial = jnp.zeros(cond_float.shape, jnp.float32)
    grad_layers = [None] * layers
    for layer_index in reversed(range(layers)):
        gathered = fetch_again(shards, layer_index)
        gradient, cond_grad, grads = backward_layer(
            gradient, scaled_cond, gathered, saved_list[layer_index]
        )
        cond_partial = cond_partial + cond_grad
        grad_layers[layer_index] = reduce_rows(grads)
    stacked = [
        jnp.stack([grad_layers[layer_index][member] for layer_index in range(layers)])
        for member in range(10)
    ]
    totals = (
        lax.psum(stacked[0].astype(jnp.bfloat16), "seq").astype(jnp.float32),
        lax.psum(stacked[1].astype(jnp.bfloat16), "seq").astype(jnp.float32),
        lax.psum(stacked[2].astype(jnp.bfloat16), "seq").astype(jnp.float32),
        lax.psum(stacked[3].astype(jnp.bfloat16), "seq").astype(jnp.float32),
        lax.psum(stacked[4].astype(jnp.bfloat16), "seq").astype(jnp.float32),
        lax.psum(stacked[5].astype(jnp.bfloat16), "seq").astype(jnp.float32),
        lax.psum(stacked[6].astype(jnp.bfloat16), "seq").astype(jnp.float32),
        lax.psum(stacked[7].astype(jnp.bfloat16), "seq").astype(jnp.float32),
        lax.psum(stacked[8].astype(jnp.bfloat16), "seq").astype(jnp.float32),
        lax.psum(stacked[9].astype(jnp.bfloat16), "seq").astype(jnp.float32),
        lax.psum(cond_partial.astype(jnp.bfloat16), "seq").astype(jnp.float32),
    )
    grad_list = totals[:10]
    cond_summed = totals[10]
    unused_value, silu_back = jax.vjp(jax.nn.silu, cond_float)
    grad_condition = silu_back(cond_summed)[0]
    return (
        block_out,
        gradient,
        grad_condition,
        grad_list[0],
        grad_list[1],
        grad_list[2],
        grad_list[3],
        grad_list[4],
        grad_list[5],
        grad_list[6],
        grad_list[7],
        grad_list[8],
        grad_list[9],
    )


def solution(mesh):
    placed = (
        P("fsdp", "seq", None),
        P("fsdp", None),
        P(None, "fsdp", None),
        P(None, "fsdp"),
        P(None, "fsdp", None),
        P(None, "fsdp"),
        P(None, "fsdp", None),
        P(None, "fsdp"),
        P(None, "fsdp", None),
        P(None, "fsdp"),
        P(None, "fsdp", None),
        P(None, "fsdp"),
        P("fsdp", "seq", None),
    )
    return jax.shard_map(
        per_device,
        mesh=mesh,
        in_specs=placed,
        out_specs=(
            P("fsdp", "seq", None),
            P("fsdp", "seq", None),
            P("fsdp", None),
            P(None, "fsdp", None),
            P(None, "fsdp"),
            P(None, "fsdp", None),
            P(None, "fsdp"),
            P(None, "fsdp", None),
            P(None, "fsdp"),
            P(None, "fsdp", None),
            P(None, "fsdp"),
            P(None, "fsdp", None),
            P(None, "fsdp"),
        ),
        check_vma=False,
    )
```

profile of v0, /device:TPU:0, one launch (start us, length us, event | category | flops | bytes accessed | tf_op | source)
XLA Modules:
  0.0 1995.2 jit_solution(11888481461048757320)
XLA Ops:
  23.4 41.9 %all-reduce.19 = (bf16[1536]{0:T(1024)(128)(2,1)S(1)}, bf16[4608]{0:T(1024)(128)(2,1)S(1)}, bf16[768]{0:T(1024)(128)(2,1)}, bf16[768]{0:T(1024)(128)(2,1)S(1)}, ...) all-reduce(bf16[1536]{0:T(1024)(128)(2,1)S(1)} %dynamic-update-slic, ...), channel_id=5, replica_groups=mesh['fsdp'=8,'seq'=4] {'fsdp'}, use_global_device_ids=true, to_apply=%add.1 | all-reduce | flops 15360 | bytes 61440
  66.0 57.1 %all-gather.31.cloned.1.call-done = bf16[1,768,4608]{2,1,0:T(8,128)(2,1)} async-done(((bf16[1,96,4608]{2,1,0:T(8,128)(2,1)}), bf16[1,768,4608]{2,1,0:T(8,128)(2,1)}) %all-gather.31.cloned.1.call-update) | async-done | bytes 7077904 | tf_op jit(solution)/shard_map/all_gather | solution.py:112
  127.1 105.2 %all-gather.41.cloned.1.call-done = bf16[1,768,4608]{2,1,0:T(8,128)(2,1)} async-done(((bf16[1,96,4608]{2,1,0:T(8,128)(2,1)}), bf16[1,768,4608]{2,1,0:T(8,128)(2,1)}) %all-gather.41.cloned.1.call-update) | async-done | bytes 7077904 | tf_op jit(solution)/shard_map/all_gather | solution.py:112
  237.7 60.3 %all-gather.33.cloned.1.call-done = bf16[1,768,2304]{2,1,0:T(8,128)(2,1)} async-done(((bf16[1,96,2304]{2,1,0:T(8,128)(2,1)}), bf16[1,768,2304]{2,1,0:T(8,128)(2,1)}) %all-gather.33.cloned.1.call-update) | async-done | bytes 3538960 | tf_op jit(solution)/shard_map/all_gather | solution.py:114
  340.2 5.5 fusion.94
  352.0 12.1 all-to-all-start.3
  364.7 26.8 %all-gather.7 = bf16[1,3072]{1,0:T(2,128)(2,1)S(1)} all-gather(bf16[1,384]{1,0:T(2,128)(2,1)S(1)} %get-tuple-element.213), channel_id=9, replica_groups=mesh['fsdp'=8,'seq'=4] {'fsdp'}, dimensions={1}, use_global_device_ids=true | all-gather | bytes 6912 | tf_op jit(solution)/shard_map/all_gather | solution.py:119
  397.0 23.1 %all-gather.37.cloned.1.call-done = bf16[1,768,3072]{2,1,0:T(8,128)(2,1)} async-done(((bf16[1,96,3072]{2,1,0:T(8,128)(2,1)}), bf16[1,768,3072]{2,1,0:T(8,128)(2,1)}) %all-gather.37.cloned.1.call-update) | async-done | bytes 4718608 | tf_op jit(solution)/shard_map/all_gather | solution.py:118
  420.0 5.5 fusion.38
  425.5 74.8 %all-gather.39.cloned.1.call-done = bf16[1,3072,768]{2,1,0:T(8,128)(2,1)} async-done(((bf16[1,384,768]{2,1,0:T(8,128)(2,1)}), bf16[1,3072,768]{2,1,0:T(8,128)(2,1)}) %all-gather.39.cloned.1.call-update) | async-done | bytes 4718608 | tf_op jit(solution)/shard_map/all_gather | solution.py:120
  500.4 6.2 fusion.254
  506.8 58.8 %all-gather.43.cloned.1.call-done = bf16[1,768,2304]{2,1,0:T(8,128)(2,1)} async-done(((bf16[1,96,2304]{2,1,0:T(8,128)(2,1)}), bf16[1,768,2304]{2,1,0:T(8,128)(2,1)}) %all-gather.43.cloned.1.call-update) | async-done | bytes 3538960 | tf_op jit(solution)/shard_map/all_gather | solution.py:114
  614.6 5.5 fusion.100
  633.1 27.1 %all-gather.17 = bf16[1,3072]{1,0:T(2,128)(2,1)S(1)} all-gather(bf16[1,384]{1,0:T(2,128)(2,1)S(1)} %copy-done.83), channel_id=19, replica_groups=mesh['fsdp'=8,'seq'=4] {'fsdp'}, dimensions={1}, use_global_device_ids=true | all-gather | bytes 6912 | tf_op jit(solution)/shard_map/all_gather | solution.py:119
  669.0 19.6 all-gather.47.cloned.1.call-done
  688.6 5.5 fusion.41
  694.1 74.8 %all-gather.49.cloned.1.call-done = bf16[1,3072,768]{2,1,0:T(8,128)(2,1)} async-done(((bf16[1,384,768]{2,1,0:T(8,128)(2,1)}), bf16[1,3072,768]{2,1,0:T(8,128)(2,1)}) %all-gather.49.cloned.1.call-update) | async-done | bytes 4718608 | tf_op jit(solution)/shard_map/all_gather | solution.py:120
  768.9 7.5 fusion.265
  796.3 12.0 all_to_all.258
  815.9 8.2 fusion.103
  824.1 7.5 fusion.267
  835.2 5.7 reduce.117
  847.6 14.0 multiply_reduce_fusion.1
  861.6 9.7 multiply_convert_fusion.3
  877.7 5.7 reduce.118
  898.3 5.7 reduce.119
  977.6 10.5 all_to_all.259
  990.9 8.1 fusion.97
  1002.6 5.7 reduce.121
  1015.3 6.4 fusion.268
  1021.7 13.5 multiply_reduce_fusion
  1035.2 9.7 multiply_convert_fusion.2
  1106.3 6.5 convolution_convert_fusion
  1113.0 6.4 convolution_convert_fusion.1
  1125.3 5.2 convolution_convert_fusion.3
  1141.3 10.1 multiply_convert_fusion.1
  1157.7 53.4 %reduce-scatter.15.cloned.1.call-done = bf16[96,2304]{1,0:T(8,128)(2,1)} async-done(((bf16[768,2304]{1,0:T(8,128)(2,1)}), bf16[96,2304]{1,0:T(8,128)(2,1)}) %reduce-scatter.15.cloned.1.call-update) | async-done | bytes 442384 | tf_op jit(solution)/shard_map/reduce_scatter | solution.py:325
  1213.3 96.7 %reduce-scatter.29.cloned.1.call-done = bf16[384,768]{1,0:T(8,128)(2,1)} async-done(((bf16[3072,768]{1,0:T(8,128)(2,1)}), bf16[384,768]{1,0:T(8,128)(2,1)}) %reduce-scatter.29.cloned.1.call-update) | async-done | bytes 589840 | tf_op jit(solution)/shard_map/reduce_scatter | solution.py:343
  1310.0 98.8 %reduce-scatter.27.cloned.1.call-done = bf16[384,768]{1,0:T(8,128)(2,1)} async-done(((bf16[3072,768]{1,0:T(8,128)(2,1)}), bf16[384,768]{1,0:T(8,128)(2,1)}) %reduce-scatter.27.cloned.1.call-update) | async-done | bytes 589840 | tf_op jit(solution)/shard_map/reduce_scatter | solution.py:343
  1411.1 96.5 %reduce-scatter.25.cloned.1.call-done = bf16[96,3072]{1,0:T(8,128)(2,1)} async-done(((bf16[768,3072]{1,0:T(8,128)(2,1)}), bf16[96,3072]{1,0:T(8,128)(2,1)}) %reduce-scatter.25.cloned.1.call-update) | async-done | bytes 589840 | tf_op jit(solution)/shard_map/reduce_scatter | solution.py:337
  1507.6 98.8 %reduce-scatter.23.cloned.1.call-done = bf16[96,3072]{1,0:T(8,128)(2,1)} async-done(((bf16[768,3072]{1,0:T(8,128)(2,1)}), bf16[96,3072]{1,0:T(8,128)(2,1)}) %reduce-scatter.23.cloned.1.call-update) | async-done | bytes 589840 | tf_op jit(solution)/shard_map/reduce_scatter | solution.py:337
  1608.8 130.5 %reduce-scatter.11.cloned.1.call-done = bf16[96,4608]{1,0:T(8,128)(2,1)} async-done(((bf16[768,4608]{1,0:T(8,128)(2,1)}), bf16[96,4608]{1,0:T(8,128)(2,1)}) %reduce-scatter.11.cloned.1.call-update) | async-done | bytes 884752 | tf_op jit(solution)/shard_map/reduce_scatter | solution.py:319
  1739.2 131.8 %reduce-scatter.13.cloned.1.call-done = bf16[96,4608]{1,0:T(8,128)(2,1)} async-done(((bf16[768,4608]{1,0:T(8,128)(2,1)}), bf16[96,4608]{1,0:T(8,128)(2,1)}) %reduce-scatter.13.cloned.1.call-update) | async-done | bytes 884752 | tf_op jit(solution)/shard_map/reduce_scatter | solution.py:319
  1873.9 7.8 fusion.121
  1882.8 7.8 fusion.118
  1890.7 35.8 %all-reduce.18 = (bf16[4608]{0:T(1024)(128)(2,1)S(1)}, bf16[4608]{0:T(1024)(128)(2,1)S(1)}, bf16[1536]{0:T(1024)(128)(2,1)S(1)}, bf16[1536]{0:T(1024)(128)(2,1)S...) all-reduce(bf16[4608]{0:T(1024)(128)(2,1)S(1)} %convert_element_typ, ...), channel_id=25, replica_groups=mesh['fsdp'=8,'seq'=4] {'fsdp'}, use_global_device_ids=true, to_apply=%region_37.38.clone | all-reduce | flops 21504 | bytes 86016
  1927.4 5.9 all-reduce.20
  1936.8 40.9 %all-reduce.24.cloned.1.call-done = (bf16[2,96,4608]{2,1,0:T(8,128)(2,1)}, bf16[2,96,2304]{2,1,0:T(8,128)(2,1)}, bf16[2,96,768]{2,1,0:T(8,128)(2,1)}, bf16[2,96,3072]{2,1,0:T(8,128)(2,1)}, bf16[2,384,768]{2,1,0:T(8,128)(2,1)}) async-done(((bf16[2,96,4608]{2,1,0:T(8,128)(2,1)}, bf16[2,96,2304]{2,1,0:T(8,128)(2,1)}, bf16[2,96,768]{2,1,0:T(8,128)(2,1)}, bf16[2,96,3072]{2,1,0:T(8,128)(2,1)}, ...) | async-done | bytes 5308432 | tf_op jit(solution)/shard_map/psum | solution.py:406
  (570 shorter events, 401.8 us)
Async XLA Ops:
  7.2 115.9 %all-gather.31.cloned.1.call-start = ((), (), s32[]{:S(2)}) async-start(), calls=%async_computation.36 | async-start | bytes 7962624 | tf_op jit(solution)/shard_map/all_gather | solution.py:112
  10.1 222.2 %all-gather.41.cloned.1.call-start = ((), (), s32[]{:S(2)}) async-start(), calls=%async_computation.41 | async-start | bytes 7962624 | tf_op jit(solution)/shard_map/all_gather | solution.py:112
  10.9 287.1 %all-gather.33.cloned.1.call-start = ((), (), s32[]{:S(2)}) async-start(), calls=%async_computation.37 | async-start | bytes 3981312 | tf_op jit(solution)/shard_map/all_gather | solution.py:114
  11.9 382.0 %all-gather.35.cloned.1.call-start = ((), (), s32[]{:S(2)}) async-start(), calls=%async_computation.38 | async-start | bytes 1327104 | tf_op jit(solution)/shard_map/all_gather | solution.py:116
  12.8 407.3 %all-gather.37.cloned.1.call-start = ((), (), s32[]{:S(2)}) async-start(), calls=%async_computation.39 | async-start | bytes 5308416 | tf_op jit(solution)/shard_map/all_gather | solution.py:118
  14.0 486.4 %all-gather.39.cloned.1.call-start = ((), (), s32[]{:S(2)}) async-start(), calls=%async_computation.40 | async-start | bytes 5308416 | tf_op jit(solution)/shard_map/all_gather | solution.py:120
  15.1 550.4 %all-gather.43.cloned.1.call-start = ((), (), s32[]{:S(2)}) async-start(), calls=%async_computation.42 | async-start | bytes 3981312 | tf_op jit(solution)/shard_map/all_gather | solution.py:114
  15.9 649.5 %all-gather.45.cloned.1.call-start = ((), (), s32[]{:S(2)}) async-start(), calls=%async_computation.43 | async-start | bytes 1327104 | tf_op jit(solution)/shard_map/all_gather | solution.py:116
  16.6 671.9 %all-gather.47.cloned.1.call-start = ((), (), s32[]{:S(2)}) async-start(), calls=%async_computation.44 | async-start | bytes 5308416 | tf_op jit(solution)/shard_map/all_gather | solution.py:118
  17.4 751.5 %all-gather.49.cloned.1.call-start = ((), (), s32[]{:S(2)}) async-start(), calls=%async_computation.45 | async-start | bytes 5308416 | tf_op jit(solution)/shard_map/all_gather | solution.py:120
  20.7 277.2 %copy-start.71 = (f32[256]{0:T(256)}, f32[256]{0:T(256)S(1)}, u32[]{:S(2)}) copy-start(f32[256]{0:T(256)S(1)} %broadcast_multiply_fusion.11) | copy-start | bytes 3076
  21.0 276.9 %copy-start.90 = (f32[256]{0:T(256)}, f32[256]{0:T(256)S(1)}, u32[]{:S(2)}) copy-start(f32[256]{0:T(256)S(1)} %add_rsqrt_fusion.3) | copy-start | bytes 3076
  21.8 210.6 %copy-start.46 = (f32[1,768]{1,0:T(1,128)}, f32[1,768]{1,0:T(1,128)S(1)}, u32[]{:S(2)}) copy-start(f32[1,768]{1,0:T(1,128)S(1)} %get-tuple-element.169) | copy-start | bytes 9220
  237.7 63.5 %copy-start.48 = (f32[768]{0:T(1024)}, f32[768]{0:T(1024)S(1)}, u32[]{:S(2)}) copy-start(f32[768]{0:T(1024)S(1)} %get-tuple-element.129) | copy-start | bytes 9220
  237.7 63.5 %copy-start.88 = (f32[768]{0:T(1024)}, f32[768]{0:T(1024)S(1)}, u32[]{:S(2)}) copy-start(f32[768]{0:T(1024)S(1)} %get-tuple-element.128) | copy-start | bytes 9220
  237.7 182.4 %copy-start.41 = (f32[768]{0:T(1024)}, f32[768]{0:T(1024)S(1)}, u32[]{:S(2)}) copy-start(f32[768]{0:T(1024)S(1)} %get-tuple-element.126) | copy-start | bytes 9220
  306.4 11.1 all-to-all-start.2
  317.4 10.8 all-to-all-start.1
  328.3 10.8 all-to-all-start
  352.0 40.1 %all-to-all-start.3 = ((bf16[4,2,24576]{2,1,0:T(2,128)(2,1)}), bf16[4,2,24576]{2,1,0:T(2,128)(2,1)S(1)}, u32[]{:S(2)}, u32[]{:S(2)}) async-start(bf16[4,2,24576]{2,1,0:T(2,128)(2,1)} %reshape.866), calls=%async_computation.3 | async-start | bytes 786432 | tf_op jit(solution)/shard_map/all_to_all | solution.py:187
  392.2 173.4 %copy-start.50 = (f32[768]{0:T(1024)}, f32[768]{0:T(1024)S(1)}, u32[]{:S(2)}) copy-start(f32[768]{0:T(1024)S(1)} %get-tuple-element.123) | copy-start | bytes 9220
  392.2 173.4 %copy-start.89 = (f32[768]{0:T(1024)}, f32[768]{0:T(1024)S(1)}, u32[]{:S(2)}) copy-start(f32[768]{0:T(1024)S(1)} %get-tuple-element.122) | copy-start | bytes 9220
  420.0 80.3 %copy-start.63 = (f32[768]{0:T(1024)S(1)}, f32[768]{0:T(1024)}, u32[]{:S(2)}) copy-start(f32[768]{0:T(1024)} %get-tuple-element.125) | copy-start | bytes 9220
  420.0 80.3 %copy-start.85 = (f32[768]{0:T(1024)S(1)}, f32[768]{0:T(1024)}, u32[]{:S(2)}) copy-start(f32[768]{0:T(1024)} %convert_element_type.520) | copy-start | bytes 9220
  500.4 65.2 %copy-start.69 = (f32[2304]{0:T(1024)S(1)}, f32[2304]{0:T(1024)}, u32[]{:S(2)}) copy-start(f32[2304]{0:T(1024)} %get-tuple-element.210) | copy-start | bytes 27652
  506.6 62.2 %copy-start.73 = (f32[256]{0:T(256)}, f32[256]{0:T(256)S(1)}, u32[]{:S(2)}) copy-start(f32[256]{0:T(256)S(1)} %broadcast_multiply_fusion.9) | copy-start | bytes 3076
  577.4 11.6 all-to-all-start.6
  589.0 11.2 all-to-all-start.5
  600.3 11.6 all-to-all-start.4
  628.4 32.3 %all-to-all-start.7 = ((bf16[4,2,24576]{2,1,0:T(2,128)(2,1)}), bf16[4,2,24576]{2,1,0:T(2,128)(2,1)S(1)}, u32[]{:S(2)}, u32[]{:S(2)}) async-start(bf16[4,2,24576]{2,1,0:T(2,128)(2,1)} %reshape.874), calls=%async_computation.7 | async-start | bytes 786432 | tf_op jit(solution)/shard_map/all_to_all | solution.py:187
  688.6 80.3 %copy-start.35 = (bf16[1,256,768]{2,1,0:T(8,128)(2,1)S(1)}, bf16[1,256,768]{2,1,0:T(8,128)(2,1)}, u32[]{:S(2)}) copy-start(bf16[1,256,768]{2,1,0:T(8,128)(2,1)} %param.25) | copy-start | bytes 1179652
  843.3 42.5 %all-to-all-start.11 = ((bf16[4,2,24576]{2,1,0:T(2,128)(2,1)}), bf16[4,2,24576]{2,1,0:T(2,128)(2,1)}, u32[]{:S(2)}, u32[]{:S(2)}) async-start(bf16[4,2,24576]{2,1,0:T(2,128)(2,1)} %reshape.878), calls=%async_computation.11 | async-start | bytes 786432 | tf_op jit(solution)/shard_map/all_to_all | solution.py:274
  885.8 20.7 %all-to-all-start.10 = ((bf16[4,2,24576]{2,1,0:T(2,128)(2,1)}), bf16[4,2,24576]{2,1,0:T(2,128)(2,1)}, u32[]{:S(2)}, u32[]{:S(2)}) async-start(bf16[4,2,24576]{2,1,0:T(2,128)(2,1)} %reshape.880), calls=%async_computation.10 | async-start | bytes 786432 | tf_op jit(solution)/shard_map/all_to_all | solution.py:273
  906.5 29.0 %all-to-all-start.9 = ((bf16[4,2,24576]{2,1,0:T(2,128)(2,1)}), bf16[4,2,24576]{2,1,0:T(2,128)(2,1)}, u32[]{:S(2)}, u32[]{:S(2)}) async-start(bf16[4,2,24576]{2,1,0:T(2,128)(2,1)} %reshape.882), calls=%async_computation.9 | async-start | bytes 786432 | tf_op jit(solution)/shard_map/all_to_all | solution.py:272
  910.6 245.3 %reduce-scatter.21.cloned.1.call-start = ((), (), s32[]{:S(2)}) async-start(), calls=%async_computation.31 | async-start | bytes 1327104 | tf_op jit(solution)/shard_map/reduce_scatter | solution.py:331
  913.3 242.7 %reduce-scatter.19.cloned.1.call-start = ((), (), s32[]{:S(2)}) async-start(), calls=%async_computation.30 | async-start | bytes 1327104 | tf_op jit(solution)/shard_map/reduce_scatter | solution.py:331
  962.4 195.3 %reduce-scatter.17.cloned.1.call-start = ((), (), s32[]{:S(2)}) async-start(), calls=%async_computation.29 | async-start | bytes 3981312 | tf_op jit(solution)/shard_map/reduce_scatter | solution.py:325
  1010.7 45.1 %all-to-all-start.15 = ((bf16[4,2,24576]{2,1,0:T(2,128)(2,1)}), bf16[4,2,24576]{2,1,0:T(2,128)(2,1)}, u32[]{:S(2)}, u32[]{:S(2)}) async-start(bf16[4,2,24576]{2,1,0:T(2,128)(2,1)} %reshape.886), calls=%async_computation.15 | async-start | bytes 786432 | tf_op jit(solution)/shard_map/all_to_all | solution.py:274
  1055.8 16.8 all-to-all-start.14
  1072.6 20.3 %all-to-all-start.13 = ((bf16[4,2,24576]{2,1,0:T(2,128)(2,1)}), bf16[4,2,24576]{2,1,0:T(2,128)(2,1)}, u32[]{:S(2)}, u32[]{:S(2)}) async-start(bf16[4,2,24576]{2,1,0:T(2,128)(2,1)} %reshape.890), calls=%async_computation.13 | async-start | bytes 786432 | tf_op jit(solution)/shard_map/all_to_all | solution.py:272
  1076.7 134.4 %reduce-scatter.15.cloned.1.call-start = ((), (), s32[]{:S(2)}) async-start(), calls=%async_computation.28 | async-start | bytes 3981312 | tf_op jit(solution)/shard_map/reduce_scatter | solution.py:325
  1106.2 203.7 %reduce-scatter.29.cloned.1.call-start = ((), (), s32[]{:S(2)}) async-start(), calls=%async_computation.35 | async-start | bytes 5308416 | tf_op jit(solution)/shard_map/reduce_scatter | solution.py:343
  1112.8 296.0 %reduce-scatter.27.cloned.1.call-start = ((), (), s32[]{:S(2)}) async-start(), calls=%async_computation.34 | async-start | bytes 5308416 | tf_op jit(solution)/shard_map/reduce_scatter | solution.py:343
  1119.4 388.2 %reduce-scatter.25.cloned.1.call-start = ((), (), s32[]{:S(2)}) async-start(), calls=%async_computation.33 | async-start | bytes 5308416 | tf_op jit(solution)/shard_map/reduce_scatter | solution.py:337
  1124.7 481.7 %reduce-scatter.23.cloned.1.call-start = ((), (), s32[]{:S(2)}) async-start(), calls=%async_computation.32 | async-start | bytes 5308416 | tf_op jit(solution)/shard_map/reduce_scatter | solution.py:337
  1130.6 608.6 %reduce-scatter.11.cloned.1.call-start = ((), (), s32[]{:S(2)}) async-start(), calls=%async_computation.26 | async-start | bytes 7962624 | tf_op jit(solution)/shard_map/reduce_scatter | solution.py:319
  1151.4 719.6 %reduce-scatter.13.cloned.1.call-start = ((), (), s32[]{:S(2)}) async-start(), calls=%async_computation.27 | async-start | bytes 7962624 | tf_op jit(solution)/shard_map/reduce_scatter | solution.py:319
  1152.0 825.7 %all-reduce.24.cloned.1.call-start = ((), (), s32[]{:S(2)}) async-start(), calls=%async_computation.46 | async-start | bytes 10616832 | tf_op jit(solution)/shard_map/psum | solution.py:406
  (95 other events, 886.4 us)
Sparse Core Ops, SparseCore 0:
  10.8 112.2 all-gather.30
  125.9 106.4 all-gather.40
  235.1 62.7 all-gather.32
  300.0 39.8 all-gather.34
  341.9 78.1 all-gather.36
  422.6 77.6 all-gather.38
  502.6 62.9 all-gather.42
  567.7 39.8 all-gather.44
  610.4 78.1 all-gather.46
  691.2 77.6 all-gather.48
  915.4 63.7 reduce-scatter.20
  982.4 63.6 reduce-scatter.18
  1050.2 78.3 reduce-scatter.16
  1132.1 78.9 reduce-scatter.14
  1214.6 95.2 reduce-scatter.28
  1313.5 95.2 reduce-scatter.26
  1412.3 95.2 reduce-scatter.24
  1511.1 95.2 reduce-scatter.22
  1610.1 129.1 reduce-scatter.10
  1742.8 128.2 reduce-scatter.12
  1874.9 102.7 all-reduce.23
where the time goes:
time: 2010 us; the launch traced here: 2000 us
  waiting for transfers between devices  1240 us (62%)
  matrix products  202 us (10%)
  local copies, waits for them, and re-layouts  163 us (8%)
  blocking collectives  160 us (8%)
  other arithmetic  141 us (7%)
  starting transfers between devices  65.7 us (3%)
  between operations  21.1 us (1%)
    reduce_scatter x2, waiting for transfers between devices, reduce_rows(): lax.psum_scatter(first.astype(jnp.bfloat16), 'fsdp', scatter_dimension=0,...  262 us
    reduce_scatter x2, waiting for transfers between devices, reduce_rows(): lax.psum_scatter(ninth.astype(jnp.bfloat16), 'fsdp', scatter_dimension=0,...  196 us
    reduce_scatter x2, waiting for transfers between devices, reduce_rows(): lax.psum_scatter(seventh.astype(jnp.bfloat16), 'fsdp', scatter_dimension=...  195 us
    all_gather x2, waiting for transfers between devices, fetch_layer(): lax.all_gather(ada_weight[layer_index], 'fsdp', axis=0, tiled=True)  162 us
    all_gather x2, waiting for transfers between devices, fetch_layer(): lax.all_gather(down_weight[layer_index], 'fsdp', axis=0, tiled=True)  150 us
    all_gather x2, waiting for transfers between devices, fetch_layer(): lax.all_gather(qkv_weight[layer_index], 'fsdp', axis=0, tiled=True)  119 us
    unnamed x2, blocking collectives  77.7 us
    unnamed x290, local copies, waits for them, and re-layouts  76.3 us
  transfers between devices with their start and end apart: 35, of which 22 were waited for; matrix products, arithmetic and copies ran while one was open for 21% of the time, Pallas kernels for 0%

commit v1 on v0

v1 whole, which is shorter than its diff:
```python
import jax
import jax.numpy as jnp
from jax import lax
from jax.sharding import PartitionSpec as P

HEAD_DIM = 64
SCORE_SCALE = HEAD_DIM ** (-0.5)
EPSILON = 1e-06
HIGHEST = lax.Precision.HIGHEST
F32 = jnp.float32
BF16 = jnp.bfloat16


def normalize(values):
    centred = values - jnp.mean(values, axis=-1, keepdims=True)
    inverse = lax.rsqrt(jnp.mean(centred * centred, axis=-1, keepdims=True) + EPSILON)
    return centred * inverse, inverse


def norm_back(gradient, normed, inverse):
    return inverse * (
        gradient
        - jnp.mean(gradient, axis=-1, keepdims=True)
        - normed * jnp.mean(gradient * normed, axis=-1, keepdims=True)
    )


def mm(a, b):
    return lax.dot_general(a, b, (((1,), (0,)), ((), ())), preferred_element_type=F32)


def mm_nt(a, b):
    return lax.dot_general(a, b, (((1,), (1,)), ((), ())), preferred_element_type=F32)


def mm_tn(a, b):
    return lax.dot_general(a, b, (((0,), (0,)), ((), ())), preferred_element_type=F32)


def split_heads(rows):
    return rows.reshape(rows.shape[0], -1, HEAD_DIM).transpose(1, 0, 2)


def join_heads(heads):
    return heads.transpose(1, 0, 2).reshape(heads.shape[1], -1)


def attend(q, k, v):
    q, k, v = split_heads(q), split_heads(k), split_heads(v)
    scores = jnp.einsum("hqd,hkd->hqk", q, k, preferred_element_type=F32) * SCORE_SCALE
    logsum = jnp.log(jnp.sum(jnp.exp(scores), axis=-1, keepdims=True))
    prob = jnp.exp(scores - logsum).astype(BF16)
    out = jnp.einsum("hqk,hkd->hqd", prob, v, preferred_element_type=F32)
    return join_heads(out).astype(BF16), logsum


def attend_back(q, k, v, logsum, out_grad):
    q, k, v, out_grad = split_heads(q), split_heads(k), split_heads(v), split_heads(out_grad)
    scores = jnp.einsum("hqd,hkd->hqk", q, k, preferred_element_type=F32) * SCORE_SCALE
    prob = jnp.exp(scores - logsum)
    dv = jnp.einsum("hqk,hqd->hkd", prob.astype(BF16), out_grad, preferred_element_type=F32)
    dp = jnp.einsum("hqd,hkd->hqk", out_grad, v, preferred_element_type=F32)
    inner = jnp.sum(prob * dp, axis=-1, keepdims=True)
    ds = (prob * (dp - inner)).astype(BF16)
    dq = jnp.einsum("hqk,hkd->hqd", ds, k, preferred_element_type=F32) * SCORE_SCALE
    dk = jnp.einsum("hqk,hqd->hkd", ds, q, preferred_element_type=F32) * SCORE_SCALE
    return [join_heads(t).astype(BF16) for t in (dq, dk, dv)]


def gelu_parts(u):
    c = 0.7978845608028654
    inner = c * (u + 0.044715 * (u * u * u))
    t = jnp.tanh(inner)
    value = 0.5 * u * (1.0 + t)
    slope = 0.5 * (1.0 + t) + 0.5 * u * (1.0 - t * t) * (c * (1.0 + 3.0 * 0.044715 * u * u))
    return value, slope


def per_device(
    tokens, condition, ada_weight, ada_bias, qkv_weight, qv_bias, out_weight, out_bias,
    up_weight, up_bias, down_weight, down_bias, cotangent,
):
    n = lax.axis_size("fsdp")
    ns = lax.axis_size("seq")
    f = lax.axis_index("fsdp")
    s = lax.axis_index("seq")
    layers, rows, width6 = ada_weight.shape
    width = rows * n
    ff = up_weight.shape[2]
    hc = width // ns
    fc = ff // (ns * n)

    def take(x, axis):
        return lax.dynamic_index_in_dim(x, s, axis, keepdims=False)

    def own(x, axis, size):
        return lax.dynamic_slice_in_dim(x, f * size, size, axis)

    w_qkv, w_rest = [], []
    for l in range(layers):
        q_part = take(qkv_weight[l].reshape(rows, 3, ns, hc), 2).reshape(rows, 3 * hc)
        u_part = take(up_weight[l].reshape(rows, n, ns, fc), 2).reshape(rows, n * fc)
        d_part = take(down_weight[l].reshape(ns, fc, width), 0)
        w_qkv.append(lax.all_gather(q_part, "fsdp", axis=0, tiled=True))
        rest = jnp.concatenate([u_part, d_part, out_weight[l]], axis=1)
        w_rest.append(lax.all_gather(rest, "fsdp", axis=0, tiled=True))
    fw = n * fc

    cond_float = condition.astype(F32)
    cond_act = jax.nn.silu(cond_float).astype(BF16)
    small = jnp.concatenate(
        [ada_bias.reshape(-1), qv_bias.reshape(-1), out_bias.reshape(-1), up_bias.reshape(-1),
         down_bias.reshape(-1), cond_act.reshape(-1)]
    )
    small = lax.all_gather(small, "fsdp", axis=0, tiled=False)
    pos = 0

    def unpack(per_layer):
        nonlocal pos
        part = small[:, pos: pos + layers * per_layer].reshape(n, layers, per_layer)
        pos += layers * per_layer
        return part.transpose(1, 0, 2).reshape(layers, n * per_layer)

    ada_b = unpack(ada_bias.shape[1]).astype(F32)
    qv_b = unpack(qv_bias.shape[1]).astype(F32)
    out_b = unpack(out_bias.shape[1]).astype(F32)
    up_b = unpack(up_bias.shape[1]).astype(F32)
    down_b = unpack(down_bias.shape[1]).astype(F32)
    cond_all = small[:, pos:]
    cond_rows = own(cond_all, 1, rows)
    q_b = take(qv_b[:, :width].reshape(layers, ns, hc), 1)
    v_b = take(qv_b[:, width:].reshape(layers, ns, hc), 1)
    qkv_b = jnp.concatenate([q_b, jnp.zeros_like(q_b), v_b], axis=1)
    up_bs = take(up_b.reshape(layers, n, ns, fc), 2).reshape(layers, fw)

    mod_partial = jnp.stack([mm(cond_rows, ada_weight[l]) for l in range(layers)], axis=1)
    mod = lax.psum_scatter(mod_partial, "fsdp", scatter_dimension=0, tiled=True)[0] + ada_b

    hidden = tokens[0].astype(F32)
    saved = []
    for l in range(layers):
        shift_a, scale_a, gate_a, shift_m, scale_m, gate_m = jnp.split(mod[l], 6)
        n_a, r_a = normalize(hidden)
        attn_in = (n_a * (1.0 + scale_a) + shift_a).astype(BF16)
        attn_all = lax.all_gather(attn_in, "seq", axis=0, tiled=True)
        qkv = (mm(attn_all, w_qkv[l]) + qkv_b[l]).astype(BF16)
        q, k, v = qkv[:, :hc], qkv[:, hc: 2 * hc], qkv[:, 2 * hc:]
        head_out, logsum = attend(q, k, v)
        tok_out = lax.all_to_all(head_out, "seq", split_axis=0, concat_axis=1, tiled=True)
        branch = mm(tok_out, w_rest[l][:, fw + width:]) + out_b[l]
        middle = hidden + gate_a * branch
        n_m, r_m = normalize(middle)
        mlp_in = (n_m * (1.0 + scale_m) + shift_m).astype(BF16)
        mlp_all = lax.all_gather(mlp_in, "seq", axis=0, tiled=True)
        up = mm(mlp_all, w_rest[l][:, :fw]) + up_bs[l]
        act = gelu_parts(up)[0].astype(BF16)
        feed = mm(act, w_rest[l][:, fw: fw + width])
        feed = lax.psum_scatter(feed, "seq", scatter_dimension=0, tiled=True) + down_b[l]
        saved.append((n_a, r_a, attn_all, q, k, v, logsum, tok_out, branch, n_m, r_m, mlp_all, up, act, feed))
        hidden = middle + gate_m * feed
    block_out = hidden.astype(BF16)

    g = cotangent[0].astype(F32)
    d_mods = [None] * layers
    reduced = [None] * layers
    bias_grads = [None] * layers
    for l in reversed(range(layers)):
        shift_a, scale_a, gate_a, shift_m, scale_m, gate_m = jnp.split(mod[l], 6)
        n_a, r_a, attn_all, q, k, v, logsum, tok_out, branch, n_m, r_m, mlp_all, up, act, feed = saved[l]
        g_feed = (gate_m * g).astype(BF16)
        d_gate_m = jnp.sum(g * feed, axis=0)
        g_feed_all = lax.all_gather(g_feed, "seq", axis=0, tiled=True)
        grad_down = mm_tn(act, g_feed_all)
        g_up = (mm_nt(g_feed_all, w_rest[l][:, fw: fw + width]) * gelu_parts(up)[1]).astype(BF16)
        grad_up = mm_tn(mlp_all, g_up)
        g_min = lax.psum_scatter(mm_nt(g_up, w_rest[l][:, :fw]), "seq", scatter_dimension=0, tiled=True)
        d_scale_m = jnp.sum(g_min * n_m, axis=0)
        d_shift_m = jnp.sum(g_min, axis=0)
        g_mid = g + norm_back(g_min * (1.0 + scale_m), n_m, r_m)
        g_branch = (gate_a * g_mid).astype(BF16)
        d_gate_a = jnp.sum(g_mid * branch, axis=0)
        grad_out = mm_tn(tok_out, g_branch)
        g_o = mm_nt(g_branch, w_rest[l][:, fw + width:]).astype(BF16)
        g_o_heads = lax.all_to_all(g_o, "seq", split_axis=1, concat_axis=0, tiled=True)
        dq, dk, dv = attend_back(q, k, v, logsum, g_o_heads)
        g_qkv = jnp.concatenate([dq, dk, dv], axis=1)
        grad_qkv = mm_tn(attn_all, g_qkv)
        g_ain = lax.psum_scatter(mm_nt(g_qkv, w_qkv[l]), "seq", scatter_dimension=0, tiled=True)
        d_scale_a = jnp.sum(g_ain * n_a, axis=0)
        d_shift_a = jnp.sum(g_ain, axis=0)
        g = g_mid + norm_back(g_ain * (1.0 + scale_a), n_a, r_a)
        d_mods[l] = jnp.concatenate([d_shift_a, d_scale_a, d_gate_a, d_shift_m, d_scale_m, d_gate_m])
        packed = jnp.concatenate([grad_up, grad_down, grad_out, grad_qkv], axis=1).astype(BF16)
        reduced[l] = lax.psum_scatter(packed, "fsdp", scatter_dimension=0, tiled=True)

        def place(x, axis):
            zeros = jnp.zeros(x.shape[:axis] + (ns,) + x.shape[axis + 1:], F32)
            return lax.dynamic_update_slice_in_dim(zeros, x, s, axis)

        qv_g = place(jnp.stack([jnp.sum(dq.astype(F32), axis=0), jnp.sum(dv.astype(F32), axis=0)])[:, None, :], 1)
        up_g = place(jnp.sum(g_up.astype(F32), axis=0).reshape(n, 1, fc), 1)
        bias_grads[l] = jnp.concatenate([
            qv_g.reshape(n, -1), jnp.sum(g_branch.astype(F32), axis=0).reshape(n, -1),
            up_g.reshape(n, -1), jnp.sum(g_feed.astype(F32), axis=0).reshape(n, -1)], axis=1)

    red = jnp.stack(reduced)
    shared = jnp.concatenate([red[:, :, : fw + width], red[:, :, fw + 2 * width:]], axis=2)
    shared = lax.all_gather(shared, "seq", axis=0, tiled=False).astype(F32)
    grad_up = shared[..., :fw].reshape(ns, layers, rows, n, fc).transpose(1, 2, 3, 0, 4).reshape(layers, rows, ff)
    grad_down = shared[..., fw: fw + width].transpose(1, 0, 2, 3).reshape(layers, ns * fc, width)
    grad_qkv = shared[..., fw + width:].reshape(ns, layers, rows, 3, hc).transpose(1, 2, 3, 0, 4)
    grad_qkv = grad_qkv.reshape(layers, rows, 3 * width)
    grad_out = lax.psum(red[:, :, fw + width: fw + 2 * width], "seq").astype(F32)

    bias = lax.psum(jnp.stack(bias_grads), ("fsdp", "seq"))
    bias = lax.dynamic_index_in_dim(bias, f, 1, keepdims=False)
    cuts = [qv_bias.shape[1], out_bias.shape[1], up_bias.shape[1], down_bias.shape[1]]
    grad_bias, at = [], 0
    for size in cuts:
        grad_bias.append(bias[:, at: at + size])
        at += size

    d_mod = lax.psum(jnp.stack(d_mods), "seq")
    d_mod_all = lax.all_gather(d_mod, "fsdp", axis=0, tiled=False)
    cond_rows32 = cond_rows.astype(F32)
    grad_ada = jnp.stack([
        lax.dot_general(cond_rows32, d_mod_all[:, l], (((0,), (0,)), ((), ())), precision=HIGHEST,
                        preferred_element_type=F32) for l in range(layers)])
    grad_ada_bias = own(jnp.sum(d_mod_all, axis=0), 1, width6 // n)
    g_cond = sum(
        lax.dot_general(d_mod_all[:, l], ada_weight[l].astype(F32), (((1,), (1,)), ((), ())),
                        precision=HIGHEST, preferred_element_type=F32) for l in range(layers))
    g_cond = lax.all_to_all(g_cond, "fsdp", split_axis=0, concat_axis=1, tiled=True)
    _, silu_back = jax.vjp(jax.nn.silu, cond_float)
    grad_condition = silu_back(g_cond)[0]
    return (
        block_out[None], g[None], grad_condition, grad_ada, grad_ada_bias, grad_qkv, grad_bias[0],
        grad_out, grad_bias[1], grad_up, grad_bias[2], grad_down, grad_bias[3],
    )


def solution(mesh):
    token = P("fsdp", "seq", None)
    matrix = P(None, "fsdp", None)
    vector = P(None, "fsdp")
    return jax.shard_map(
        per_device,
        mesh=mesh,
        in_specs=(token, P("fsdp", None)) + (matrix, vector) * 5 + (token,),
        out_specs=(token, token, P("fsdp", None)) + (matrix, vector) * 5,
        check_vma=False,
    )
```

time: 2010 us -> 1020 us (0.51)
  waiting for transfers between devices: 1240 us -> 486 us
  other arithmetic: 141 us -> 55.2 us
  local copies, waits for them, and re-layouts: 163 us -> 90.3 us
  matrix products: 202 us -> 144 us
  starting transfers between devices: 65.7 us -> 14.2 us
  blocking collectives: 160 us -> 203 us
    reduce_scatter x10 -> x6, waiting for transfers between devices: 707 us -> 168 us  [the longest x2 76.8 us: per_device(): lax.psum_scatter(feed, 'seq', scatter_dimension=0, tiled=True) + down_b[l]]
    all_gather x10 -> x9, waiting for transfers between devices: 474 us -> 116 us  [the longest x2 43.5 us: per_device(): w_rest.append(lax.all_gather(rest, 'fsdp', axis=0, tiled=True))]
    unnamed x21 -> x22, waiting for transfers between devices: 4.06 us -> 196 us
    unnamed x2 -> x0, blocking collectives: 77.7 us -> none
    all_gather x2 -> x4, blocking collectives: 53.8 us -> 131 us  [the longest x2 67.5 us: per_device(): w_qkv.append(lax.all_gather(q_part, 'fsdp', axis=0, tiled=True))]
    unnamed x18 -> x4, other arithmetic: 69.3 us -> 0.01 us
    all_to_all x14 -> x3, starting transfers between devices: 63.8 us -> 12.2 us  [the longest x2 6.92 us: per_device(): lax.all_to_all(head_out, 'seq', split_axis=0, concat_axis=1, tiled=True)]
    unnamed x290 -> x158, local copies, waits for them, and re-layouts: 76.3 us -> 27.4 us
  transfers between devices with their start and end apart: 35 -> 22, of which waited for: 22 -> 16; matrix products, arithmetic and copies ran while one was open for 21% -> 15% of each run, Pallas kernels for 0% -> 0%
where the time goes in v1:
time: 1020 us; the launch traced here: 1010 us
  waiting for transfers between devices  486 us (48%)
  blocking collectives  203 us (20%)
  matrix products  144 us (14%)
  local copies, waits for them, and re-layouts  90.3 us (9%)
  other arithmetic  55.2 us (5%)
  between operations  15.9 us (2%)
  starting transfers between devices  14.2 us (1%)
    unnamed x22, waiting for transfers between devices  196 us
    reduce_scatter x2, waiting for transfers between devices, per_device(): lax.psum_scatter(feed, 'seq', scatter_dimension=0, tiled=True) + down_b[l]  76.8 us
    all_gather x2, blocking collectives, per_device(): w_qkv.append(lax.all_gather(q_part, 'fsdp', axis=0, tiled=True))  67.5 us
    reduce_scatter x2, waiting for transfers between devices, per_device(): lax.psum_scatter(mm_nt(g_up, w_rest[l][:, :fw]), 'seq', scatter_dimension...  52.9 us
    all_gather x2, waiting for transfers between devices, per_device(): w_rest.append(lax.all_gather(rest, 'fsdp', axis=0, tiled=True))  43.5 us
    psum x1, blocking collectives, per_device(): bias = lax.psum(jnp.stack(bias_grads), ('fsdp', 'seq'))  40.9 us
    reduce_scatter x2, waiting for transfers between devices, per_device(): lax.psum_scatter(mm_nt(g_qkv, w_qkv[l]), 'seq', scatter_dimension=0, tile...  38 us
    all_gather x2, waiting for transfers between devices, per_device(): g_feed_all = lax.all_gather(g_feed, 'seq', axis=0, tiled=True)  36.3 us
  transfers between devices with their start and end apart: 22, of which 16 were waited for; matrix products, arithmetic and copies ran while one was open for 15% of the time, Pallas kernels for 0%

profile of v1, /device:TPU:0, one launch (start us, length us, event | category | flops | bytes accessed | tf_op | source)
XLA Modules:
  0.0 1008.8 jit_solution(16156190823706369313)
XLA Ops:
  12.4 32.4 %all-gather.2 = bf16[8,1,3456]{2,1,0:T(2,128)(2,1)S(1)} all-gather(bf16[1,1,3456]{2,1,0:T(2,128)(2,1)S(1)} %reshape.391), channel_id=2, replica_groups=mesh['fsdp'=8,'seq'=4] {'fsdp'}, dimensions={0}, use_global_device_ids=true | all-gather | bytes 62208 | tf_op jit(solution)/shard_map/all_gather | solution.py:115
  50.2 71.0 %all-reduce.6.cloned.1.call-done = f32[8,2,4608]{2,1,0:T(2,128)} async-done(((f32[8,2,4608]{2,1,0:T(2,128)}), f32[8,2,4608]{2,1,0:T(2,128)}) %all-reduce.6.cloned.1.call-update) | async-done | bytes 294928
  135.6 34.4 %all_gather.51 = bf16[768,576]{1,0:T(8,128)(2,1)S(1)} all-gather(bf16[96,576]{1,0:T(8,128)(2,1)S(1)} %copy.123), channel_id=1, replica_groups=mesh['fsdp'=8,'seq'=4] {'fsdp'}, dimensions={0}, use_global_device_ids=true | all-gather | bytes 995328 | tf_op jit(solution)/shard_map/all_gather | solution.py:104
  173.0 6.9 fusion.3
  179.9 5.8 fusion.65
  191.1 6.5 all-to-all-done
  197.6 14.9 %all-gather.15.cloned.1.call-done = bf16[768,2304]{1,0:T(8,128)(2,1)} async-done(((bf16[96,2304]{1,0:T(8,128)(2,1)}), bf16[768,2304]{1,0:T(8,128)(2,1)}) %all-gather.15.cloned.1.call-update) | async-done | bytes 3538960 | tf_op jit(solution)/shard_map/all_gather | solution.py:106
  216.7 18.3 %all-gather.17.cloned.1.call-done = bf16[1024,768]{1,0:T(8,128)(2,1)} async-done(((bf16[256,768]{1,0:T(8,128)(2,1)}), bf16[1024,768]{1,0:T(8,128)(2,1)}) %all-gather.17.cloned.1.call-update) | async-done | bytes 1572880 | tf_op jit(solution)/shard_map/all_gather | solution.py:154
  239.7 5.0 fusion.78
  244.9 37.9 %reduce-scatter.13.cloned.1.call-done = f32[256,768]{1,0:T(8,128)} async-done(((f32[1024,768]{1,0:T(8,128)}), f32[256,768]{1,0:T(8,128)}) %reduce-scatter.13.cloned.1.call-update) | async-done | bytes 786448 | tf_op jit(solution)/shard_map/reduce_scatter | solution.py:158
  289.8 33.0 %all_gather.55 = bf16[768,576]{1,0:T(8,128)(2,1)S(1)} all-gather(bf16[96,576]{1,0:T(8,128)(2,1)S(1)} %copy.129), channel_id=1, replica_groups=mesh['fsdp'=8,'seq'=4] {'fsdp'}, dimensions={0}, use_global_device_ids=true | all-gather | bytes 995328 | tf_op jit(solution)/shard_map/all_gather | solution.py:104
  326.4 6.9 fusion.2
  333.3 5.8 fusion.62
  343.9 28.6 %all-gather.21.cloned.1.call-done = bf16[768,2304]{1,0:T(8,128)(2,1)} async-done(((bf16[96,2304]{1,0:T(8,128)(2,1)}), bf16[768,2304]{1,0:T(8,128)(2,1)}) %all-gather.21.cloned.1.call-update) | async-done | bytes 3538960 | tf_op jit(solution)/shard_map/all_gather | solution.py:106
  377.7 17.5 %all-gather.23.cloned.1.call-done = bf16[1024,768]{1,0:T(8,128)(2,1)} async-done(((bf16[256,768]{1,0:T(8,128)(2,1)}), bf16[1024,768]{1,0:T(8,128)(2,1)}) %all-gather.23.cloned.1.call-update) | async-done | bytes 1572880 | tf_op jit(solution)/shard_map/all_gather | solution.py:154
  395.2 4.8 fusion.73
  400.0 17.0 %all-gather.25.cloned.1.call-done = bf16[1024,768]{1,0:T(8,128)(2,1)} async-done(((bf16[256,768]{1,0:T(8,128)(2,1)}), bf16[1024,768]{1,0:T(8,128)(2,1)}) %all-gather.25.cloned.1.call-update) | async-done | bytes 1572880 | tf_op jit(solution)/shard_map/all_gather | solution.py:172
  417.0 5.6 convert_reduce_fusion
  423.7 4.3 fusion.71
  428.1 6.0 fusion.69
  434.2 31.9 %reduce-scatter.17.cloned.1.call-done = f32[256,768]{1,0:T(8,128)} async-done(((f32[1024,768]{1,0:T(8,128)}), f32[256,768]{1,0:T(8,128)}) %reduce-scatter.17.cloned.1.call-update) | async-done | bytes 786448 | tf_op jit(solution)/shard_map/reduce_scatter | solution.py:176
  467.6 38.9 %reduce-scatter.15.cloned.1.call-done = f32[256,768]{1,0:T(8,128)} async-done(((f32[1024,768]{1,0:T(8,128)}), f32[256,768]{1,0:T(8,128)}) %reduce-scatter.15.cloned.1.call-update) | async-done | bytes 786448 | tf_op jit(solution)/shard_map/reduce_scatter | solution.py:158
  511.5 10.0 all_to_all.80
  522.9 7.5 convert_reduce_fusion.5
  530.4 6.8 multiply_reduce_fusion.1
  537.7 5.2 multiply_convert_fusion.1
  542.9 5.0 fusion.46
  553.2 38.0 %reduce-scatter.19.cloned.1.call-done = f32[256,768]{1,0:T(8,128)} async-done(((f32[1024,768]{1,0:T(8,128)}), f32[256,768]{1,0:T(8,128)}) %reduce-scatter.19.cloned.1.call-update) | async-done | bytes 786448 | tf_op jit(solution)/shard_map/reduce_scatter | solution.py:188
  595.6 19.3 %all-gather.27.cloned.1.call-done = bf16[1024,768]{1,0:T(8,128)(2,1)} async-done(((bf16[256,768]{1,0:T(8,128)(2,1)}), bf16[1024,768]{1,0:T(8,128)(2,1)}) %all-gather.27.cloned.1.call-update) | async-done | bytes 1572880 | tf_op jit(solution)/shard_map/all_gather | solution.py:172
  614.9 5.6 convert_reduce_fusion.1
  621.6 4.3 fusion.80
  636.4 6.5 copy.160
  643.0 21.0 %reduce-scatter.21.cloned.1.call-done = f32[256,768]{1,0:T(8,128)} async-done(((f32[1024,768]{1,0:T(8,128)}), f32[256,768]{1,0:T(8,128)}) %reduce-scatter.21.cloned.1.call-update) | async-done | bytes 786448 | tf_op jit(solution)/shard_map/reduce_scatter | solution.py:176
  670.0 10.0 all_to_all.81
  680.6 11.1 %multiply_reduce_fusion = (f32[3,1024]{1,0:T(4,128)S(1)}, f32[3,1024,1024]{1,2,0:T(8,128)}) fusion(f32[3,1024,1024]{1,2,0:T(8,128)} %fusion.3, bf16[3,1024,64]{1,2,0:T(8,128)(2,1)S(1)} %bitcast.272, bf16[1024,3,64]{0,2,1:T(8,128)(2,1)S(1)} %reshape.363), kind=kOutput, calls=%fused_computation.7 | convolution fusion | flops 408941568 | bytes 25964544 | tf_op jit(solution)/shard_map/hqd,hkd->hqk/dot_general | solution.py:62
  691.7 10.3 %multiply_convert_fusion = bf16[3,1024,1024]{1,2,0:T(8,128)(2,1)S(1)} fusion(f32[3,1024,1024]{1,2,0:T(8,128)} %fusion.3, f32[3,1024,1024]{1,2,0:T(8,128)} %get-tuple-element.173, f32[3,1024]{1,0:T(4,128)S(1)} %get-tuple-element.172), kind=kLoop, calls=%fused_computation.6 | loop fusion | flops 9437184 | bytes 31469568 | tf_op jit(solution)/shard_map/convert_element_type | solution.py:64
  711.0 3.5 convolution_convert_fusion.5
  720.4 6.5 copy.158
  728.2 32.9 %reduce-scatter.27.cloned.1.call-done = bf16[96,2880]{1,0:T(8,128)(2,1)} async-done(((bf16[768,2880]{1,0:T(8,128)(2,1)}), bf16[96,2880]{1,0:T(8,128)(2,1)}) %reduce-scatter.27.cloned.1.call-update) | async-done | bytes 552976
  763.0 40.9 %psum.22 = f32[2,8,768]{2,0,1:T(2,128)S(1)} all-reduce(f32[2,8,768]{2,0,1:T(2,128)S(1)} %pad_maximum_fusion.14), channel_id=1, replica_groups=mesh['fsdp'=8,'seq'=4] {'fsdp','seq'}, use_global_device_ids=true, to_apply=%region_53.54 | all-reduce | flops 12288 | bytes 98304 | tf_op jit(solution)/shard_map/psum | solution.py:215
  807.4 92.1 %reduce-scatter.25.cloned.1.call-done = bf16[96,2880]{1,0:T(8,128)(2,1)} async-done(((bf16[768,2880]{1,0:T(8,128)(2,1)}), bf16[96,2880]{1,0:T(8,128)(2,1)}) %reduce-scatter.25.cloned.1.call-update) | async-done | bytes 552976
  908.3 11.0 %psum.21 = f32[1,2,4608]{2,1,0:T(2,128)S(1)} all-reduce(f32[1,2,4608]{2,1,0:T(2,128)S(1)} %maximum_bitcast_fusion), channel_id=1, replica_groups=mesh['fsdp'=8,'seq'=4] {'seq'}, use_global_device_ids=true, to_apply=%region_39.40 | all-reduce | flops 9216 | bytes 73728 | tf_op jit(solution)/shard_map/psum | solution.py:223
  919.3 31.0 %all_gather.61 = f32[8,2,4608]{2,1,0:T(2,128)S(1)} all-gather(f32[1,2,4608]{2,1,0:T(2,128)S(1)} %psum.21), channel_id=1, replica_groups=mesh['fsdp'=8,'seq'=4] {'fsdp'}, dimensions={0}, use_global_device_ids=true | all-gather | bytes 331776 | tf_op jit(solution)/shard_map/all_gather | solution.py:224
  952.9 5.3 all-to-all-start.4
  968.4 6.8 copy.145
  978.5 5.1 slice_bitcast_fusion
  990.1 5.3 reshape.377
  998.1 3.7 reshape.365
  (399 shorter events, 154.8 us)
Async XLA Ops:
  7.2 42.1 %copy-start.56 = (u32[32]{0:T(128)S(1)}, u32[32]{0:T(128)}, u32[]{:S(2)}) copy-start(u32[32]{0:T(128)} %constant.102) | copy-start | bytes 388
  7.2 41.7 %copy-start.3 = (bf16[1,256,768]{2,1,0:T(8,128)(2,1)S(1)}, bf16[1,256,768]{2,1,0:T(8,128)(2,1)}, u32[]{:S(2)}) copy-start(bf16[1,256,768]{2,1,0:T(8,128)(2,1)} %param.13) | copy-start | bytes 1179652
  7.2 113.9 %all-reduce.6.cloned.1.call-start = ((), (), s32[]{:S(2)}) async-start(), calls=%async_computation.31 | async-start | bytes 589824
  44.8 79.0 %copy-start.29 = (bf16[2,96,3072]{2,1,0:T(8,128)(2,1)S(1)}, bf16[2,96,3072]{2,1,0:T(8,128)(2,1)}, u32[]{:S(2)}) copy-start(bf16[2,96,3072]{2,1,0:T(8,128)(2,1)} %param.21) | copy-start | bytes 3538948
  44.9 76.3 %copy-start.44 = (bf16[8,768]{1,0:T(8,128)(2,1)}, bf16[8,768]{1,0:T(8,128)(2,1)S(1)}, u32[]{:S(2)}) copy-start(bf16[8,768]{1,0:T(8,128)(2,1)S(1)} %get-tuple-element.163) | copy-start | bytes 36868
  48.8 121.1 %all-gather.13.cloned.1.call-start = ((), (), s32[]{:S(2)}) async-start(), calls=%async_computation.13 | async-start | bytes 1966080 | tf_op jit(solution)/shard_map/all_gather | solution.py:145
  49.1 76.8 %copy-start.45 = (f32[256]{0:T(256)}, f32[256]{0:T(256)S(1)}, u32[]{:S(2)}) copy-start(f32[256]{0:T(256)S(1)} %broadcast_multiply_fusion.11) | copy-start | bytes 3076
  50.1 78.1 %copy-start.47 = (f32[256]{0:T(256)}, f32[256]{0:T(256)S(1)}, u32[]{:S(2)}) copy-start(f32[256]{0:T(256)S(1)} %add_rsqrt_fusion.3) | copy-start | bytes 3076
  123.7 88.8 %all-gather.15.cloned.1.call-start = ((), (), s32[]{:S(2)}) async-start(), calls=%async_computation.14 | async-start | bytes 3981312 | tf_op jit(solution)/shard_map/all_gather | solution.py:106
  186.8 10.8 %all-to-all-start = ((bf16[4,256,192]{1,2,0:T(8,128)(2,1)}), bf16[4,256,192]{1,2,0:T(8,128)(2,1)S(1)}, u32[]{:S(2)}, u32[]{:S(2)}) async-start(bf16[4,256,192]{1,2,0:T(8,128)(2,1)} %copy.126), calls=%async_computation | async-start | bytes 786432 | tf_op jit(solution)/shard_map/all_to_all | solution.py:149
  190.2 44.7 %all-gather.17.cloned.1.call-start = ((), (), s32[]{:S(2)}) async-start(), calls=%async_computation.15 | async-start | bytes 1966080 | tf_op jit(solution)/shard_map/all_gather | solution.py:154
  197.6 40.5 %copy-start.13 = (bf16[4,256,192]{1,2,0:T(8,128)(2,1)}, bf16[4,256,192]{1,2,0:T(8,128)(2,1)S(1)}, u32[]{:S(2)}) copy-start(bf16[4,256,192]{1,2,0:T(8,128)(2,1)S(1)} %all-to-all-done) | copy-start | bytes 1179652
  215.2 67.6 %copy-start.1 = (f32[256,768]{1,0:T(8,128)}, f32[256,768]{1,0:T(8,128)S(1)}, u32[]{:S(2)}) copy-start(f32[256,768]{1,0:T(8,128)S(1)} %get-tuple-element.130) | copy-start | bytes 2359300
  216.4 66.4 %reduce-scatter.13.cloned.1.call-start = ((), (), s32[]{:S(2)}) async-start(), calls=%async_computation.16 | async-start | bytes 3932160 | tf_op jit(solution)/shard_map/reduce_scatter | solution.py:158
  244.8 78.0 %all-gather.19.cloned.1.call-start = ((), (), s32[]{:S(2)}) async-start(), calls=%async_computation.17 | async-start | bytes 1966080 | tf_op jit(solution)/shard_map/all_gather | solution.py:145
  285.4 87.2 %all-gather.21.cloned.1.call-start = ((), (), s32[]{:S(2)}) async-start(), calls=%async_computation.18 | async-start | bytes 3981312 | tf_op jit(solution)/shard_map/all_gather | solution.py:106
  326.4 6.9 copy-start.21
  340.2 32.4 %all-to-all-start.1 = ((bf16[4,256,192]{1,2,0:T(8,128)(2,1)}), bf16[4,256,192]{1,2,0:T(8,128)(2,1)S(1)}, u32[]{:S(2)}, u32[]{:S(2)}) async-start(bf16[4,256,192]{1,2,0:T(8,128)(2,1)} %copy.131), calls=%async_computation.2 | async-start | bytes 786432 | tf_op jit(solution)/shard_map/all_to_all | solution.py:149
  343.7 51.5 %all-gather.23.cloned.1.call-start = ((), (), s32[]{:S(2)}) async-start(), calls=%async_computation.19 | async-start | bytes 1966080 | tf_op jit(solution)/shard_map/all_gather | solution.py:154
  376.7 40.3 %all-gather.25.cloned.1.call-start = ((), (), s32[]{:S(2)}) async-start(), calls=%async_computation.21 | async-start | bytes 1966080 | tf_op jit(solution)/shard_map/all_gather | solution.py:172
  377.6 88.5 %reduce-scatter.17.cloned.1.call-start = ((), (), s32[]{:S(2)}) async-start(), calls=%async_computation.22 | async-start | bytes 3932160 | tf_op jit(solution)/shard_map/reduce_scatter | solution.py:176
  428.0 78.5 %reduce-scatter.15.cloned.1.call-start = ((), (), s32[]{:S(2)}) async-start(), calls=%async_computation.20 | async-start | bytes 3932160 | tf_op jit(solution)/shard_map/reduce_scatter | solution.py:158
  434.1 157.1 %reduce-scatter.19.cloned.1.call-start = ((), (), s32[]{:S(2)}) async-start(), calls=%async_computation.23 | async-start | bytes 3932160 | tf_op jit(solution)/shard_map/reduce_scatter | solution.py:188
  509.4 12.1 %copy-start.23 = (bf16[256,768]{1,0:T(8,128)(2,1)}, bf16[256,768]{1,0:T(8,128)(2,1)S(1)}, u32[]{:S(2)}) copy-start(bf16[256,768]{1,0:T(8,128)(2,1)S(1)} %get-tuple-element.150) | copy-start | bytes 1179652
  522.9 14.3 %slice-start.3 = ((s8[12582912]{0:T(1024)(128)(4,1)}), s8[4194304]{0:T(1024)(128)(4,1)S(1)}, s32[]{:S(2)}) async-start(s8[12582912]{0:T(1024)(128)(4,1)} %bitcast.259), calls=%async_computation.35 | async-start | bytes 8388608
  530.4 7.3 slice-start.5
  553.1 39.6 %copy-start.15 = (f32[256,768]{1,0:T(8,128)S(1)}, f32[256,768]{1,0:T(8,128)}, u32[]{:S(2)}) copy-start(f32[256,768]{1,0:T(8,128)} %get-tuple-element.151) | copy-start | bytes 2359300
  553.2 39.6 %copy-start.16 = (f32[256,768]{1,0:T(8,128)S(1)}, f32[256,768]{1,0:T(8,128)}, u32[]{:S(2)}) copy-start(f32[256,768]{1,0:T(8,128)} %get-tuple-element.169) | copy-start | bytes 2359300
  553.2 61.7 %all-gather.27.cloned.1.call-start = ((), (), s32[]{:S(2)}) async-start(), calls=%async_computation.24 | async-start | bytes 1966080 | tf_op jit(solution)/shard_map/all_gather | solution.py:172
  595.1 68.9 %reduce-scatter.21.cloned.1.call-start = ((), (), s32[]{:S(2)}) async-start(), calls=%async_computation.25 | async-start | bytes 3932160 | tf_op jit(solution)/shard_map/reduce_scatter | solution.py:176
  626.0 135.1 %reduce-scatter.27.cloned.1.call-start = ((), (), s32[]{:S(2)}) async-start(), calls=%async_computation.30 | async-start | bytes 5087232
  642.9 21.1 %copy-start.2 = (f32[256,768]{1,0:T(8,128)S(1)}, f32[256,768]{1,0:T(8,128)}, u32[]{:S(2)}) copy-start(f32[256,768]{1,0:T(8,128)} %copy-done.1) | copy-start | bytes 2359300
  642.9 22.6 %copy-start.18 = (f32[256,768]{1,0:T(8,128)S(1)}, f32[256,768]{1,0:T(8,128)}, u32[]{:S(2)}) copy-start(f32[256,768]{1,0:T(8,128)} %reduce-scatter.13.cloned.1.call-done) | copy-start | bytes 2359300
  643.0 162.8 %reduce-scatter.23.cloned.1.call-start = ((), (), s32[]{:S(2)}) async-start(), calls=%async_computation.26 | async-start | bytes 3932160 | tf_op jit(solution)/shard_map/reduce_scatter | solution.py:188
  668.0 12.6 %copy-start.8 = (bf16[1024,192]{0,1:T(8,128)(2,1)S(1)}, bf16[1024,192]{0,1:T(8,128)(2,1)}, u32[]{:S(2)}) copy-start(bf16[1024,192]{0,1:T(8,128)(2,1)} %copy-done.7) | copy-start | bytes 1179652
  680.6 24.8 %slice-start = ((s8[12582912]{0:T(1024)(128)(4,1)}), s8[4194304]{0:T(1024)(128)(4,1)S(1)}, s32[]{:S(2)}) async-start(s8[12582912]{0:T(1024)(128)(4,1)} %bitcast.257), calls=%async_computation.32 | async-start | bytes 8388608
  680.6 24.8 %slice-start.1 = ((s8[12582912]{0:T(1024)(128)(4,1)}), s8[4194304]{0:T(1024)(128)(4,1)S(1)}, s32[]{:S(2)}) async-start(s8[12582912]{0:T(1024)(128)(4,1)} %bitcast.257), calls=%async_computation.33 | async-start | bytes 8388608
  691.7 10.3 %copy-start.26 = (bf16[1024,192]{0,1:T(8,128)(2,1)S(1)}, bf16[1024,192]{0,1:T(8,128)(2,1)}, u32[]{:S(2)}) copy-start(bf16[1024,192]{0,1:T(8,128)(2,1)} %copy-done.25) | copy-start | bytes 1179652
  691.7 13.7 %slice-start.2 = ((s8[12582912]{0:T(1024)(128)(4,1)}), s8[4194304]{0:T(1024)(128)(4,1)S(1)}, s32[]{:S(2)}) async-start(s8[12582912]{0:T(1024)(128)(4,1)} %bitcast.257), calls=%async_computation.34 | async-start | bytes 8388608
  710.7 188.8 %reduce-scatter.25.cloned.1.call-start = ((), (), s32[]{:S(2)}) async-start(), calls=%async_computation.29 | async-start | bytes 5087232
  726.9 78.9 %copy-start.4 = (bf16[1,256,768]{2,1,0:T(8,128)(2,1)S(1)}, bf16[1,256,768]{2,1,0:T(8,128)(2,1)}, u32[]{:S(2)}) copy-start(bf16[1,256,768]{2,1,0:T(8,128)(2,1)} %param.13) | copy-start | bytes 1179652
  726.9 78.9 %copy-start.43 = (f32[768]{0:T(1024)S(1)}, f32[768]{0:T(1024)}, u32[]{:S(2)}) copy-start(f32[768]{0:T(1024)} %copy-done.42) | copy-start | bytes 9220
  726.9 78.9 %copy-start.46 = (f32[256]{0:T(256)S(1)}, f32[256]{0:T(256)}, u32[]{:S(2)}) copy-start(f32[256]{0:T(256)} %copy-done.45) | copy-start | bytes 3076
  727.0 78.9 %copy-start.48 = (f32[256]{0:T(256)S(1)}, f32[256]{0:T(256)}, u32[]{:S(2)}) copy-start(f32[256]{0:T(256)} %copy-done.47) | copy-start | bytes 3076
  727.0 239.4 %all-reduce.4.cloned.1.call-start = ((), (), s32[]{:S(2)}) async-start(), calls=%async_computation.27 | async-start | bytes 786432 | tf_op jit(solution)/shard_map/psum | solution.py:213
  902.7 65.6 %all-gather.29.cloned.1.call-start = ((), (), s32[]{:S(2)}) async-start(), calls=%async_computation.28 | async-start | bytes 4177920 | tf_op jit(solution)/shard_map/all_gather | solution.py:208
  905.3 45.3 %copy-start.6 = (bf16[2,96,4608]{2,1,0:T(8,128)(2,1)S(1)}, bf16[2,96,4608]{2,1,0:T(8,128)(2,1)}, u32[]{:S(2)}) copy-start(bf16[2,96,4608]{2,1,0:T(8,128)(2,1)} %param.15) | copy-start | bytes 5308420
  952.9 11.7 %all-to-all-start.4 = ((f32[8,1,96]{2,1,0:T(1,128)}), f32[8,1,96]{2,1,0:T(1,128)S(1)}, u32[]{:S(2)}, u32[]{:S(2)}) async-start(f32[8,1,96]{2,1,0:T(1,128)} %bitcast.68), calls=%async_computation.10 | async-start | bytes 8192 | tf_op jit(solution)/shard_map/all_to_all | solution.py:233
  (42 other events, 142.9 us)
Sparse Core Ops, SparseCore 0:
  49.0 72.1 all-reduce.5
  123.8 18.6 all-gather.12
  145.3 67.1 all-gather.14
  216.5 18.3 all-gather.16
  244.9 37.8 reduce-scatter.12
  285.5 19.6 all-gather.18
  307.9 64.5 all-gather.20
  376.8 18.3 all-gather.22
  397.3 19.6 all-gather.24
  428.2 37.8 reduce-scatter.16
  468.6 37.8 reduce-scatter.14
  553.3 37.8 reduce-scatter.18
  595.2 19.6 all-gather.26
  626.1 37.8 reduce-scatter.20
  667.5 93.5 reduce-scatter.26
  764.0 37.6 reduce-scatter.22
  805.2 94.2 reduce-scatter.24
  902.9 32.6 all-reduce.3
  937.6 29.6 all-gather.28

commit v2 on v1

--- a/solution.py
+++ b/solution.py
@@ -1,6 +1,10 @@
+import functools
+
 import jax
 import jax.numpy as jnp
 from jax import lax
+from jax.experimental import pallas as pl
+from jax.experimental.pallas import tpu as pltpu
 from jax.sharding import PartitionSpec as P
 
 HEAD_DIM = 64
@@ -76,7 +80,7 @@
     return value, slope
 
 
-def per_device(
+def plain_device(
     tokens, condition, ada_weight, ada_bias, qkv_weight, qv_bias, out_weight, out_bias,
     up_weight, up_bias, down_weight, down_bias, cotangent,
 ):
@@ -239,10 +243,528 @@
     )
 
 
+MESH = pl.DeviceIdType.MESH
+FAST = 2
+VMEM_LIMIT = 66_000_000
+
+
+def rcopy(src, dst, send, recv, device):
+    return pltpu.make_async_remote_copy(
+        src_ref=src, dst_ref=dst, send_sem=send, recv_sem=recv, device_id=device, device_id_type=MESH
+    )
+
+
+def vmem_specs(count):
+    return [pl.BlockSpec(memory_space=pltpu.VMEM)] * count
+
+
+def entry_barrier(devices):
+    barrier = pltpu.get_barrier_semaphore()
+    for device in devices:
+        pl.semaphore_signal(barrier, inc=1, device_id=device, device_id_type=MESH)
+    pl.semaphore_wait(barrier, len(devices))
+
+
+def relative(s, j):
+    half = j // 2
+    return ((s // 2 + 1 - half) % 2) * 2 + (s % 2 + half + j) % 2
+
+
+def prep_kernel(n, cond_ref, small_ref, ada_ref, rows_ref, small_all, mod_ref,
+                crecv, msend, mrecv, c_s, c_r, b_s, b_r, m_s, m_r):
+    f = lax.axis_index("fsdp")
+    layers, rows, _ = ada_ref.shape
+    others = [{"fsdp": (f + k) % n} for k in range(1, n)]
+    entry_barrier(others)
+    first, second = [], []
+    for k in range(1, n):
+        to = (f + k) % n
+        first.append(rcopy(cond_ref.at[to], crecv.at[f], c_s.at[k], c_r.at[k], {"fsdp": to}))
+        first[-1].start()
+    for k in range(1, n):
+        to = (f + k) % n
+        second.append(rcopy(small_ref, small_all.at[f], b_s.at[k], b_r.at[k], {"fsdp": to}))
+        second[-1].start()
+    crecv[f] = cond_ref[f]
+    small_all[f] = small_ref[...]
+    for k in range(1, n):
+        at = (f - k + n) % n
+        rcopy(cond_ref.at[at], crecv.at[at], c_s.at[k], c_r.at[k], {"fsdp": at}).wait_recv()
+    cond_rows = jnp.sum(crecv[...], axis=1)
+    rows_ref[...] = cond_rows
+    cond_rows = cond_rows[:, :rows].astype(BF16)
+    for l in range(layers):
+        part = mm(cond_rows, ada_ref[l])
+        for i in range(n):
+            msend[i, l: l + 1, :] = part[i: i + 1, :]
+    third = []
+    for k in range(1, n):
+        to = (f + k) % n
+        third.append(rcopy(msend.at[to], mrecv.at[f], m_s.at[k], m_r.at[k], {"fsdp": to}))
+        third[-1].start()
+    mrecv[f] = msend[f]
+    for k in range(1, n):
+        at = (f - k + n) % n
+        rcopy(msend.at[at], mrecv.at[at], m_s.at[k], m_r.at[k], {"fsdp": at}).wait_recv()
+    mod_ref[...] = jnp.sum(mrecv[...], axis=0)
+    for k in range(1, n):
+        at = (f - k + n) % n
+        rcopy(small_ref, small_all.at[at], b_s.at[k], b_r.at[k], {"fsdp": at}).wait_recv()
+    for copy in first + second + third:
+        copy.wait_send()
+
+
+def prep(n, cond_blocks, small, ada_weight):
+    layers, rows, width6 = ada_weight.shape
+    lanes = cond_blocks.shape[-1]
+    return pl.pallas_call(
+        functools.partial(prep_kernel, n),
+        out_shape=(
+            jax.ShapeDtypeStruct((n, lanes), F32),
+            jax.ShapeDtypeStruct((n,) + small.shape, F32),
+            jax.ShapeDtypeStruct((layers, width6), F32),
+        ),
+        in_specs=vmem_specs(3),
+        out_specs=tuple(vmem_specs(3)),
+        scratch_shapes=[
+            pltpu.VMEM((n, 8, lanes), F32),
+            pltpu.VMEM((n, layers, width6), F32),
+            pltpu.VMEM((n, layers, width6), F32),
+        ] + [pltpu.SemaphoreType.DMA((n,))] * 6,
+        compiler_params=pltpu.CompilerParams(collective_id=0, has_side_effects=True),
+    )(cond_blocks, small, ada_weight)
+
+
+def forward_kernel(n, *refs):
+    (x_ref, mod_ref, bq_ref, bo_ref, bu_ref, bd_ref, sq_ref, so_ref, su_ref, sd_ref,
+     out_ref, wq_ref, wo_ref, wu_ref, wd_ref, xs_ref, attn_ref, qh_ref, tok_ref, branch_ref,
+     mid_ref, mlp_ref, up_ref, feed_ref,
+     osend, psend, precv, xsend, xrecv, own_feed,
+     z_s, z_r, y_s, y_r, a_s, a_r, t_s, t_r, g_s, g_r, r_s, r_r) = refs
+    f = lax.axis_index("fsdp")
+    s = lax.axis_index("seq")
+    slow = n // FAST
+    a, b = f // FAST, f % FAST
+    layers, rows = sq_ref.shape[0], sq_ref.shape[1]
+    block = x_ref.shape[0]
+    width = x_ref.shape[1]
+    hc = sq_ref.shape[2] // 3
+    heads = hc // HEAD_DIM
+    shards = (sq_ref, so_ref, su_ref, sd_ref)
+    full = (wq_ref, wo_ref, wu_ref, wd_ref)
+    across, diagonal, partner = relative(s, 0), relative(s, 1), relative(s, 2)
+    y_dev = {"fsdp": a * FAST + (1 - b)}
+
+    entry_barrier(
+        [{"fsdp": ((a + k) % slow) * FAST + b} for k in range(1, slow)] + [y_dev]
+        + [{"seq": across}, {"seq": diagonal}, {"seq": partner}]
+    )
+
+    def z_copy(l, p, k, to):
+        return rcopy(shards[p].at[l], full[p].at[l, f], z_s.at[l, p, k], z_r.at[l, p, k], {"fsdp": to})
+
+    def y_copy(l, p, k):
+        at = ((a - k + slow) % slow) * FAST + b
+        src = shards[p].at[l] if k == 0 else full[p].at[l, at]
+        return rcopy(src, full[p].at[l, at], y_s.at[l, p, k], y_r.at[l, p, k], y_dev)
+
+    for l in range(layers):
+        for p in range(4):
+            y_copy(l, p, 0).start()
+            for k in range(1, slow):
+                z_copy(l, p, k, ((a + k) % slow) * FAST + b).start()
+
+    def forward_weights(l, p):
+        for k in range(1, slow):
+            at = ((a - k + slow) % slow) * FAST + b
+            rcopy(shards[p].at[l], full[p].at[l, at], z_s.at[l, p, k], z_r.at[l, p, k], {"fsdp": at}).wait_recv()
+            y_copy(l, p, k).start()
+
+    def ready(l, p):
+        for k in range(slow):
+            at = ((a - k + slow) % slow) * FAST + 1 - b
+            rcopy(shards[p].at[l], full[p].at[l, at], y_s.at[l, p, k], y_r.at[l, p, k], y_dev).wait_recv()
+
+    xs_ref[0] = x_ref[...].astype(F32)
+    for l in range(layers):
+        for p in range(4):
+            full[p][l, f] = shards[p][l]
+
+    def matrix(ref, l):
+        return ref[l].reshape(n * rows, ref.shape[3])
+
+    def gather(buf, l, send, recv, visit):
+        mine = buf.at[l, s]
+        to_partner = rcopy(mine, mine, send.at[0], recv.at[0], {"seq": partner})
+        to_across = rcopy(mine, mine, send.at[1], recv.at[1], {"seq": across})
+        to_across.start()
+        to_partner.start()
+        theirs = buf.at[l, across]
+        relay = rcopy(theirs, theirs, send.at[2], recv.at[2], {"seq": partner})
+
+        def step(i, carry):
+            @pl.when(i == 1)
+            def _():
+                ref = buf.at[l, partner]
+                rcopy(ref, ref, send.at[0], recv.at[0], {"seq": partner}).wait_recv()
+
+            @pl.when(i == 2)
+            def _():
+                rcopy(theirs, theirs, send.at[1], recv.at[1], {"seq": across}).wait_recv()
+                relay.start()
+
+            @pl.when(i == 3)
+            def _():
+                ref = buf.at[l, diagonal]
+                rcopy(ref, ref, send.at[2], recv.at[2], {"seq": partner}).wait_recv()
+
+            visit(i, relative(s, pick(i)))
+            return carry
+
+        lax.fori_loop(0, 4, step, 0)
+        for copy in (to_partner, to_across, relay):
+            copy.wait_send()
+
+    def pick(i):
+        return (3 - i) * (1 - i // 2) + (i - 2) * (i // 2)
+
+    def layer(l, carry):
+        row = lambda i: mod_ref[l, i: i + 1, :]
+        x = xs_ref[l]
+        normed, _ = normalize(x)
+        attn_ref[l, s] = (normed * (1.0 + row(1)) + row(0)).astype(BF16)
+
+        @pl.when(l == 0)
+        def _():
+            forward_weights(0, 0)
+
+        def qkv_block(i, t):
+            @pl.when(i == 0)
+            def _():
+                ready(l, 0)
+
+            val = (mm(attn_ref[l, t], matrix(wq_ref, l)) + bq_ref[l]).astype(BF16)
+            for h in range(3 * heads):
+                qh_ref[l, h, pl.ds(pl.multiple_of(t * block, block), block), :] = (
+                    val[:, h * HEAD_DIM: (h + 1) * HEAD_DIM]
+                )
+
+        gather(attn_ref, l, a_s, a_r, qkv_block)
+        forward_weights(l, 1)
+
+        def attend_block(j, carry):
+            t = relative(s, j)
+            outs = []
+            for h in range(heads):
+                q = qh_ref[l, h, pl.ds(pl.multiple_of(t * block, block), block), :]
+                scores = mm_nt(q, qh_ref[l, heads + h]) * SCORE_SCALE
+                e = jnp.exp(scores)
+                inverse = 1.0 / jnp.sum(e, axis=-1, keepdims=True)
+                prob = (e * inverse).astype(BF16)
+                outs.append(mm(prob, qh_ref[l, 2 * heads + h]))
+            osend[j] = jnp.concatenate(outs, axis=1).astype(BF16)
+
+            @pl.when(j < 3)
+            def _():
+                rcopy(osend.at[j], tok_ref.at[l, s], t_s.at[j], t_r.at[j], {"seq": t}).start()
+
+            @pl.when(j == 1)
+            def _():
+                forward_weights(l, 2)
+
+            return carry
+
+        lax.fori_loop(0, 4, attend_block, 0)
+        tok_ref[l, s] = osend[3]
+        forward_weights(l, 3)
+        ready(l, 1)
+        for j in range(3):
+            t = relative(s, j)
+            rcopy(osend.at[j], tok_ref.at[l, t], t_s.at[j], t_r.at[j], {"seq": t}).wait_recv()
+        tokens_out = jnp.concatenate([tok_ref[l, t] for t in range(4)], axis=1)
+        branch = mm(tokens_out, matrix(wo_ref, l)) + bo_ref[l]
+        branch_ref[l] = branch
+        middle = xs_ref[l] + row(2) * branch
+        mid_ref[l] = middle
+        normed, _ = normalize(middle)
+        mlp_ref[l, s] = (normed * (1.0 + row(4)) + row(3)).astype(BF16)
+
+        def mlp_block(i, t):
+            @pl.when(i == 0)
+            def _():
+                ready(l, 2)
+                ready(l, 3)
+
+            up = mm(mlp_ref[l, t], matrix(wu_ref, l)) + bu_ref[l]
+            up_ref[l, t] = up
+            act = gelu_parts(up)[0].astype(BF16)
+            part = mm(act, matrix(wd_ref, l))
+
+            @pl.when(i == 0)
+            def _():
+                own_feed[...] = part
+
+            @pl.when(i == 1)
+            def _():
+                psend[0] = part
+                rcopy(psend.at[0], precv.at[0], r_s.at[0], r_r.at[0], {"seq": partner}).start()
+
+            @pl.when(i == 2)
+            def _():
+                xsend[...] = part
+
+            @pl.when(i == 3)
+            def _():
+                psend[1] = part
+                rcopy(psend.at[1], precv.at[1], r_s.at[1], r_r.at[1], {"seq": partner}).start()
+
+            @pl.when((i == 1) & (l + 1 < layers))
+            def _():
+                forward_weights(1, 0)
+
+        gather(mlp_ref, l, g_s, g_r, mlp_block)
+        rcopy(psend.at[1], precv.at[1], r_s.at[1], r_r.at[1], {"seq": partner}).wait_recv()
+        xsend[...] = xsend[...] + precv[1]
+        over = rcopy(xsend, xrecv, r_s.at[2], r_r.at[2], {"seq": across})
+        over.start()
+        rcopy(psend.at[0], precv.at[0], r_s.at[0], r_r.at[0], {"seq": partner}).wait_recv()
+        own_feed[...] = own_feed[...] + precv[0] + bd_ref[l]
+        over.wait_recv()
+        feed = own_feed[...] + xrecv[...]
+        feed_ref[l] = feed
+        nxt = mid_ref[l] + row(5) * feed
+
+        @pl.when(l + 1 < layers)
+        def _():
+            xs_ref[1] = nxt
+
+        @pl.when(l + 1 == layers)
+        def _():
+            out_ref[...] = nxt.astype(BF16)
+
+        over.wait_send()
+        for i in range(2):
+            rcopy(psend.at[i], precv.at[i], r_s.at[i], r_r.at[i], {"seq": partner}).wait_send()
+        for j in range(3):
+            rcopy(osend.at[j], tok_ref.at[l, s], t_s.at[j], t_r.at[j], {"seq": relative(s, j)}).wait_send()
+        return carry
+
+    lax.fori_loop(0, layers, layer, 0)
+    for l in range(layers):
+        for p in range(4):
+            y_copy(l, p, 0).wait_send()
+            for k in range(1, slow):
+                z_copy(l, p, k, ((a + k) % slow) * FAST + b).wait_send()
+                y_copy(l, p, k).wait_send()
+
+
+def forward(n, x, mod, bq, bo, bu, bd, sq, so, su, sd):
+    layers, rows, qc = sq.shape
+    block, width = x.shape
+    hc = qc // 3
+    nh = qc // HEAD_DIM
+    uc = su.shape[2]
+    total = 4 * block
+    sds = jax.ShapeDtypeStruct
+    outs = (
+        sds((block, width), BF16),
+        sds((layers, n, rows, qc), BF16),
+        sds((layers, n, rows, width), BF16),
+        sds((layers, n, rows, uc), BF16),
+        sds((layers, n, rows, width), BF16),
+        sds((layers, block, width), F32),
+        sds((layers, 4, block, width), BF16),
+        sds((layers, nh, total, HEAD_DIM), BF16),
+        sds((layers, 4, block, hc), BF16),
+        sds((layers, block, width), F32),
+        sds((layers, block, width), F32),
+        sds((layers, 4, block, width), BF16),
+        sds((layers, 4, block, uc), F32),
+        sds((layers, block, width), F32),
+    )
+    slow = n // FAST
+    dma = pltpu.SemaphoreType.DMA
+    scratch = [
+        pltpu.VMEM((4, block, hc), BF16),
+        pltpu.VMEM((2, block, width), F32),
+        pltpu.VMEM((2, block, width), F32),
+        pltpu.VMEM((block, width), F32),
+        pltpu.VMEM((block, width), F32),
+        pltpu.VMEM((block, width), F32),
+    ] + [dma((layers, 4, slow))] * 4 + [dma((3,))] * 8
+    return pl.pallas_call(
+        functools.partial(forward_kernel, n),
+        out_shape=outs,
+        in_specs=vmem_specs(10),
+        out_specs=tuple(vmem_specs(len(outs))),
+        scratch_shapes=scratch,
+        compiler_params=pltpu.CompilerParams(
+            collective_id=1, has_side_effects=True, vmem_limit_bytes=VMEM_LIMIT
+        ),
+    )(x, mod, bq, bo, bu, bd, sq, so, su, sd)
+
+
+def fused_device(
+    tokens, condition, ada_weight, ada_bias, qkv_weight, qv_bias, out_weight, out_bias,
+    up_weight, up_bias, down_weight, down_bias, cotangent,
+):
+    n = lax.axis_size("fsdp")
+    ns = lax.axis_size("seq")
+    f = lax.axis_index("fsdp")
+    s = lax.axis_index("seq")
+    layers, rows, width6 = ada_weight.shape
+    width = rows * n
+    ff = up_weight.shape[2]
+    hc = width // ns
+    fc = ff // (ns * n)
+
+    def take(x, axis):
+        return lax.dynamic_index_in_dim(x, s, axis, keepdims=False)
+
+    def own(x, axis, size):
+        return lax.dynamic_slice_in_dim(x, f * size, size, axis)
+
+    fw = n * fc
+    s_q = take(qkv_weight.reshape(layers, rows, 3, ns, hc), 3).reshape(layers, rows, 3 * hc)
+    s_u = take(up_weight.reshape(layers, rows, n, ns, fc), 3).reshape(layers, rows, fw)
+    s_d = take(down_weight.reshape(layers, ns, fc, width), 1)
+
+    cond_float = condition.astype(F32)
+    cond_act = jax.nn.silu(cond_float).astype(BF16)
+    cond_blocks = jnp.pad(cond_act.astype(F32).reshape(n, 1, rows), ((0, 0), (0, 7), (0, -rows % 128)))
+    small = jnp.concatenate(
+        [ada_bias.reshape(-1), qv_bias.reshape(-1), out_bias.reshape(-1), up_bias.reshape(-1),
+         down_bias.reshape(-1)]
+    ).astype(F32).reshape(8, -1)
+    cond_rows, small, mod = prep(n, cond_blocks, small, ada_weight)
+    cond_rows = cond_rows[:, :rows]
+    small = small.reshape(n, -1)
+    pos = 0
+
+    def unpack(per_layer):
+        nonlocal pos
+        part = small[:, pos: pos + layers * per_layer].reshape(n, layers, per_layer)
+        pos += layers * per_layer
+        return part.transpose(1, 0, 2).reshape(layers, n * per_layer)
+
+    ada_b = unpack(ada_bias.shape[1])
+    qv_b = unpack(qv_bias.shape[1])
+    out_b = unpack(out_bias.shape[1])
+    up_b = unpack(up_bias.shape[1])
+    down_b = unpack(down_bias.shape[1])
+    q_b = take(qv_b[:, :width].reshape(layers, ns, hc), 1)
+    v_b = take(qv_b[:, width:].reshape(layers, ns, hc), 1)
+    qkv_b = jnp.concatenate([q_b, jnp.zeros_like(q_b), v_b], axis=1)
+    up_bs = take(up_b.reshape(layers, n, ns, fc), 2).reshape(layers, fw)
+    mod = mod + ada_b
+
+    (block_out, w_q, w_o, w_u, w_d, xs, attn, qh, tok, branches, mids, mlp, ups, feeds) = forward(
+        n, tokens[0], mod.reshape(layers, 6, width), qkv_b[:, None], out_b[:, None], up_bs[:, None],
+        down_b[:, None], s_q, out_weight, s_u, s_d)
+    saved, w_qkv, w_rest = [], [], []
+    nh = hc // HEAD_DIM
+    for l in range(layers):
+        n_a, r_a = normalize(xs[l])
+        n_m, r_m = normalize(mids[l])
+        q, k, v = [join_heads(qh[l, i * nh: (i + 1) * nh]) for i in range(3)]
+        scores = jnp.einsum("hqd,hkd->hqk", split_heads(q), split_heads(k), preferred_element_type=F32) * SCORE_SCALE
+        logsum = jnp.log(jnp.sum(jnp.exp(scores), axis=-1, keepdims=True))
+        up = ups[l].reshape(-1, fw)
+        saved.append((n_a, r_a, attn[l].reshape(-1, width), q, k, v, logsum,
+                      tok[l].transpose(1, 0, 2).reshape(-1, width), branches[l], n_m, r_m,
+                      mlp[l].reshape(-1, width), up, gelu_parts(up)[0].astype(BF16), feeds[l]))
+        w_qkv.append(w_q[l].reshape(width, -1))
+        w_rest.append(jnp.concatenate([w.reshape(width, -1) for w in (w_u[l], w_d[l], w_o[l])], axis=1))
+
+    g = cotangent[0].astype(F32)
+    d_mods = [None] * layers
+    reduced = [None] * layers
+    bias_grads = [None] * layers
+    for l in reversed(range(layers)):
+        shift_a, scale_a, gate_a, shift_m, scale_m, gate_m = jnp.split(mod[l], 6)
+        n_a, r_a, attn_all, q, k, v, logsum, tok_out, branch, n_m, r_m, mlp_all, up, act, feed = saved[l]
+        g_feed = (gate_m * g).astype(BF16)
+        d_gate_m = jnp.sum(g * feed, axis=0)
+        g_feed_all = lax.all_gather(g_feed, "seq", axis=0, tiled=True)
+        grad_down = mm_tn(act, g_feed_all)
+        g_up = (mm_nt(g_feed_all, w_rest[l][:, fw: fw + width]) * gelu_parts(up)[1]).astype(BF16)
+        grad_up = mm_tn(mlp_all, g_up)
+        g_min = lax.psum_scatter(mm_nt(g_up, w_rest[l][:, :fw]), "seq", scatter_dimension=0, tiled=True)
+        d_scale_m = jnp.sum(g_min * n_m, axis=0)
+        d_shift_m = jnp.sum(g_min, axis=0)
+        g_mid = g + norm_back(g_min * (1.0 + scale_m), n_m, r_m)
+        g_branch = (gate_a * g_mid).astype(BF16)
+        d_gate_a = jnp.sum(g_mid * branch, axis=0)
+        grad_out = mm_tn(tok_out, g_branch)
+        g_o = mm_nt(g_branch, w_rest[l][:, fw + width:]).astype(BF16)
+        g_o_heads = lax.all_to_all(g_o, "seq", split_axis=1, concat_axis=0, tiled=True)
+        dq, dk, dv = attend_back(q, k, v, logsum, g_o_heads)
+        g_qkv = jnp.concatenate([dq, dk, dv], axis=1)
+        grad_qkv = mm_tn(attn_all, g_qkv)
+        g_ain = lax.psum_scatter(mm_nt(g_qkv, w_qkv[l]), "seq", scatter_dimension=0, tiled=True)
+        d_scale_a = jnp.sum(g_ain * n_a, axis=0)
+        d_shift_a = jnp.sum(g_ain, axis=0)
+        g = g_mid + norm_back(g_ain * (1.0 + scale_a), n_a, r_a)
+        d_mods[l] = jnp.concatenate([d_shift_a, d_scale_a, d_gate_a, d_shift_m, d_scale_m, d_gate_m])
+        packed = jnp.concatenate([grad_up, grad_down, grad_out, grad_qkv], axis=1).astype(BF16)
+        reduced[l] = lax.psum_scatter(packed, "fsdp", scatter_dimension=0, tiled=True)
+
+        def place(x, axis):
+            zeros = jnp.zeros(x.shape[:axis] + (ns,) + x.shape[axis + 1:], F32)
+            return lax.dynamic_update_slice_in_dim(zeros, x, s, axis)
+
+        qv_g = place(jnp.stack([jnp.sum(dq.astype(F32), axis=0), jnp.sum(dv.astype(F32), axis=0)])[:, None, :], 1)
+        up_g = place(jnp.sum(g_up.astype(F32), axis=0).reshape(n, 1, fc), 1)
+        bias_grads[l] = jnp.concatenate([
+            qv_g.reshape(n, -1), jnp.sum(g_branch.astype(F32), axis=0).reshape(n, -1),
+            up_g.reshape(n, -1), jnp.sum(g_feed.astype(F32), axis=0).reshape(n, -1)], axis=1)
+
+    red = jnp.stack(reduced)
+    shared = jnp.concatenate([red[:, :, : fw + width], red[:, :, fw + 2 * width:]], axis=2)
+    shared = lax.all_gather(shared, "seq", axis=0, tiled=False).astype(F32)
+    grad_up = shared[..., :fw].reshape(ns, layers, rows, n, fc).transpose(1, 2, 3, 0, 4).reshape(layers, rows, ff)
+    grad_down = shared[..., fw: fw + width].transpose(1, 0, 2, 3).reshape(layers, ns * fc, width)
+    grad_qkv = shared[..., fw + width:].reshape(ns, layers, rows, 3, hc).transpose(1, 2, 3, 0, 4)
+    grad_qkv = grad_qkv.reshape(layers, rows, 3 * width)
+    grad_out = lax.psum(red[:, :, fw + width: fw + 2 * width], "seq").astype(F32)
+
+    bias = lax.psum(jnp.stack(bias_grads), ("fsdp", "seq"))
+    bias = lax.dynamic_index_in_dim(bias, f, 1, keepdims=False)
+    cuts = [qv_bias.shape[1], out_bias.shape[1], up_bias.shape[1], down_bias.shape[1]]
+    grad_bias, at = [], 0
+    for size in cuts:
+        grad_bias.append(bias[:, at: at + size])
+        at += size
+
+    d_mod = lax.psum(jnp.stack(d_mods), "seq")
+    d_mod_all = lax.all_gather(d_mod, "fsdp", axis=0, tiled=False)
+    cond_rows32 = cond_rows.astype(F32)
+    grad_ada = jnp.stack([
+        lax.dot_general(cond_rows32, d_mod_all[:, l], (((0,), (0,)), ((), ())), precision=HIGHEST,
+                        preferred_element_type=F32) for l in range(layers)])
+    grad_ada_bias = own(jnp.sum(d_mod_all, axis=0), 1, width6 // n)
+    g_cond = sum(
+        lax.dot_general(d_mod_all[:, l], ada_weight[l].astype(F32), (((1,), (1,)), ((), ())),
+                        precision=HIGHEST, preferred_element_type=F32) for l in range(layers))
+    g_cond = lax.all_to_all(g_cond, "fsdp", split_axis=0, concat_axis=1, tiled=True)
+    _, silu_back = jax.vjp(jax.nn.silu, cond_float)
+    grad_condition = silu_back(g_cond)[0]
+    return (
+        block_out[None], g[None], grad_condition, grad_ada, grad_ada_bias, grad_qkv, grad_bias[0],
+        grad_out, grad_bias[1], grad_up, grad_bias[2], grad_down, grad_bias[3],
+    )
+
+
 def solution(mesh):
     token = P("fsdp", "seq", None)
     matrix = P(None, "fsdp", None)
     vector = P(None, "fsdp")
+
+    def per_device(*args):
+        rows = args[2].shape[1]
+        fits = rows % 32 == 0 and mesh.shape["seq"] == 4 and args[0].shape[0] == 1
+        return (fused_device if fits else plain_device)(*args)
+
     return jax.shard_map(
         per_device,
         mesh=mesh,

time: 1020 us -> 834 us (0.82)
  waiting for transfers between devices: 486 us -> 218 us
  Pallas kernels: 0 us -> 206 us
  blocking collectives: 203 us -> 93.6 us
  matrix products: 144 us -> 104 us
  local copies, waits for them, and re-layouts: 90.3 us -> 115 us
    pallas_call x0 -> x2, Pallas kernels: none -> 206 us  [the longest x1 186 us: forward(): pl.pallas_call(functools.partial(forward_kernel, n), out_shape=outs, in_s...]
    all_gather x4 -> x1, blocking collectives: 131 us -> 30.9 us  [fused_device(): d_mod_all = lax.all_gather(d_mod, 'fsdp', axis=0, tiled=False)]
    all_gather x9 -> x3, waiting for transfers between devices: 116 us -> 19.3 us  [the longest x2 19.3 us: fused_device(): g_feed_all = lax.all_gather(g_feed, 'seq', axis=0, tiled=True)]
    unnamed x22 -> x12, waiting for transfers between devices: 196 us -> 110 us
    reduce_scatter x6 -> x4, waiting for transfers between devices: 168 us -> 84.2 us  [the longest x2 49 us: fused_device(): lax.psum_scatter(mm_nt(g_up, w_rest[l][:, :fw]), 'seq', scatter_dimension...]
    dot_general x16 -> x4, matrix products: 50 us -> 5.35 us  [the longest x2 3.14 us: fused_device(): lax.dot_general(cond_rows32, d_mod_all[:, l], (((0,), (0,)), ((), ())), p...]
    slice x14 -> x13, local copies, waits for them, and re-layouts: 9.22 us -> 22 us  [the longest x1 3.89 us: fused_device(): mlp[l].reshape(-1, width)]
    reduce_sum x2, matrix products: 13.8 us -> 26.3 us  [fused_device(): logsum = jnp.log(jnp.sum(jnp.exp(scores), axis=-1, keepdims=True))]
  transfers between devices with their start and end apart: 22 -> 12, of which waited for: 16 -> 8; matrix products, arithmetic and copies ran while one was open for 15% -> 17% of each run, Pallas kernels for 0% -> 23%
where the time goes in v2:
time: 834 us; the launch traced here: 823 us
  waiting for transfers between devices  218 us (26%)
  Pallas kernels  206 us (25%)
  local copies, waits for them, and re-layouts  115 us (14%)
  matrix products  104 us (12%)
  blocking collectives  93.6 us (11%)
  other arithmetic  61.7 us (7%)
  between operations  15.7 us (2%)
  starting transfers between devices  8.84 us (1%)
    pallas_call x1, Pallas kernels, forward(): pl.pallas_call(functools.partial(forward_kernel, n), out_shape=outs, in_s...  186 us
    unnamed x12, waiting for transfers between devices  110 us
    reduce_scatter x2, waiting for transfers between devices, fused_device(): lax.psum_scatter(mm_nt(g_up, w_rest[l][:, :fw]), 'seq', scatter_dimension...  49 us
    psum x1, blocking collectives, fused_device(): bias = lax.psum(jnp.stack(bias_grads), ('fsdp', 'seq'))  40.9 us
    reduce_scatter x2, waiting for transfers between devices, fused_device(): lax.psum_scatter(mm_nt(g_qkv, w_qkv[l]), 'seq', scatter_dimension=0, tile...  35.2 us
    unnamed x147, local copies, waits for them, and re-layouts  31.5 us
    all_gather x1, blocking collectives, fused_device(): d_mod_all = lax.all_gather(d_mod, 'fsdp', axis=0, tiled=False)  30.9 us
    reduce_sum x2, matrix products, fused_device(): logsum = jnp.log(jnp.sum(jnp.exp(scores), axis=-1, keepdims=True))  26.3 us
  transfers between devices with their start and end apart: 12, of which 8 were waited for; matrix products, arithmetic and copies ran while one was open for 17% of the time, Pallas kernels for 23%

profile of v2, /device:TPU:0, one launch (start us, length us, event | category | flops | bytes accessed | tf_op | source)
XLA Modules:
  0.0 823.1 jit_solution(4197014731732370818)
XLA Ops:
  13.7 19.3 %shard_map.228 = (f32[8,128]{1,0:T(8,128)}, f32[8,8,336]{2,1,0:T(8,128)}, f32[2,4608]{1,0:T(2,128)}) custom-call(f32[8,8,128]{2,1,0:T(8,128)} %pad_convert_fusion.cond_ref, f32[8,336]{1,0:T(8,128)} %reshape.336.small_ref, bf16[2,96,4608]{2,1,0:T(8,128)(2,1)} %ada_ref.1), custom_call_target="tpu_custom_call" | custom-call | tf_op jit(solution)/shard_map/pallas_call | solution.py:320
  54.1 186.4 %shard_map.229 = (bf16[256,768]{1,0:T(8,128)(2,1)}, bf16[2,8,96,576]{3,2,1,0:T(8,128)(2,1)}, bf16[2,8,96,768]{3,2,1,0:T(8,128)(2,1)}, bf16[2,8,96,768]{3,2,1,0:T...) custom-call(bf16[256,768]{1,0:T(8,128)(2,1)} %bitcast.362, ...), custom_call_target="tpu_custom_call" | custom-call | tf_op jit(solution)/shard_map/pallas_call | solution.py:595
  240.5 3.3 fusion.154
  248.7 6.3 convert_reduce_fusion
  256.1 3.1 fusion.176
  262.6 38.3 %reduce-scatter.11.cloned.1.call-done = f32[256,768]{1,0:T(8,128)} async-done(((f32[1024,768]{1,0:T(8,128)}), f32[256,768]{1,0:T(8,128)}) %reduce-scatter.11.cloned.1.call-update) | async-done | bytes 786448 | tf_op jit(solution)/shard_map/reduce_scatter | solution.py:692
  303.1 3.0 convert_reduce_fusion.3
  307.5 3.5 all-to-all-start
  314.0 4.4 all-to-all-done
  318.9 7.5 fusion.78
  326.4 13.2 %multiply_reduce_fusion.1 = (f32[3,1024]{1,0:T(4,128)S(1)}, f32[3,1024,1024]{1,2,0:T(8,128)}) fusion(f32[3,1024,1024]{1,2,0:T(8,128)} %fusion.78, bf16[2,9,1024,64]{3,2,1,0:T(8,128)(2,1)} %get-tuple-element.38), kind=kOutput, calls=%fused_computation.11 | convolution fusion | flops 821036032 | bytes 28323840 | tf_op jit(solution)/shard_map/reduce_sum | solution.py:671
  339.6 7.4 convert_reduce_fusion.4
  347.8 6.6 multiply_convert_fusion.1
  354.4 3.2 fusion.43
  357.6 3.2 convert_reduce_fusion.5
  361.6 3.1 fusion.120
  367.6 35.2 %reduce-scatter.13.cloned.1.call-done = f32[256,768]{1,0:T(8,128)} async-done(((f32[1024,768]{1,0:T(8,128)}), f32[256,768]{1,0:T(8,128)}) %reduce-scatter.13.cloned.1.call-update) | async-done | bytes 786448 | tf_op jit(solution)/shard_map/reduce_scatter | solution.py:704
  405.1 3.3 convert_reduce_fusion.6
  408.9 19.3 %all-gather.7.cloned.1.call-done = bf16[1024,768]{1,0:T(8,128)(2,1)} async-done(((bf16[256,768]{1,0:T(8,128)(2,1)}), bf16[1024,768]{1,0:T(8,128)(2,1)}) %all-gather.7.cloned.1.call-update) | async-done | bytes 1572880 | tf_op jit(solution)/shard_map/all_gather | solution.py:688
  428.2 6.1 convert_reduce_fusion.1
  435.5 3.1 fusion.177
  442.9 3.9 fusion.150
  458.1 6.5 copy.215
  465.9 10.8 %reduce-scatter.15.cloned.1.call-done = f32[256,768]{1,0:T(8,128)} async-done(((f32[1024,768]{1,0:T(8,128)}), f32[256,768]{1,0:T(8,128)}) %reduce-scatter.15.cloned.1.call-update) | async-done | bytes 786448 | tf_op jit(solution)/shard_map/reduce_scatter | solution.py:692
  478.2 3.8 fusion.61
  483.5 10.0 %all_to_all.48 = bf16[256,4,192]{0,2,1:T(8,128)(2,1)S(1)} all-to-all(bf16[256,4,192]{0,2,1:T(8,128)(2,1)S(1)} %bitcast.338), channel_id=1, replica_groups=mesh['fsdp'=8,'seq'=4] {'seq'}, dimensions={1} | all-to-all | bytes 786432 | tf_op jit(solution)/shard_map/all_to_all | solution.py:700
  494.0 7.4 fusion.63
  501.4 13.1 %multiply_reduce_fusion = (f32[3,1024]{1,0:T(4,128)S(1)}, f32[3,1024,1024]{1,2,0:T(8,128)}) fusion(f32[3,1024,1024]{1,2,0:T(8,128)} %fusion.63, bf16[2,9,1024,64]{3,2,1,0:T(8,128)(2,1)} %get-tuple-element.38), kind=kOutput, calls=%fused_computation.7 | convolution fusion | flops 821036032 | bytes 28323840 | tf_op jit(solution)/shard_map/reduce_sum | solution.py:671
  514.6 9.8 %multiply_convert_fusion = bf16[3,1024,1024]{1,2,0:T(8,128)(2,1)S(1)} fusion(f32[3,1024,1024]{1,2,0:T(8,128)} %get-tuple-element.192, f32[3,1024,1024]{1,2,0:T(8,128)} %fusion.63, f32[3,1024]{1,0:T(4,128)S(1)} %get-tuple-element.191), kind=kLoop, calls=%fused_computation.6 | loop fusion | flops 9437184 | bytes 31469568 | tf_op jit(solution)/shard_map/convert_element_type | solution.py:68
  524.4 3.3 fusion.45
  527.8 3.2 convert_reduce_fusion.9
  533.1 3.1 fusion.119
  537.5 3.0 multiply_convert_fusion.3
  547.7 6.5 copy.213
  555.9 17.7 %reduce-scatter.21.cloned.1.call-done = bf16[96,2880]{1,0:T(8,128)(2,1)} async-done(((bf16[768,2880]{1,0:T(8,128)(2,1)}), bf16[96,2880]{1,0:T(8,128)(2,1)}) %reduce-scatter.21.cloned.1.call-update) | async-done | bytes 552976
  575.6 40.9 %psum.22 = f32[2,8,768]{2,0,1:T(2,128)S(1)} all-reduce(f32[2,8,768]{2,0,1:T(2,128)S(1)} %pad_maximum_fusion.11), channel_id=1, replica_groups=mesh['fsdp'=8,'seq'=4] {'fsdp','seq'}, use_global_device_ids=true, to_apply=%region_50.51 | all-reduce | flops 12288 | bytes 98304 | tf_op jit(solution)/shard_map/psum | solution.py:731
  620.0 91.9 %reduce-scatter.19.cloned.1.call-done = bf16[96,2880]{1,0:T(8,128)(2,1)} async-done(((bf16[768,2880]{1,0:T(8,128)(2,1)}), bf16[96,2880]{1,0:T(8,128)(2,1)}) %reduce-scatter.19.cloned.1.call-update) | async-done | bytes 552976
  718.1 3.4 fusion.62
  721.7 11.8 %psum.21 = f32[1,2,4608]{2,1,0:T(2,128)S(1)} all-reduce(f32[1,2,4608]{2,1,0:T(2,128)S(1)} %maximum_bitcast_fusion), channel_id=1, replica_groups=mesh['fsdp'=8,'seq'=4] {'seq'}, use_global_device_ids=true, to_apply=%region_36.37 | all-reduce | flops 9216 | bytes 73728 | tf_op jit(solution)/shard_map/psum | solution.py:739
  733.5 30.9 %all_gather.21 = f32[8,2,4608]{2,1,0:T(2,128)S(1)} all-gather(f32[1,2,4608]{2,1,0:T(2,128)S(1)} %psum.21), channel_id=1, replica_groups=mesh['fsdp'=8,'seq'=4] {'fsdp'}, dimensions={0}, use_global_device_ids=true | all-gather | bytes 331776 | tf_op jit(solution)/shard_map/all_gather | solution.py:740
  767.0 4.3 all-to-all-start.2
  781.6 6.8 copy.192
  788.4 3.3 slice.241
  791.8 5.1 slice_bitcast_fusion
  796.9 3.4 copy.195
  800.2 3.1 copy.194
  803.3 5.3 reshape.334
  811.4 3.7 reshape.322
  (331 shorter events, 112.2 us)
Async XLA Ops:
  7.2 241.6 %all-gather.5.cloned.1.call-start = ((), (), s32[]{:S(2)}) async-start(), calls=%async_computation.9 | async-start | bytes 1966080 | tf_op jit(solution)/shard_map/all_gather | solution.py:688
  35.6 11.6 %copy-start.21 = (bf16[2,96,3072]{2,1,0:T(8,128)(2,1)S(1)}, bf16[2,96,3072]{2,1,0:T(8,128)(2,1)}, u32[]{:S(2)}) copy-start(bf16[2,96,3072]{2,1,0:T(8,128)(2,1)} %param.21) | copy-start | bytes 3538948
  38.2 262.7 %reduce-scatter.11.cloned.1.call-start = ((), (), s32[]{:S(2)}) async-start(), calls=%async_computation.10 | async-start | bytes 3932160 | tf_op jit(solution)/shard_map/reduce_scatter | solution.py:692
  240.5 3.4 copy-start.16
  240.5 5.9 copy-start.8
  248.7 6.3 copy-start.4
  248.7 7.4 copy-start.23
  259.3 2.1 copy-start.15
  260.8 42.3 %copy-start.32 = (f32[256]{0:T(256)}, f32[256]{0:T(256)S(1)}, u32[]{:S(2)}) copy-start(f32[256]{0:T(256)S(1)} %broadcast_multiply_fusion.11) | copy-start | bytes 3076
  261.0 42.0 %copy-start.44 = (f32[256]{0:T(256)}, f32[256]{0:T(256)S(1)}, u32[]{:S(2)}) copy-start(f32[256]{0:T(256)S(1)} %broadcast_multiply_fusion.5) | copy-start | bytes 3076
  261.1 42.0 %copy-start.47 = (f32[256]{0:T(256)}, f32[256]{0:T(256)S(1)}, u32[]{:S(2)}) copy-start(f32[256]{0:T(256)S(1)} %add_rsqrt_fusion.3) | copy-start | bytes 3076
  261.4 41.7 %copy-start.10 = (bf16[1,256,768]{2,1,0:T(8,128)(2,1)S(1)}, bf16[1,256,768]{2,1,0:T(8,128)(2,1)}, u32[]{:S(2)}) copy-start(bf16[1,256,768]{2,1,0:T(8,128)(2,1)} %param.25) | copy-start | bytes 1179652
  307.5 10.8 %all-to-all-start = ((bf16[256,4,192]{0,2,1:T(8,128)(2,1)}), bf16[256,4,192]{0,2,1:T(8,128)(2,1)S(1)}, u32[]{:S(2)}, u32[]{:S(2)}) async-start(bf16[256,4,192]{0,2,1:T(8,128)(2,1)} %bitcast.21), calls=%async_computation.1 | async-start | bytes 786432 | tf_op jit(solution)/shard_map/all_to_all | solution.py:700
  311.0 91.8 %reduce-scatter.13.cloned.1.call-start = ((), (), s32[]{:S(2)}) async-start(), calls=%async_computation.11 | async-start | bytes 3932160 | tf_op jit(solution)/shard_map/reduce_scatter | solution.py:704
  339.6 8.2 copy-start
  347.1 13.8 %copy-start.26 = (bf16[3,1024,64]{1,2,0:T(8,128)(2,1)}, bf16[3,1024,64]{1,2,0:T(8,128)(2,1)S(1)}, u32[]{:S(2)}) copy-start(bf16[3,1024,64]{1,2,0:T(8,128)(2,1)S(1)} %get-tuple-element.196) | copy-start | bytes 1179652
  357.6 3.3 copy-start.28
  357.6 4.0 copy-start.25
  364.8 63.4 %all-gather.7.cloned.1.call-start = ((), (), s32[]{:S(2)}) async-start(), calls=%async_computation.12 | async-start | bytes 1966080 | tf_op jit(solution)/shard_map/all_gather | solution.py:688
  408.4 68.2 %reduce-scatter.15.cloned.1.call-start = ((), (), s32[]{:S(2)}) async-start(), calls=%async_computation.13 | async-start | bytes 3932160 | tf_op jit(solution)/shard_map/reduce_scatter | solution.py:692
  428.2 7.3 copy-start.22
  438.6 135.1 %reduce-scatter.21.cloned.1.call-start = ((), (), s32[]{:S(2)}) async-start(), calls=%async_computation.18 | async-start | bytes 5087232
  442.9 3.9 copy-start.14
  446.8 2.7 copy-start.5
  464.6 13.6 %copy-start.11 = (bf16[1,256,768]{2,1,0:T(8,128)(2,1)S(1)}, bf16[1,256,768]{2,1,0:T(8,128)(2,1)}, u32[]{:S(2)}) copy-start(bf16[1,256,768]{2,1,0:T(8,128)(2,1)} %param.25) | copy-start | bytes 1179652
  464.6 153.8 %reduce-scatter.17.cloned.1.call-start = ((), (), s32[]{:S(2)}) async-start(), calls=%async_computation.14 | async-start | bytes 3932160 | tf_op jit(solution)/shard_map/reduce_scatter | solution.py:704
  478.2 4.6 copy-start.9
  524.4 6.5 copy-start.1
  530.9 2.1 copy-start.58
  530.9 2.1 copy-start.24
  536.2 175.6 %reduce-scatter.19.cloned.1.call-start = ((), (), s32[]{:S(2)}) async-start(), calls=%async_computation.17 | async-start | bytes 5087232
  537.5 3.0 copy-start.19
  537.5 3.0 copy-start.63
  554.3 20.9 %copy-start.42 = (f32[768]{0:T(1024)S(1)}, f32[768]{0:T(1024)}, u32[]{:S(2)}) copy-start(f32[768]{0:T(1024)} %get-tuple-element.177) | copy-start | bytes 9220
  554.3 64.2 %copy-start.43 = (f32[256]{0:T(256)S(1)}, f32[256]{0:T(256)}, u32[]{:S(2)}) copy-start(f32[256]{0:T(256)} %broadcast_multiply_fusion.2) | copy-start | bytes 3076
  554.3 225.3 %all-reduce.3.cloned.1.call-start = ((), (), s32[]{:S(2)}) async-start(), calls=%async_computation.15 | async-start | bytes 786432 | tf_op jit(solution)/shard_map/psum | solution.py:729
  715.3 66.3 %all-gather.9.cloned.1.call-start = ((), (), s32[]{:S(2)}) async-start(), calls=%async_computation.16 | async-start | bytes 4177920 | tf_op jit(solution)/shard_map/all_gather | solution.py:724
  718.0 3.5 copy-start.41
  718.0 3.6 copy-start.34
  718.0 3.6 copy-start.33
  718.0 3.6 copy-start.40
  718.1 46.8 %copy-start.7 = (bf16[2,96,4608]{2,1,0:T(8,128)(2,1)S(1)}, bf16[2,96,4608]{2,1,0:T(8,128)(2,1)}, u32[]{:S(2)}) copy-start(bf16[2,96,4608]{2,1,0:T(8,128)(2,1)} %ada_ref.1) | copy-start | bytes 5308420
  721.5 49.9 %copy-start.31 = (f32[8,128]{1,0:T(8,128)S(1)}, f32[8,128]{1,0:T(8,128)}, u32[]{:S(2)}) copy-start(f32[8,128]{1,0:T(8,128)} %get-tuple-element.43) | copy-start | bytes 12292
  767.0 10.7 %all-to-all-start.2 = ((f32[8,1,96]{2,1,0:T(1,128)}), f32[8,1,96]{2,1,0:T(1,128)S(1)}, u32[]{:S(2)}, u32[]{:S(2)}) async-start(f32[8,1,96]{2,1,0:T(1,128)} %bitcast.60), calls=%async_computation.6 | async-start | bytes 8192 | tf_op jit(solution)/shard_map/all_to_all | solution.py:749
  774.6 4.5 copy-start.45
  774.6 4.5 copy-start.46
  803.3 5.3 copy-start.6
  811.4 3.7 copy-start.30
  (28 other events, 37.8 us)
Sparse Core Ops, SparseCore 0:
  38.3 19.5 all-gather.4
  259.4 41.4 reduce-scatter.10
  364.9 37.9 reduce-scatter.12
  408.5 19.6 all-gather.6
  438.7 37.8 reduce-scatter.14
  480.1 93.5 reduce-scatter.20
  576.2 37.6 reduce-scatter.16
  617.6 94.2 reduce-scatter.18
  715.4 32.4 all-reduce.2
  749.9 29.6 all-gather.8

commit v3 on v2

--- a/solution.py
+++ b/solution.py
@@ -604,6 +604,438 @@
     )(x, mod, bq, bo, bu, bd, sq, so, su, sd)
 
 
+def backward_kernel(n, *refs):
+    (cot_ref, mod_ref), rest = refs[:2], refs[2:]
+    stored, rest = rest[:13], rest[13:]
+    (g_ref, dmod_ref, gob_ref, gdb_ref, gub_ref, gqb_ref), rest = rest[:6], rest[6:]
+    fin, rest = rest[:4], rest[4:]
+    loaded, rest = rest[:13], rest[13:]
+    grads, rest = rest[:4], rest[4:]
+    y_in, rest = rest[:4], rest[4:]
+    z_out, rest = rest[:4], rest[4:]
+    z_in, rest = rest[:4], rest[4:]
+    kept, rest = rest[:4], rest[4:]
+    (gf_ref, act_ref, gup_ref, gosend, go_ref, goh_ref, gqh_ref, gqkv_ref, psend, precv, xsend, xrecv,
+     own_part, gmid_ref, dk_acc, dv_acc,
+     l_s, y_s, y_r, z_s, z_r, f_s, f_r, g_s, g_r, t_s, t_r, r_s, r_r) = rest
+    wq, wo, wu, wd, xs, attn, qh, tok, branch, mid, mlp, up, feed = range(13)
+    down, upw, outw, qkvw = range(4)
+    f = lax.axis_index("fsdp")
+    s = lax.axis_index("seq")
+    slow = n // FAST
+    a, b = f // FAST, f % FAST
+    layers = mod_ref.shape[0]
+    block, width = cot_ref.shape
+    rows = width // n
+    hc = gosend.shape[2]
+    heads = hc // HEAD_DIM
+    across, diagonal, partner = relative(s, 0), relative(s, 1), relative(s, 2)
+    y_dev = {"fsdp": a * FAST + (1 - b)}
+
+    def load(i, l):
+        return pltpu.make_async_copy(stored[i].at[l], loaded[i], l_s.at[i])
+
+    for i in (feed, wd, up, wu, mlp, mid, branch, wo, tok, qh, wq, attn, xs):
+        load(i, layers - 1).start()
+
+    entry_barrier(
+        [{"fsdp": ((a + k) % slow) * FAST + b} for k in range(1, slow)] + [y_dev]
+        + [{"seq": across}, {"seq": diagonal}, {"seq": partner}]
+    )
+
+    def y_copy(l, p):
+        return rcopy(grads[p].at[:, 1 - b], y_in[p].at[l], y_s.at[p], y_r.at[l, p], y_dev)
+
+    def z_copy(l, p, k):
+        to = (a + k) % slow
+        return rcopy(z_out[p].at[to], z_in[p].at[l, k - 1], z_s.at[p, k], z_r.at[l, p, k], {"fsdp": to * FAST + b})
+
+    def z_start(l, p):
+        y_copy(l, p).wait_recv()
+        for i in range(slow):
+            z_out[p][i] = (grads[p][i, b].astype(F32) + y_in[p][l, i].astype(F32)).astype(BF16)
+        kept[p][...] = grads[p][a, b].astype(F32) + y_in[p][l, a].astype(F32)
+        for k in range(1, slow):
+            z_copy(l, p, k).start()
+        y_copy(l, p).wait_send()
+
+    def fin_copy(l, p, i):
+        mine, theirs = fin[p].at[l, s], fin[p].at[l, across]
+        ref = theirs if i == 2 else mine
+        return rcopy(ref, ref, f_s.at[l, p, i], f_r.at[l, p, i], {"seq": across if i == 1 else partner})
+
+    def z_finish(l, p):
+        total = kept[p][...]
+        for k in range(1, slow):
+            z_copy(l, p, k).wait_recv()
+            total = total + z_in[p][l, k - 1].astype(F32)
+        fin[p][l, s] = total.astype(BF16)
+        fin_copy(l, p, 1).start()
+        fin_copy(l, p, 0).start()
+        for k in range(1, slow):
+            z_copy(l, p, k).wait_send()
+
+    def fin_arrived(l, p, i):
+        ref = fin[p].at[l, (partner, across, diagonal)[i]]
+        rcopy(ref, ref, f_s.at[l, p, i], f_r.at[l, p, i], {"seq": partner}).wait_recv()
+
+    def matrix(i):
+        return loaded[i][...].reshape(width, loaded[i].shape[2])
+
+    def part_copy(i):
+        return rcopy(psend.at[i], precv.at[i], r_s.at[i], r_r.at[i], {"seq": partner})
+
+    over = rcopy(xsend, xrecv, r_s.at[2], r_r.at[2], {"seq": across})
+
+    def place(j, part):
+        @pl.when(j == 3)
+        def _():
+            own_part[...] = part
+
+        @pl.when(j == 2)
+        def _():
+            psend[0] = part
+            part_copy(0).start()
+
+        @pl.when(j == 0)
+        def _():
+            xsend[...] = part
+
+        @pl.when(j == 1)
+        def _():
+            psend[1] = part
+            part_copy(1).start()
+
+    def send_across():
+        part_copy(1).wait_recv()
+        xsend[...] = xsend[...] + precv[1]
+        over.start()
+
+    def collect():
+        part_copy(0).wait_recv()
+        own_part[...] = own_part[...] + precv[0]
+        over.wait_recv()
+        own_part[...] = own_part[...] + xrecv[...]
+        over.wait_send()
+        part_copy(0).wait_send()
+        part_copy(1).wait_send()
+
+    def sums(value):
+        return jnp.sum(value, axis=0, keepdims=True)
+
+    def layer(step, carry):
+        l = layers - 1 - step
+        row = lambda i: mod_ref[l, i: i + 1, :]
+
+        @pl.when(step == 0)
+        def _():
+            g_ref[...] = cot_ref[...].astype(F32)
+
+        load(feed, l).wait()
+        g = g_ref[...]
+        g_feed = (row(5) * g).astype(BF16)
+        gf_ref[s] = g_feed
+        mine, theirs = gf_ref.at[s], gf_ref.at[across]
+        to_partner = rcopy(mine, mine, g_s.at[0], g_r.at[0], {"seq": partner})
+        to_across = rcopy(mine, mine, g_s.at[1], g_r.at[1], {"seq": across})
+        relay = rcopy(theirs, theirs, g_s.at[2], g_r.at[2], {"seq": partner})
+        to_across.start()
+        to_partner.start()
+        dmod_ref[l, 5:6, :] = sums(g * loaded[feed][...])
+        gdb_ref[l] = sums(g_feed.astype(F32))
+        gub_ref[l] = jnp.zeros((1, gub_ref.shape[2]), F32)
+        for i in (wd, up, wu, mlp):
+            load(i, l).wait()
+
+        def mlp_block(i, carry):
+            @pl.when(i == 1)
+            def _():
+                ref = gf_ref.at[partner]
+                rcopy(ref, ref, g_s.at[0], g_r.at[0], {"seq": partner}).wait_recv()
+
+            @pl.when(i == 2)
+            def _():
+                rcopy(theirs, theirs, g_s.at[1], g_r.at[1], {"seq": across}).wait_recv()
+                relay.start()
+
+            @pl.when(i == 3)
+            def _():
+                ref = gf_ref.at[diagonal]
+                rcopy(ref, ref, g_s.at[2], g_r.at[2], {"seq": partner}).wait_recv()
+
+            j = (3 - i) * (1 - i // 2) + (i - 2) * (i // 2)
+            t = relative(s, j)
+            value, slope = gelu_parts(loaded[up][t])
+            act_ref[t] = value.astype(BF16)
+            g_up = (mm_nt(gf_ref[t], matrix(wd)) * slope).astype(BF16)
+            gup_ref[t] = g_up
+            gub_ref[l] = gub_ref[l] + sums(g_up.astype(F32))
+            place(j, mm_nt(g_up, matrix(wu)))
+            return carry
+
+        lax.fori_loop(0, 4, mlp_block, 0)
+        for copy in (to_partner, to_across, relay):
+            copy.wait_send()
+        send_across()
+
+        @pl.when(step > 0)
+        def _():
+            z_start(l + 1, qkvw)
+            z_finish(l + 1, outw)
+
+        whole = lambda ref: ref[...].reshape(4 * block, ref.shape[2])
+        grads[down][...] = mm_tn(whole(act_ref), whole(gf_ref)).astype(BF16).reshape(grads[down].shape)
+        y_copy(l, down).start()
+        grads[upw][...] = mm_tn(whole(loaded[mlp]), whole(gup_ref)).astype(BF16).reshape(grads[upw].shape)
+        y_copy(l, upw).start()
+
+        @pl.when(l > 0)
+        def _():
+            for i in (feed, wd, up, wu, mlp):
+                load(i, l - 1).start()
+
+        load(mid, l).wait()
+        normed, inverse = normalize(loaded[mid][...])
+        for i in (branch, wo, tok):
+            load(i, l).wait()
+        collect()
+        g_min = own_part[...]
+        dmod_ref[l, 4:5, :] = sums(g_min * normed)
+        dmod_ref[l, 3:4, :] = sums(g_min)
+        g_mid = g_ref[...] + norm_back(g_min * (1.0 + row(4)), normed, inverse)
+        gmid_ref[...] = g_mid
+        g_branch = (row(2) * g_mid).astype(BF16)
+        dmod_ref[l, 2:3, :] = sums(g_mid * loaded[branch][...])
+        gob_ref[l] = sums(g_branch.astype(F32))
+        g_o = mm_nt(g_branch, matrix(wo)).astype(BF16)
+        for t in range(4):
+            gosend[t] = g_o[:, t * hc: (t + 1) * hc]
+
+        def head_copy(j):
+            t = relative(s, j)
+            return rcopy(gosend.at[t], go_ref.at[s], t_s.at[j], t_r.at[j], {"seq": t})
+
+        for j in range(3):
+            head_copy(j).start()
+        go_ref[s] = gosend[s]
+        tokens_out = jnp.concatenate([loaded[tok][t] for t in range(4)], axis=1)
+        grads[outw][...] = mm_tn(tokens_out, g_branch).astype(BF16).reshape(grads[outw].shape)
+        y_copy(l, outw).start()
+
+        @pl.when(l > 0)
+        def _():
+            for i in (mid, branch, wo, tok):
+                load(i, l - 1).start()
+
+        @pl.when(step > 0)
+        def _():
+            z_finish(l + 1, qkvw)
+
+        load(qh, l).wait()
+        for j in range(3):
+            t = relative(s, j)
+            rcopy(gosend.at[t], go_ref.at[t], t_s.at[j], t_r.at[j], {"seq": t}).wait_recv()
+        for t in range(4):
+            part = go_ref[t]
+            for h in range(heads):
+                goh_ref[h, t * block: (t + 1) * block, :] = part[:, h * HEAD_DIM: (h + 1) * HEAD_DIM]
+
+        for h in range(heads):
+            dk_acc[...] = jnp.zeros_like(dk_acc)
+            dv_acc[...] = jnp.zeros_like(dv_acc)
+
+            def tile(t, carry):
+                at = pl.ds(pl.multiple_of(t * block, block), block)
+                q = loaded[qh][h, at, :]
+                k = loaded[qh][heads + h]
+                g_out = goh_ref[h, at, :]
+                e = jnp.exp(mm_nt(q, k) * SCORE_SCALE)
+                prob = e * (1.0 / jnp.sum(e, axis=-1, keepdims=True))
+                dv_acc[...] = dv_acc[...] + mm_tn(prob.astype(BF16), g_out)
+                dp = mm_nt(g_out, loaded[qh][2 * heads + h])
+                inner = jnp.sum(prob * dp, axis=-1, keepdims=True)
+                ds = (prob * (dp - inner)).astype(BF16)
+                gqh_ref[h, at, :] = (mm(ds, k) * SCORE_SCALE).astype(BF16)
+                dk_acc[...] = dk_acc[...] + mm_tn(ds, q)
+                return carry
+
+            lax.fori_loop(0, 4, tile, 0)
+            gqh_ref[heads + h] = (dk_acc[...] * SCORE_SCALE).astype(BF16)
+            gqh_ref[2 * heads + h] = dv_acc[...].astype(BF16)
+            if h < 2:
+                z_start(l, h)
+
+        for j in range(3):
+            head_copy(j).wait_send()
+
+        @pl.when(l > 0)
+        def _():
+            load(qh, l - 1).start()
+
+        for t in range(4):
+            gqkv_ref[t] = jnp.concatenate(
+                [gqh_ref[i, t * block: (t + 1) * block, :] for i in range(3 * heads)], axis=1
+            )
+        load(wq, l).wait()
+
+        def back_block(i, carry):
+            j = (1 - i) * (1 - i // 2) + i * (i // 2)
+            place(j, mm_nt(gqkv_ref[relative(s, j)], matrix(wq)))
+            return carry
+
+        lax.fori_loop(0, 4, back_block, 0)
+        send_across()
+        load(attn, l).wait()
+        grads[qkvw][...] = mm_tn(whole(loaded[attn]), whole(gqkv_ref)).astype(BF16).reshape(grads[qkvw].shape)
+        y_copy(l, qkvw).start()
+        gqb_ref[l] = sums(whole(gqkv_ref).astype(F32))
+        z_start(l, outw)
+        z_finish(l, down)
+        z_finish(l, upw)
+        load(xs, l).wait()
+        normed, inverse = normalize(loaded[xs][...])
+
+        @pl.when(l > 0)
+        def _():
+            for i in (wq, attn, xs):
+                load(i, l - 1).start()
+
+        collect()
+        g_ain = own_part[...]
+        dmod_ref[l, 1:2, :] = sums(g_ain * normed)
+        dmod_ref[l, 0:1, :] = sums(g_ain)
+        g_ref[...] = gmid_ref[...] + norm_back(g_ain * (1.0 + row(1)), normed, inverse)
+        return carry
+
+    lax.fori_loop(0, layers, layer, 0)
+    z_start(0, qkvw)
+    z_finish(0, outw)
+    z_finish(0, qkvw)
+    for l in reversed(range(layers)):
+        for p in (down, upw, outw, qkvw):
+            fin_arrived(l, p, 1)
+            fin_copy(l, p, 2).start()
+    for l in range(layers):
+        for p in range(4):
+            fin_arrived(l, p, 0)
+            fin_arrived(l, p, 2)
+            for i in range(3):
+                fin_copy(l, p, i).wait_send()
+
+
+def backward(n, cot, mod, stored):
+    layers = mod.shape[0]
+    block, width = cot.shape
+    rows = width // n
+    slow = n // FAST
+    qc = stored[0].shape[3]
+    uc = stored[2].shape[3]
+    hc = qc // 3
+    nh = qc // HEAD_DIM
+    sds = jax.ShapeDtypeStruct
+    dma = pltpu.SemaphoreType.DMA
+    columns = (width, uc, width, qc)
+    outs = [
+        sds((block, width), F32),
+        sds((layers, 6, width), F32),
+        sds((layers, 1, width), F32),
+        sds((layers, 1, width), F32),
+        sds((layers, 1, uc), F32),
+        sds((layers, 1, qc), F32),
+    ] + [sds((layers, 4, rows, c), BF16) for c in columns]
+    scratch = (
+        [pltpu.VMEM(x.shape[1:], x.dtype) for x in stored]
+        + [pltpu.VMEM((slow, FAST, rows, c), BF16) for c in columns]
+        + [pltpu.VMEM((layers, slow, rows, c), BF16) for c in columns]
+        + [pltpu.VMEM((slow, rows, c), BF16) for c in columns]
+        + [pltpu.VMEM((layers, slow - 1, rows, c), BF16) for c in columns]
+        + [pltpu.VMEM((rows, c), F32) for c in columns]
+        + [
+            pltpu.VMEM((4, block, width), BF16),
+            pltpu.VMEM((4, block, uc), BF16),
+            pltpu.VMEM((4, block, uc), BF16),
+            pltpu.VMEM((4, block, hc), BF16),
+            pltpu.VMEM((4, block, hc), BF16),
+            pltpu.VMEM((nh // 3, 4 * block, HEAD_DIM), BF16),
+            pltpu.VMEM((nh, 4 * block, HEAD_DIM), BF16),
+            pltpu.VMEM((4, block, qc), BF16),
+            pltpu.VMEM((2, block, width), F32),
+            pltpu.VMEM((2, block, width), F32),
+            pltpu.VMEM((block, width), F32),
+            pltpu.VMEM((block, width), F32),
+            pltpu.VMEM((block, width), F32),
+            pltpu.VMEM((block, width), F32),
+            pltpu.VMEM((4 * block, HEAD_DIM), F32),
+            pltpu.VMEM((4 * block, HEAD_DIM), F32),
+            dma((13,)),
+            dma((4,)), dma((layers, 4)),
+            dma((4, slow)), dma((layers, 4, slow)),
+            dma((layers, 4, 3)), dma((layers, 4, 3)),
+        ]
+        + [dma((3,))] * 6
+    )
+    return pl.pallas_call(
+        functools.partial(backward_kernel, n),
+        out_shape=tuple(outs),
+        in_specs=vmem_specs(2) + [pl.BlockSpec(memory_space=pl.ANY)] * 13,
+        out_specs=tuple(vmem_specs(len(outs))),
+        scratch_shapes=scratch,
+        compiler_params=pltpu.CompilerParams(
+            collective_id=2, has_side_effects=True, vmem_limit_bytes=VMEM_LIMIT
+        ),
+    )(cot, mod, *stored)
+
+
+def tail_kernel(n, sum_ref, cat_ref, sums_all, cats_all, s_in, c_all, s_tot,
+                a_s, a_r, b_s, b_r, c_s, c_r, d_s, d_r):
+    f = lax.axis_index("fsdp")
+    s = lax.axis_index("seq")
+    entry_barrier([{"seq": relative(s, j)} for j in range(3)] + [{"fsdp": (f + k) % n} for k in range(1, n)])
+    sends = []
+    for j in range(3):
+        t = relative(s, j)
+        sends.append(rcopy(sum_ref, s_in.at[s], a_s.at[j], a_r.at[j], {"seq": t}))
+        sends[-1].start()
+        sends.append(rcopy(cat_ref, c_all.at[s], b_s.at[j], b_r.at[j], {"seq": t}))
+        sends[-1].start()
+    s_in[s] = sum_ref[...]
+    c_all[s] = cat_ref[...]
+    for j in range(3):
+        t = relative(s, j)
+        rcopy(sum_ref, s_in.at[t], a_s.at[j], a_r.at[j], {"seq": t}).wait_recv()
+        rcopy(cat_ref, c_all.at[t], b_s.at[j], b_r.at[j], {"seq": t}).wait_recv()
+    s_tot[...] = jnp.sum(s_in[...], axis=0)
+    sums_all[f] = s_tot[...]
+    cats_all[f] = c_all[...]
+    for k in range(1, n):
+        to = {"fsdp": (f + k) % n}
+        sends.append(rcopy(s_tot, sums_all.at[f], c_s.at[k], c_r.at[k], to))
+        sends[-1].start()
+        sends.append(rcopy(c_all, cats_all.at[f], d_s.at[k], d_r.at[k], to))
+        sends[-1].start()
+    for k in range(1, n):
+        at = (f - k + n) % n
+        rcopy(s_tot, sums_all.at[at], c_s.at[k], c_r.at[k], {"fsdp": at}).wait_recv()
+        rcopy(c_all, cats_all.at[at], d_s.at[k], d_r.at[k], {"fsdp": at}).wait_recv()
+    for copy in sends:
+        copy.wait_send()
+
+
+def tail(n, sums, cats):
+    sds = jax.ShapeDtypeStruct
+    dma = pltpu.SemaphoreType.DMA
+    return pl.pallas_call(
+        functools.partial(tail_kernel, n),
+        out_shape=(sds((n,) + sums.shape, F32), sds((n, 4) + cats.shape, F32)),
+        in_specs=vmem_specs(2),
+        out_specs=tuple(vmem_specs(2)),
+        scratch_shapes=[
+            pltpu.VMEM((4,) + sums.shape, F32), pltpu.VMEM((4,) + cats.shape, F32), pltpu.VMEM(sums.shape, F32),
+        ] + [dma((3,))] * 4 + [dma((n,))] * 4,
+        compiler_params=pltpu.CompilerParams(collective_id=3, has_side_effects=True),
+    )(sums, cats)
+
+
 def fused_device(
     tokens, condition, ada_weight, ada_bias, qkv_weight, qv_bias, out_weight, out_bias,
     up_weight, up_bias, down_weight, down_bias, cotangent,
@@ -661,86 +1093,31 @@
     (block_out, w_q, w_o, w_u, w_d, xs, attn, qh, tok, branches, mids, mlp, ups, feeds) = forward(
         n, tokens[0], mod.reshape(layers, 6, width), qkv_b[:, None], out_b[:, None], up_bs[:, None],
         down_b[:, None], s_q, out_weight, s_u, s_d)
-    saved, w_qkv, w_rest = [], [], []
-    nh = hc // HEAD_DIM
-    for l in range(layers):
-        n_a, r_a = normalize(xs[l])
-        n_m, r_m = normalize(mids[l])
-        q, k, v = [join_heads(qh[l, i * nh: (i + 1) * nh]) for i in range(3)]
-        scores = jnp.einsum("hqd,hkd->hqk", split_heads(q), split_heads(k), preferred_element_type=F32) * SCORE_SCALE
-        logsum = jnp.log(jnp.sum(jnp.exp(scores), axis=-1, keepdims=True))
-        up = ups[l].reshape(-1, fw)
-        saved.append((n_a, r_a, attn[l].reshape(-1, width), q, k, v, logsum,
-                      tok[l].transpose(1, 0, 2).reshape(-1, width), branches[l], n_m, r_m,
-                      mlp[l].reshape(-1, width), up, gelu_parts(up)[0].astype(BF16), feeds[l]))
-        w_qkv.append(w_q[l].reshape(width, -1))
-        w_rest.append(jnp.concatenate([w.reshape(width, -1) for w in (w_u[l], w_d[l], w_o[l])], axis=1))
-
-    g = cotangent[0].astype(F32)
-    d_mods = [None] * layers
-    reduced = [None] * layers
-    bias_grads = [None] * layers
-    for l in reversed(range(layers)):
-        shift_a, scale_a, gate_a, shift_m, scale_m, gate_m = jnp.split(mod[l], 6)
-        n_a, r_a, attn_all, q, k, v, logsum, tok_out, branch, n_m, r_m, mlp_all, up, act, feed = saved[l]
-        g_feed = (gate_m * g).astype(BF16)
-        d_gate_m = jnp.sum(g * feed, axis=0)
-        g_feed_all = lax.all_gather(g_feed, "seq", axis=0, tiled=True)
-        grad_down = mm_tn(act, g_feed_all)
-        g_up = (mm_nt(g_feed_all, w_rest[l][:, fw: fw + width]) * gelu_parts(up)[1]).astype(BF16)
-        grad_up = mm_tn(mlp_all, g_up)
-        g_min = lax.psum_scatter(mm_nt(g_up, w_rest[l][:, :fw]), "seq", scatter_dimension=0, tiled=True)
-        d_scale_m = jnp.sum(g_min * n_m, axis=0)
-        d_shift_m = jnp.sum(g_min, axis=0)
-        g_mid = g + norm_back(g_min * (1.0 + scale_m), n_m, r_m)
-        g_branch = (gate_a * g_mid).astype(BF16)
-        d_gate_a = jnp.sum(g_mid * branch, axis=0)
-        grad_out = mm_tn(tok_out, g_branch)
-        g_o = mm_nt(g_branch, w_rest[l][:, fw + width:]).astype(BF16)
-        g_o_heads = lax.all_to_all(g_o, "seq", split_axis=1, concat_axis=0, tiled=True)
-        dq, dk, dv = attend_back(q, k, v, logsum, g_o_heads)
-        g_qkv = jnp.concatenate([dq, dk, dv], axis=1)
-        grad_qkv = mm_tn(attn_all, g_qkv)
-        g_ain = lax.psum_scatter(mm_nt(g_qkv, w_qkv[l]), "seq", scatter_dimension=0, tiled=True)
-        d_scale_a = jnp.sum(g_ain * n_a, axis=0)
-        d_shift_a = jnp.sum(g_ain, axis=0)
-        g = g_mid + norm_back(g_ain * (1.0 + scale_a), n_a, r_a)
-        d_mods[l] = jnp.concatenate([d_shift_a, d_scale_a, d_gate_a, d_shift_m, d_scale_m, d_gate_m])
-        packed = jnp.concatenate([grad_up, grad_down, grad_out, grad_qkv], axis=1).astype(BF16)
-        reduced[l] = lax.psum_scatter(packed, "fsdp", scatter_dimension=0, tiled=True)
-
-        def place(x, axis):
-            zeros = jnp.zeros(x.shape[:axis] + (ns,) + x.shape[axis + 1:], F32)
-            return lax.dynamic_update_slice_in_dim(zeros, x, s, axis)
-
-        qv_g = place(jnp.stack([jnp.sum(dq.astype(F32), axis=0), jnp.sum(dv.astype(F32), axis=0)])[:, None, :], 1)
-        up_g = place(jnp.sum(g_up.astype(F32), axis=0).reshape(n, 1, fc), 1)
-        bias_grads[l] = jnp.concatenate([
-            qv_g.reshape(n, -1), jnp.sum(g_branch.astype(F32), axis=0).reshape(n, -1),
-            up_g.reshape(n, -1), jnp.sum(g_feed.astype(F32), axis=0).reshape(n, -1)], axis=1)
-
-    red = jnp.stack(reduced)
-    shared = jnp.concatenate([red[:, :, : fw + width], red[:, :, fw + 2 * width:]], axis=2)
-    shared = lax.all_gather(shared, "seq", axis=0, tiled=False).astype(F32)
-    grad_up = shared[..., :fw].reshape(ns, layers, rows, n, fc).transpose(1, 2, 3, 0, 4).reshape(layers, rows, ff)
-    grad_down = shared[..., fw: fw + width].transpose(1, 0, 2, 3).reshape(layers, ns * fc, width)
-    grad_qkv = shared[..., fw + width:].reshape(ns, layers, rows, 3, hc).transpose(1, 2, 3, 0, 4)
-    grad_qkv = grad_qkv.reshape(layers, rows, 3 * width)
-    grad_out = lax.psum(red[:, :, fw + width: fw + 2 * width], "seq").astype(F32)
-
-    bias = lax.psum(jnp.stack(bias_grads), ("fsdp", "seq"))
-    bias = lax.dynamic_index_in_dim(bias, f, 1, keepdims=False)
-    cuts = [qv_bias.shape[1], out_bias.shape[1], up_bias.shape[1], down_bias.shape[1]]
-    grad_bias, at = [], 0
-    for size in cuts:
-        grad_bias.append(bias[:, at: at + size])
-        at += size
-
-    d_mod = lax.psum(jnp.stack(d_mods), "seq")
-    d_mod_all = lax.all_gather(d_mod, "fsdp", axis=0, tiled=False)
-    cond_rows32 = cond_rows.astype(F32)
+    (g, d_mod, g_ob, g_db, g_ub, g_qb, grad_down, grad_up, grad_out, grad_qkv) = backward(
+        n, cotangent[0], mod.reshape(layers, 6, width),
+        (w_q, w_o, w_u, w_d, xs, attn, qh, tok, branches, mids, mlp, ups, feeds))
+    grad_up = grad_up.reshape(layers, ns, rows, n, fc).transpose(0, 2, 3, 1, 4).reshape(layers, rows, ff).astype(F32)
+    grad_down = grad_down.reshape(layers, ns * fc, width).astype(F32)
+    grad_qkv = grad_qkv.reshape(layers, ns, rows, 3, hc).transpose(0, 2, 3, 1, 4)
+    grad_qkv = grad_qkv.reshape(layers, rows, 3 * width).astype(F32)
+    grad_out = jnp.sum(grad_out.astype(F32), axis=1)
+
+    sums = jnp.concatenate([d_mod.reshape(-1), g_ob.reshape(-1), g_db.reshape(-1)])
+    g_qvb = jnp.concatenate([g_qb[:, 0, :hc], g_qb[:, 0, 2 * hc:]], axis=1)
+    cats = jnp.concatenate([g_ub.reshape(-1), g_qvb.reshape(-1)])
+    sums_all, cats_all = tail(n, sums.reshape(8, -1), cats.reshape(8, -1))
+    sums_all = sums_all.reshape(n, -1)
+    d_mod_all = sums_all[:, : layers * width6].reshape(n, layers, width6)
+    g_bias = jnp.sum(sums_all[:, layers * width6:], axis=0).reshape(2, layers, n, rows)
+    g_bias = lax.dynamic_index_in_dim(g_bias, f, 2, keepdims=False)
+    cats_all = jnp.sum(cats_all.reshape(n, ns, -1), axis=0)
+    g_ub = cats_all[:, : layers * fw].reshape(ns, layers, n, fc)
+    g_ub = lax.dynamic_index_in_dim(g_ub, f, 2, keepdims=False).transpose(1, 0, 2).reshape(layers, ns * fc)
+    g_qvb = cats_all[:, layers * fw:].reshape(ns, layers, 2, hc).transpose(1, 2, 0, 3).reshape(layers, -1)
+    g_qvb = own(g_qvb, 1, qv_bias.shape[1])
+
     grad_ada = jnp.stack([
-        lax.dot_general(cond_rows32, d_mod_all[:, l], (((0,), (0,)), ((), ())), precision=HIGHEST,
+        lax.dot_general(cond_rows, d_mod_all[:, l], (((0,), (0,)), ((), ())), precision=HIGHEST,
                         preferred_element_type=F32) for l in range(layers)])
     grad_ada_bias = own(jnp.sum(d_mod_all, axis=0), 1, width6 // n)
     g_cond = sum(
@@ -750,8 +1127,8 @@
     _, silu_back = jax.vjp(jax.nn.silu, cond_float)
     grad_condition = silu_back(g_cond)[0]
     return (
-        block_out[None], g[None], grad_condition, grad_ada, grad_ada_bias, grad_qkv, grad_bias[0],
-        grad_out, grad_bias[1], grad_up, grad_bias[2], grad_down, grad_bias[3],
+        block_out[None], g[None], grad_condition, grad_ada, grad_ada_bias, grad_qkv, g_qvb,
+        grad_out, g_bias[0], grad_up, g_ub, grad_down, g_bias[1],
     )
 
 

time: 834 us -> 535 us (0.64)
  Pallas kernels: 206 us -> 432 us
  waiting for transfers between devices: 218 us -> 0.01 us
  matrix products: 104 us -> 6.24 us
  blocking collectives: 93.6 us -> 0 us
  local copies, waits for them, and re-layouts: 115 us -> 63.4 us
  other arithmetic: 61.7 us -> 18 us
  between operations: 15.7 us -> 1.13 us
    pallas_call x0 -> x2, Pallas kernels: none -> 226 us  [the longest x1 201 us: backward(): pl.pallas_call(functools.partial(backward_kernel, n), out_shape=tuple(out...]
    unnamed x12 -> x0, waiting for transfers between devices: 110 us -> none
    reduce_scatter x4 -> x0, waiting for transfers between devices: 84.2 us -> none  [the longest x2 49 us: fused_device(): lax.psum_scatter(mm_nt(g_up, w_rest[l][:, :fw]), 'seq', scatter_dimension...]
    dot_general x26 -> x2, matrix products: 75.5 us -> 4.05 us  [fused_device(): lax.dot_general(cond_rows, d_mod_all[:, l], (((0,), (0,)), ((), ())), pre...]
    psum x2 -> x0, blocking collectives: 52.7 us -> none  [the longest x1 40.9 us: fused_device(): bias = lax.psum(jnp.stack(bias_grads), ('fsdp', 'seq'))]
    all_gather x1 -> x0, blocking collectives: 30.9 us -> none  [fused_device(): d_mod_all = lax.all_gather(d_mod, 'fsdp', axis=0, tiled=False)]
    unnamed x147 -> x29, local copies, waits for them, and re-layouts: 31.5 us -> 4.28 us
    reduce_sum x2 -> x0, matrix products: 26.3 us -> none  [fused_device(): logsum = jnp.log(jnp.sum(jnp.exp(scores), axis=-1, keepdims=True))]
  transfers between devices with their start and end apart: 12 -> 1, of which waited for: 8 -> 0; matrix products, arithmetic and copies ran while one was open for 17% -> 9% of each run, Pallas kernels for 23% -> 0%
where the time goes in v3:
time: 535 us; the launch traced here: 530 us
  Pallas kernels  432 us (81%)
  local copies, waits for them, and re-layouts  63.4 us (12%)
  other arithmetic  18 us (3%)
  starting transfers between devices  9.81 us (2%)
  matrix products  6.24 us (1%)
    pallas_call x1, Pallas kernels, backward(): pl.pallas_call(functools.partial(backward_kernel, n), out_shape=tuple(out...  201 us
    pallas_call x1, Pallas kernels, forward(): pl.pallas_call(functools.partial(forward_kernel, n), out_shape=outs, in_s...  186 us
    pallas_call x1, Pallas kernels, tail(): pl.pallas_call(functools.partial(tail_kernel, n), out_shape=(sds((n,) + s...  25.1 us
    pallas_call x1, Pallas kernels, prep(): pl.pallas_call(functools.partial(prep_kernel, n), out_shape=(jax.ShapeDty...  19.3 us
    convert_element_type x3, local copies, waits for them, and re-layouts, fused_device(): grad_up.reshape(layers, ns, rows, n, fc).transpose(0, 2, 3, 1, 4)  12 us
  transfers between devices with their start and end apart: 1, of which 0 were waited for; matrix products, arithmetic and copies ran while one was open for 9% of the time, Pallas kernels for 0%

profile of v3, /device:TPU:0, one launch (start us, length us, event | category | flops | bytes accessed | tf_op | source)
XLA Modules:
  0.0 530.3 jit_solution(4851203490128206379)
XLA Ops:
  0.7 1.4 convert_reduce_fusion.1
  2.7 0.8 reshape.172
  3.5 0.8 reshape.173
  7.2 19.3 %shard_map.228 = (f32[8,128]{1,0:T(8,128)}, f32[8,8,336]{2,1,0:T(8,128)}, f32[2,4608]{1,0:T(2,128)}) custom-call(f32[8,8,128]{2,1,0:T(8,128)} %pad_convert_fusion.cond_ref, f32[8,336]{1,0:T(8,128)} %reshape.207.small_ref, bf16[2,96,4608]{2,1,0:T(8,128)(2,1)} %ada_ref.1), custom_call_target="tpu_custom_call" | custom-call | tf_op jit(solution)/shard_map/pallas_call | solution.py:320
  26.5 1.0 reshape.177
  27.9 0.8 add.40
  32.7 1.1 reshape.188
  35.1 0.9 copy.81.refs_6_
  36.0 1.6 reshape.190
  37.5 2.5 dynamic-slice_reduce_fusion
  40.0 1.0 reshape.191.refs_8_
  41.1 1.7 dynamic-slice_bitcast_fusion.refs_9_
  42.8 186.3 %shard_map.229 = (bf16[256,768]{1,0:T(8,128)(2,1)}, bf16[2,8,96,576]{3,2,1,0:T(8,128)(2,1)}, bf16[2,8,96,768]{3,2,1,0:T(8,128)(2,1)}, bf16[2,8,96,768]{3,2,1,0:T...) custom-call(bf16[256,768]{1,0:T(8,128)(2,1)} %bitcast.84, ...), custom_call_target="tpu_custom_call" | custom-call | tf_op jit(solution)/shard_map/pallas_call | solution.py:595
  229.0 201.1 %shard_map.230 = (f32[256,768]{1,0:T(8,128)}, f32[2,6,768]{2,1,0:T(8,128)}, f32[2,1,768]{2,1,0:T(1,128)}, f32[2,1,768]{2,1,0:T(1,128)}, f32[2,1,768]{2,1,0:T(1,1...) custom-call(bf16[256,768]{1,0:T(8,128)(2,1)} %bitcast.81, ...), custom_call_target="tpu_custom_call" | custom-call | tf_op jit(solution)/shard_map/pallas_call | solution.py:977
  430.2 0.8 slice.72
  433.1 0.8 reshape.193
  436.1 25.1 %shard_map.231 = (f32[8,8,1536]{2,1,0:T(8,128)}, f32[8,4,8,288]{3,2,1,0:T(8,128)}) custom-call(f32[8,1536]{1,0:T(8,128)} %reshape.196.sum_ref, f32[8,288]{1,0:T(8,128)} %reshape.199.cat_ref), custom_call_target="tpu_custom_call" | custom-call | tf_op jit(solution)/shard_map/pallas_call | solution.py:1027
  461.2 1.2 copy.95
  463.9 0.8 fusion.1
  464.7 1.4 convolution_add_fusion
  466.1 9.8 %all-to-all-start = ((f32[8,1,96]{2,1,0:T(1,128)}), f32[8,1,96]{2,1,0:T(1,128)}, u32[]{:S(2)}, u32[]{:S(2)}) async-start(f32[8,1,96]{2,1,0:T(1,128)} %bitcast.20), calls=%async_computation | async-start | bytes 8192 | tf_op jit(solution)/shard_map/all_to_all | solution.py:1126
  475.9 1.6 convolution_bitcast_fusion
  477.5 2.5 convolution_bitcast_fusion.1
  480.0 1.5 slice_reduce_fusion
  481.5 1.6 reduce_sum.42
  483.1 1.5 reduce_sum.43
  484.6 1.3 slice.95
  486.0 1.3 slice.97
  487.3 1.4 reduce_sum.41
  488.7 0.8 reshape.202
  490.1 1.4 reshape.203
  491.5 2.3 convert_reduce_fusion
  494.5 1.4 reshape.205
  496.0 2.8 bitcast_convert_fusion
  498.8 2.0 pad_maximum_fusion
  500.9 1.4 constant_dynamic-slice_fusion.4
  502.2 1.3 constant_dynamic-slice_fusion.3
  503.5 0.8 constant_dynamic-slice_fusion.1
  504.3 1.3 constant_dynamic-slice_fusion.2
  505.6 1.5 copy.84
  507.1 2.5 copy.85
  509.7 3.7 reshape.208
  513.3 3.0 reshape.212
  516.3 3.7 copy.87
  520.0 5.3 reshape.209
  526.5 1.3 reduce.16
  528.5 0.7 copy.106
  529.3 0.9 copy.107
  (85 shorter events, 18.2 us)
Async XLA Ops:
  0.6 32.1 %copy-start.4 = (bf16[2,96,2304]{2,1,0:T(8,128)(2,1)S(1)}, bf16[2,96,2304]{2,1,0:T(8,128)(2,1)}, u32[]{:S(2)}) copy-start(bf16[2,96,2304]{2,1,0:T(8,128)(2,1)} %param.17) | copy-start | bytes 2654212
  33.8 2.1 copy-start.3
  430.2 33.7 %copy-start = (bf16[2,96,4608]{2,1,0:T(8,128)(2,1)S(1)}, bf16[2,96,4608]{2,1,0:T(8,128)(2,1)}, u32[]{:S(2)}) copy-start(bf16[2,96,4608]{2,1,0:T(8,128)(2,1)} %ada_ref.1) | copy-start | bytes 5308420
  461.2 14.7 %copy-start.8 = (f32[8,128]{1,0:T(8,128)S(1)}, f32[8,128]{1,0:T(8,128)}, u32[]{:S(2)}) copy-start(f32[8,128]{1,0:T(8,128)} %get-tuple-element.65) | copy-start | bytes 12292
  462.4 0.7 copy-start.2
  463.9 12.0 %copy-start.1 = (f32[8,9216]{1,0:T(8,128)}, f32[8,9216]{1,0:T(8,128)S(1)}, u32[]{:S(2)}) copy-start(f32[8,9216]{1,0:T(8,128)S(1)} %get-tuple-element.74) | copy-start | bytes 884740
  466.1 59.9 %all-to-all-start = ((f32[8,1,96]{2,1,0:T(1,128)}), f32[8,1,96]{2,1,0:T(1,128)}, u32[]{:S(2)}, u32[]{:S(2)}) async-start(f32[8,1,96]{2,1,0:T(1,128)} %bitcast.20), calls=%async_computation | async-start | bytes 8192 | tf_op jit(solution)/shard_map/all_to_all | solution.py:1126
  490.1 3.7 copy-start.7
  520.0 7.9 %copy-start.9 = (bf16[1,768]{1,0:T(2,128)(2,1)S(1)}, bf16[1,768]{1,0:T(2,128)(2,1)}, u32[]{:S(2)}) copy-start(bf16[1,768]{1,0:T(2,128)(2,1)} %param.14) | copy-start | bytes 4612
  520.0 7.9 %copy-start.10 = (f32[1,768]{1,0:T(1,128)S(1)}, f32[1,768]{1,0:T(1,128)}, u32[]{:S(2)}) copy-start(f32[1,768]{1,0:T(1,128)} %get-tuple-element.72) | copy-start | bytes 9220
  520.0 8.5 %copy-start.6 = (bf16[256,768]{1,0:T(8,128)(2,1)S(1)}, bf16[256,768]{1,0:T(8,128)(2,1)}, u32[]{:S(2)}) copy-start(bf16[256,768]{1,0:T(8,128)(2,1)} %get-tuple-element.44) | copy-start | bytes 1179652
  520.0 9.2 %copy-start.5 = (f32[256,768]{1,0:T(8,128)S(1)}, f32[256,768]{1,0:T(8,128)}, u32[]{:S(2)}) copy-start(f32[256,768]{1,0:T(8,128)} %get-tuple-element.58) | copy-start | bytes 2359300

commit v4 on v3

--- a/solution.py
+++ b/solution.py
@@ -270,128 +270,163 @@
     return ((s // 2 + 1 - half) % 2) * 2 + (s % 2 + half + j) % 2
 
 
-def prep_kernel(n, cond_ref, small_ref, ada_ref, rows_ref, small_all, mod_ref,
-                crecv, msend, mrecv, c_s, c_r, b_s, b_r, m_s, m_r):
-    f = lax.axis_index("fsdp")
-    layers, rows, _ = ada_ref.shape
-    others = [{"fsdp": (f + k) % n} for k in range(1, n)]
-    entry_barrier(others)
-    first, second = [], []
-    for k in range(1, n):
-        to = (f + k) % n
-        first.append(rcopy(cond_ref.at[to], crecv.at[f], c_s.at[k], c_r.at[k], {"fsdp": to}))
-        first[-1].start()
-    for k in range(1, n):
-        to = (f + k) % n
-        second.append(rcopy(small_ref, small_all.at[f], b_s.at[k], b_r.at[k], {"fsdp": to}))
-        second[-1].start()
-    crecv[f] = cond_ref[f]
-    small_all[f] = small_ref[...]
-    for k in range(1, n):
-        at = (f - k + n) % n
-        rcopy(cond_ref.at[at], crecv.at[at], c_s.at[k], c_r.at[k], {"fsdp": at}).wait_recv()
-    cond_rows = jnp.sum(crecv[...], axis=1)
-    rows_ref[...] = cond_rows
-    cond_rows = cond_rows[:, :rows].astype(BF16)
-    for l in range(layers):
-        part = mm(cond_rows, ada_ref[l])
-        for i in range(n):
-            msend[i, l: l + 1, :] = part[i: i + 1, :]
-    third = []
-    for k in range(1, n):
-        to = (f + k) % n
-        third.append(rcopy(msend.at[to], mrecv.at[f], m_s.at[k], m_r.at[k], {"fsdp": to}))
-        third[-1].start()
-    mrecv[f] = msend[f]
-    for k in range(1, n):
-        at = (f - k + n) % n
-        rcopy(msend.at[at], mrecv.at[at], m_s.at[k], m_r.at[k], {"fsdp": at}).wait_recv()
-    mod_ref[...] = jnp.sum(mrecv[...], axis=0)
-    for k in range(1, n):
-        at = (f - k + n) % n
-        rcopy(small_ref, small_all.at[at], b_s.at[k], b_r.at[k], {"fsdp": at}).wait_recv()
-    for copy in first + second + third:
-        copy.wait_send()
-
-
-def prep(n, cond_blocks, small, ada_weight):
-    layers, rows, width6 = ada_weight.shape
-    lanes = cond_blocks.shape[-1]
-    return pl.pallas_call(
-        functools.partial(prep_kernel, n),
-        out_shape=(
-            jax.ShapeDtypeStruct((n, lanes), F32),
-            jax.ShapeDtypeStruct((n,) + small.shape, F32),
-            jax.ShapeDtypeStruct((layers, width6), F32),
-        ),
-        in_specs=vmem_specs(3),
-        out_specs=tuple(vmem_specs(3)),
-        scratch_shapes=[
-            pltpu.VMEM((n, 8, lanes), F32),
-            pltpu.VMEM((n, layers, width6), F32),
-            pltpu.VMEM((n, layers, width6), F32),
-        ] + [pltpu.SemaphoreType.DMA((n,))] * 6,
-        compiler_params=pltpu.CompilerParams(collective_id=0, has_side_effects=True),
-    )(cond_blocks, small, ada_weight)
-
-
 def forward_kernel(n, *refs):
-    (x_ref, mod_ref, bq_ref, bo_ref, bu_ref, bd_ref, sq_ref, so_ref, su_ref, sd_ref,
-     out_ref, wq_ref, wo_ref, wu_ref, wd_ref, xs_ref, attn_ref, qh_ref, tok_ref, branch_ref,
+    (x_ref, cond_ref, ada_ref, adab_ref, qkvw_ref, qvb_ref, outw_ref, outb_ref, upw_ref, upb_ref,
+     downw_ref, downb_ref,
+     out_ref, mod_ref, rows_ref, wq_ref, wo_ref, wu_ref, wd_ref, xs_ref, attn_ref, qh_ref, tok_ref, branch_ref,
      mid_ref, mlp_ref, up_ref, feed_ref,
-     osend, psend, precv, xsend, xrecv, own_feed,
-     z_s, z_r, y_s, y_r, a_s, a_r, t_s, t_r, g_s, g_r, r_s, r_r) = refs
+     osend, psend, precv, xpart, xsend, xrecv, own_feed,
+     sq_ref, so_ref, su_ref, bq_ref, bo_ref, bu_ref, bd_ref, cblock, crecv, bsend, brecv, msend, mrecv,
+     c_s, c_r, b_s, b_r, m_s, m_r, w_s, w_r, z_s, z_r, y_s, y_r, a_s, a_r, t_s, t_r, g_s, g_r, r_s, r_r) = refs
     f = lax.axis_index("fsdp")
     s = lax.axis_index("seq")
     slow = n // FAST
     a, b = f // FAST, f % FAST
-    layers, rows = sq_ref.shape[0], sq_ref.shape[1]
+    layers, rows = qkvw_ref.shape[0], qkvw_ref.shape[1]
     block = x_ref.shape[0]
     width = x_ref.shape[1]
     hc = sq_ref.shape[2] // 3
     heads = hc // HEAD_DIM
-    shards = (sq_ref, so_ref, su_ref, sd_ref)
-    full = (wq_ref, wo_ref, wu_ref, wd_ref)
+    fc = su_ref.shape[2] // n
+    chunk = downw_ref.shape[1] // 4
+    core = s % 2
     across, diagonal, partner = relative(s, 0), relative(s, 1), relative(s, 2)
     y_dev = {"fsdp": a * FAST + (1 - b)}
 
+    def place(l, p, at):
+        if p == 1:
+            return wo_ref.at[l, core, at]
+        return (wq_ref, None, wu_ref, wd_ref)[p].at[l, at]
+
     entry_barrier(
-        [{"fsdp": ((a + k) % slow) * FAST + b} for k in range(1, slow)] + [y_dev]
-        + [{"seq": across}, {"seq": diagonal}, {"seq": partner}]
+        [{"fsdp": (f + k) % n} for k in range(1, n)] + [{"seq": across}, {"seq": diagonal}, {"seq": partner}]
     )
 
+    cond = cond_ref[...].astype(F32)
+    act = cond / (1.0 + jnp.exp(-cond))
+    act = act.astype(BF16).astype(F32)
+    cblock[...] = jnp.zeros_like(cblock)
+    for i in range(n):
+        cblock[i, 0:1, :rows] = act[:, i * rows: (i + 1) * rows]
+    crecv[f] = cblock[f]
+    for k in range(1, n):
+        to = (f + k) % n
+        rcopy(cblock.at[to], crecv.at[f], c_s.at[k], c_r.at[k], {"fsdp": to}).start()
+    for l in range(layers):
+        bsend[l: l + 1, :] = jnp.concatenate(
+            [r[l: l + 1, :].astype(F32) for r in (adab_ref, outb_ref, downb_ref)], axis=1
+        )
+        bsend[layers + l: layers + l + 1, : hc + 4 * fc] = jnp.concatenate(
+            [r[l: l + 1, :].astype(F32) for r in (qvb_ref, upb_ref)], axis=1
+        )
+    brecv[f] = bsend[...]
+
+    def shard(l, p):
+        if p == 3:
+            return downw_ref.at[l, pl.ds(pl.multiple_of(s * chunk, chunk), chunk)]
+        return (sq_ref, so_ref, su_ref)[p].at[l]
+
+    for i in range(4):
+        @pl.when(s == i)
+        def _():
+            for l in range(layers):
+                sq_ref[l] = jnp.concatenate(
+                    [qkvw_ref[l, :, j * width + i * hc: j * width + (i + 1) * hc] for j in range(3)], axis=1
+                )
+                so_ref[l] = outw_ref[l, :, (i % 2) * (width // 2): (i % 2 + 1) * (width // 2)]
+                su_ref[l] = jnp.concatenate(
+                    [upw_ref[l, :, (4 * j + i) * fc: (4 * j + i + 1) * fc] for j in range(n)], axis=1
+                )
+
     def z_copy(l, p, k, to):
-        return rcopy(shards[p].at[l], full[p].at[l, f], z_s.at[l, p, k], z_r.at[l, p, k], {"fsdp": to})
+        return rcopy(shard(l, p), place(l, p, f), z_s.at[l, p, k], z_r.at[l, p, k], {"fsdp": to})
 
     def y_copy(l, p, k):
         at = ((a - k + slow) % slow) * FAST + b
-        src = shards[p].at[l] if k == 0 else full[p].at[l, at]
-        return rcopy(src, full[p].at[l, at], y_s.at[l, p, k], y_r.at[l, p, k], y_dev)
-
+        src = shard(l, p) if k == 0 else place(l, p, at)
+        return rcopy(src, place(l, p, at), y_s.at[l, p, k], y_r.at[l, p, k], y_dev)
+
+    def launch(l, p):
+        y_copy(l, p, 0).start()
+        for k in range(1, slow):
+            z_copy(l, p, k, ((a + k) % slow) * FAST + b).start()
+
+    launch(0, 0)
+    for k in range(1, n):
+        to = (f + k) % n
+        rcopy(bsend, brecv.at[f], b_s.at[k], b_r.at[k], {"fsdp": to}).start()
+
+    for k in range(1, n):
+        at = (f - k + n) % n
+        rcopy(cblock.at[at], crecv.at[at], c_s.at[k], c_r.at[k], {"fsdp": at}).wait_recv()
+    cond_rows = jnp.sum(crecv[...], axis=1)
+    rows_ref[...] = cond_rows
+    cond_rows = cond_rows[:, :rows].astype(BF16)
+    for l in range(layers):
+        part = mm(cond_rows, ada_ref[l])
+        for i in range(n):
+            msend[i, l: l + 1, :] = part[i: i + 1, :]
+    mrecv[f] = msend[f]
+    for k in range(1, n):
+        to = (f + k) % n
+        rcopy(msend.at[to], mrecv.at[f], m_s.at[k], m_r.at[k], {"fsdp": to}).start()
     for l in range(layers):
         for p in range(4):
-            y_copy(l, p, 0).start()
-            for k in range(1, slow):
-                z_copy(l, p, k, ((a + k) % slow) * FAST + b).start()
+            if l + p > 0:
+                launch(l, p)
 
     def forward_weights(l, p):
         for k in range(1, slow):
             at = ((a - k + slow) % slow) * FAST + b
-            rcopy(shards[p].at[l], full[p].at[l, at], z_s.at[l, p, k], z_r.at[l, p, k], {"fsdp": at}).wait_recv()
+            rcopy(shard(l, p), place(l, p, at), z_s.at[l, p, k], z_r.at[l, p, k], {"fsdp": at}).wait_recv()
             y_copy(l, p, k).start()
 
     def ready(l, p):
         for k in range(slow):
             at = ((a - k + slow) % slow) * FAST + 1 - b
-            rcopy(shards[p].at[l], full[p].at[l, at], y_s.at[l, p, k], y_r.at[l, p, k], y_dev).wait_recv()
+            rcopy(shard(l, p), place(l, p, at), y_s.at[l, p, k], y_r.at[l, p, k], y_dev).wait_recv()
 
     xs_ref[0] = x_ref[...].astype(F32)
+    for k in range(1, n):
+        at = (f - k + n) % n
+        rcopy(bsend, brecv.at[at], b_s.at[k], b_r.at[k], {"fsdp": at}).wait_recv()
+    ac = adab_ref.shape[1]
+    for l in range(layers):
+        gathered = lambda lo, size, r=l: jnp.concatenate([brecv[i, r: r + 1, lo: lo + size] for i in range(n)], axis=1)
+        bo_ref[l] = gathered(ac, rows)
+        bd_ref[l] = gathered(ac + rows, rows)
+        q_b, v_b = brecv[s, layers + l: layers + l + 1, :hc], brecv[4 + s, layers + l: layers + l + 1, :hc]
+        bq_ref[l] = jnp.concatenate([q_b, jnp.zeros_like(q_b), v_b], axis=1)
+    for i in range(4):
+        @pl.when(s == i)
+        def _():
+            for l in range(layers):
+                lo = hc + i * fc
+                bu_ref[l] = jnp.concatenate(
+                    [brecv[j, layers + l: layers + l + 1, lo: lo + fc] for j in range(n)], axis=1
+                )
+    for k in range(1, n):
+        at = (f - k + n) % n
+        rcopy(msend.at[at], mrecv.at[at], m_s.at[k], m_r.at[k], {"fsdp": at}).wait_recv()
+    mod = jnp.sum(mrecv[...], axis=0)
+    for l in range(layers):
+        full = mod[l: l + 1] + jnp.concatenate([brecv[i, l: l + 1, :ac] for i in range(n)], axis=1)
+        for r in range(6):
+            mod_ref[l, r: r + 1, :] = full[:, r * width: (r + 1) * width]
     for l in range(layers):
         for p in range(4):
-            full[p][l, f] = shards[p][l]
+            place(l, p, f)[...] = shard(l, p)[...]
 
     def matrix(ref, l):
         return ref[l].reshape(n * rows, ref.shape[3])
+
+    def half_copy(l):
+        ref = wo_ref.at[l, core]
+        return rcopy(ref, ref, w_s.at[l], w_r.at[l], {"seq": partner})
+
+    def half_arrived(l):
+        ref = wo_ref.at[l, 1 - core]
+        rcopy(ref, ref, w_s.at[l], w_r.at[l], {"seq": partner}).wait_recv()
 
     def gather(buf, l, send, recv, visit):
         mine = buf.at[l, s]
@@ -450,7 +485,14 @@
                 )
 
         gather(attn_ref, l, a_s, a_r, qkv_block)
-        forward_weights(l, 1)
+
+        @pl.when(l == 0)
+        def _():
+            forward_weights(0, 1)
+
+        @pl.when(l > 0)
+        def _():
+            forward_weights(l, 2)
 
         def attend_block(j, carry):
             t = relative(s, j)
@@ -468,21 +510,31 @@
             def _():
                 rcopy(osend.at[j], tok_ref.at[l, s], t_s.at[j], t_r.at[j], {"seq": t}).start()
 
-            @pl.when(j == 1)
-            def _():
-                forward_weights(l, 2)
+            @pl.when((j == 1) & (l == 0))
+            def _():
+                forward_weights(0, 2)
+
+            @pl.when((j == 1) & (l > 0))
+            def _():
+                forward_weights(l, 3)
+
+            @pl.when(j == 2)
+            def _():
+                ready(l, 1)
+                half_copy(l).start()
 
             return carry
 
         lax.fori_loop(0, 4, attend_block, 0)
         tok_ref[l, s] = osend[3]
-        forward_weights(l, 3)
-        ready(l, 1)
         for j in range(3):
             t = relative(s, j)
             rcopy(osend.at[j], tok_ref.at[l, t], t_s.at[j], t_r.at[j], {"seq": t}).wait_recv()
         tokens_out = jnp.concatenate([tok_ref[l, t] for t in range(4)], axis=1)
-        branch = mm(tokens_out, matrix(wo_ref, l)) + bo_ref[l]
+        half_arrived(l)
+        branch = jnp.concatenate(
+            [mm(tokens_out, wo_ref[l, c].reshape(n * rows, width // 2)) for c in range(2)], axis=1
+        ) + bo_ref[l]
         branch_ref[l] = branch
         middle = xs_ref[l] + row(2) * branch
         mid_ref[l] = middle
@@ -490,6 +542,10 @@
         mlp_ref[l, s] = (normed * (1.0 + row(4)) + row(3)).astype(BF16)
 
         def mlp_block(i, t):
+            @pl.when((i == 0) & (l == 0))
+            def _():
+                forward_weights(0, 3)
+
             @pl.when(i == 0)
             def _():
                 ready(l, 2)
@@ -511,26 +567,31 @@
 
             @pl.when(i == 2)
             def _():
-                xsend[...] = part
+                xpart[...] = part
 
             @pl.when(i == 3)
             def _():
                 psend[1] = part
                 rcopy(psend.at[1], precv.at[1], r_s.at[1], r_r.at[1], {"seq": partner}).start()
 
-            @pl.when((i == 1) & (l + 1 < layers))
+            @pl.when((i == 2) & (l + 1 < layers))
             def _():
                 forward_weights(1, 0)
 
         gather(mlp_ref, l, g_s, g_r, mlp_block)
         rcopy(psend.at[1], precv.at[1], r_s.at[1], r_r.at[1], {"seq": partner}).wait_recv()
-        xsend[...] = xsend[...] + precv[1]
+        xsend[...] = (xpart[...] + precv[1]).astype(BF16)
         over = rcopy(xsend, xrecv, r_s.at[2], r_r.at[2], {"seq": across})
         over.start()
+
+        @pl.when(l + 1 < layers)
+        def _():
+            forward_weights(1, 1)
+
         rcopy(psend.at[0], precv.at[0], r_s.at[0], r_r.at[0], {"seq": partner}).wait_recv()
         own_feed[...] = own_feed[...] + precv[0] + bd_ref[l]
         over.wait_recv()
-        feed = own_feed[...] + xrecv[...]
+        feed = own_feed[...] + xrecv[...].astype(F32)
         feed_ref[l] = feed
         nxt = mid_ref[l] + row(5) * feed
 
@@ -543,6 +604,7 @@
             out_ref[...] = nxt.astype(BF16)
 
         over.wait_send()
+        half_copy(l).wait_send()
         for i in range(2):
             rcopy(psend.at[i], precv.at[i], r_s.at[i], r_r.at[i], {"seq": partner}).wait_send()
         for j in range(3):
@@ -556,20 +618,29 @@
             for k in range(1, slow):
                 z_copy(l, p, k, ((a + k) % slow) * FAST + b).wait_send()
                 y_copy(l, p, k).wait_send()
-
-
-def forward(n, x, mod, bq, bo, bu, bd, sq, so, su, sd):
-    layers, rows, qc = sq.shape
+    for k in range(1, n):
+        to = (f + k) % n
+        rcopy(cblock.at[to], crecv.at[f], c_s.at[k], c_r.at[k], {"fsdp": to}).wait_send()
+        rcopy(bsend, brecv.at[f], b_s.at[k], b_r.at[k], {"fsdp": to}).wait_send()
+        rcopy(msend.at[to], mrecv.at[f], m_s.at[k], m_r.at[k], {"fsdp": to}).wait_send()
+
+
+def forward(n, x, cond, weights):
+    layers, rows, width6 = weights[0].shape
     block, width = x.shape
+    qc = weights[2].shape[2] // 4
     hc = qc // 3
     nh = qc // HEAD_DIM
-    uc = su.shape[2]
+    uc = weights[6].shape[2] // 4
     total = 4 * block
+    lanes = rows + -rows % 128
     sds = jax.ShapeDtypeStruct
     outs = (
         sds((block, width), BF16),
+        sds((layers, 6, width), F32),
+        sds((n, lanes), F32),
         sds((layers, n, rows, qc), BF16),
-        sds((layers, n, rows, width), BF16),
+        sds((layers, 2, n, rows, width // 2), BF16),
         sds((layers, n, rows, uc), BF16),
         sds((layers, n, rows, width), BF16),
         sds((layers, block, width), F32),
@@ -589,25 +660,39 @@
         pltpu.VMEM((2, block, width), F32),
         pltpu.VMEM((2, block, width), F32),
         pltpu.VMEM((block, width), F32),
+        pltpu.VMEM((block, width), BF16),
+        pltpu.VMEM((block, width), BF16),
         pltpu.VMEM((block, width), F32),
-        pltpu.VMEM((block, width), F32),
-    ] + [dma((layers, 4, slow))] * 4 + [dma((3,))] * 8
+        pltpu.VMEM((layers, rows, qc), BF16),
+        pltpu.VMEM((layers, rows, width // 2), BF16),
+        pltpu.VMEM((layers, rows, uc), BF16),
+        pltpu.VMEM((layers, 1, qc), F32),
+        pltpu.VMEM((layers, 1, width), F32),
+        pltpu.VMEM((layers, 1, uc), F32),
+        pltpu.VMEM((layers, 1, width), F32),
+        pltpu.VMEM((n, 8, lanes), F32),
+        pltpu.VMEM((n, 8, lanes), F32),
+        pltpu.VMEM((2 * layers, width), F32),
+        pltpu.VMEM((n, 2 * layers, width), F32),
+        pltpu.VMEM((n, layers, width6), F32),
+        pltpu.VMEM((n, layers, width6), F32),
+    ] + [dma((n,))] * 6 + [dma((layers,))] * 2 + [dma((layers, 4, slow))] * 4 + [dma((3,))] * 8
     return pl.pallas_call(
         functools.partial(forward_kernel, n),
         out_shape=outs,
-        in_specs=vmem_specs(10),
+        in_specs=vmem_specs(12),
         out_specs=tuple(vmem_specs(len(outs))),
         scratch_shapes=scratch,
         compiler_params=pltpu.CompilerParams(
             collective_id=1, has_side_effects=True, vmem_limit_bytes=VMEM_LIMIT
         ),
-    )(x, mod, bq, bo, bu, bd, sq, so, su, sd)
+    )(x, cond, *weights)
 
 
 def backward_kernel(n, *refs):
-    (cot_ref, mod_ref), rest = refs[:2], refs[2:]
+    (cot_ref, mod_ref, ada_ref), rest = refs[:3], refs[3:]
     stored, rest = rest[:13], rest[13:]
-    (g_ref, dmod_ref, gob_ref, gdb_ref, gub_ref, gqb_ref), rest = rest[:6], rest[6:]
+    (g_ref, vec_all, cat_all, gcond_ref), rest = rest[:4], rest[4:]
     fin, rest = rest[:4], rest[4:]
     loaded, rest = rest[:13], rest[13:]
     grads, rest = rest[:4], rest[4:]
@@ -615,9 +700,10 @@
     z_out, rest = rest[:4], rest[4:]
     z_in, rest = rest[:4], rest[4:]
     kept, rest = rest[:4], rest[4:]
-    (gf_ref, act_ref, gup_ref, gosend, go_ref, goh_ref, gqh_ref, gqkv_ref, psend, precv, xsend, xrecv,
-     own_part, gmid_ref, dk_acc, dv_acc,
-     l_s, y_s, y_r, z_s, z_r, f_s, f_r, g_s, g_r, t_s, t_r, r_s, r_r) = rest
+    (gf_ref, act_ref, gup_ref, gosend, go_ref, goh_ref, gqh_ref, gqkv_ref, psend, precv, xpart, xsend, xrecv,
+     own_part, gmid_ref, osend, orecv,
+     vec_ref, cat_ref, vec_in, vec_sum, cat_in, gc_send, gc_recv, v_s, v_r, u_s, u_r, k_s, k_r, h_s, h_r, i_s, i_r, dk_acc, dv_acc,
+     l_s, o_s, o_r, y_s, y_r, z_s, z_r, f_s, f_r, g_s, g_r, t_s, t_r, r_s, r_r) = rest
     wq, wo, wu, wd, xs, attn, qh, tok, branch, mid, mlp, up, feed = range(13)
     down, upw, outw, qkvw = range(4)
     f = lax.axis_index("fsdp")
@@ -639,7 +725,7 @@
         load(i, layers - 1).start()
 
     entry_barrier(
-        [{"fsdp": ((a + k) % slow) * FAST + b} for k in range(1, slow)] + [y_dev]
+        [{"fsdp": (f + k) % n} for k in range(1, n)]
         + [{"seq": across}, {"seq": diagonal}, {"seq": partner}]
     )
 
@@ -699,7 +785,7 @@
 
         @pl.when(j == 0)
         def _():
-            xsend[...] = part
+            xpart[...] = part
 
         @pl.when(j == 1)
         def _():
@@ -708,17 +794,43 @@
 
     def send_across():
         part_copy(1).wait_recv()
-        xsend[...] = xsend[...] + precv[1]
+        xsend[...] = (xpart[...] + precv[1]).astype(BF16)
         over.start()
 
     def collect():
         part_copy(0).wait_recv()
         own_part[...] = own_part[...] + precv[0]
         over.wait_recv()
-        own_part[...] = own_part[...] + xrecv[...]
+        own_part[...] = own_part[...] + xrecv[...].astype(F32)
         over.wait_send()
         part_copy(0).wait_send()
         part_copy(1).wait_send()
+
+    def vec_copy(l, j):
+        return rcopy(vec_ref.at[l], vec_in.at[l, s], v_s.at[l, j], v_r.at[l, j], {"seq": relative(s, j)})
+
+    def vec_start(l):
+        vec_in[l, s] = vec_ref[l]
+        for j in range(3):
+            vec_copy(l, j).start()
+
+    def vec_spread(l):
+        for j in range(3):
+            ref = vec_in.at[l, relative(s, j)]
+            rcopy(ref, ref, v_s.at[l, j], v_r.at[l, j], {"seq": relative(s, j)}).wait_recv()
+        vec_sum[l] = jnp.sum(vec_in[l], axis=0)
+        vec_all[l, f] = vec_sum[l]
+        cat_in[l, f] = cat_ref[l]
+        for k in range(1, n):
+            to = {"fsdp": (f + k) % n}
+            rcopy(vec_sum.at[l], vec_all.at[l, f], u_s.at[l, k], u_r.at[l, k], to).start()
+            rcopy(cat_ref.at[l], cat_in.at[l, f], k_s.at[l, k], k_r.at[l, k], to).start()
+
+    def vec_arrived(l):
+        for k in range(1, n):
+            at = (f - k + n) % n
+            rcopy(vec_sum.at[l], vec_all.at[l, at], u_s.at[l, k], u_r.at[l, k], {"fsdp": at}).wait_recv()
+            rcopy(cat_ref.at[l], cat_in.at[l, at], k_s.at[l, k], k_r.at[l, k], {"fsdp": at}).wait_recv()
 
     def sums(value):
         return jnp.sum(value, axis=0, keepdims=True)
@@ -741,9 +853,9 @@
         relay = rcopy(theirs, theirs, g_s.at[2], g_r.at[2], {"seq": partner})
         to_across.start()
         to_partner.start()
-        dmod_ref[l, 5:6, :] = sums(g * loaded[feed][...])
-        gdb_ref[l] = sums(g_feed.astype(F32))
-        gub_ref[l] = jnp.zeros((1, gub_ref.shape[2]), F32)
+        vec_ref[l, 5:6, :] = sums(g * loaded[feed][...])
+        vec_ref[l, 7:8, :] = sums(g_feed.astype(F32))
+        cat_ref[l] = jnp.zeros_like(cat_ref[l])
         for i in (wd, up, wu, mlp):
             load(i, l).wait()
 
@@ -769,7 +881,7 @@
             act_ref[t] = value.astype(BF16)
             g_up = (mm_nt(gf_ref[t], matrix(wd)) * slope).astype(BF16)
             gup_ref[t] = g_up
-            gub_ref[l] = gub_ref[l] + sums(g_up.astype(F32))
+            cat_ref[l, 0:1, :] = cat_ref[l, 0:1, :] + sums(g_up.astype(F32))
             place(j, mm_nt(g_up, matrix(wu)))
             return carry
 
@@ -800,14 +912,17 @@
             load(i, l).wait()
         collect()
         g_min = own_part[...]
-        dmod_ref[l, 4:5, :] = sums(g_min * normed)
-        dmod_ref[l, 3:4, :] = sums(g_min)
+        vec_ref[l, 4:5, :] = sums(g_min * normed)
+        vec_ref[l, 3:4, :] = sums(g_min)
         g_mid = g_ref[...] + norm_back(g_min * (1.0 + row(4)), normed, inverse)
         gmid_ref[...] = g_mid
         g_branch = (row(2) * g_mid).astype(BF16)
-        dmod_ref[l, 2:3, :] = sums(g_mid * loaded[branch][...])
-        gob_ref[l] = sums(g_branch.astype(F32))
-        g_o = mm_nt(g_branch, matrix(wo)).astype(BF16)
+        vec_ref[l, 2:3, :] = sums(g_mid * loaded[branch][...])
+        vec_ref[l, 6:7, :] = sums(g_branch.astype(F32))
+        half = width // 2
+        g_o = sum(
+            mm_nt(g_branch[:, c * half: (c + 1) * half], loaded[wo][c].reshape(width, half)) for c in range(2)
+        ).astype(BF16)
         for t in range(4):
             gosend[t] = g_o[:, t * hc: (t + 1) * hc]
 
@@ -819,8 +934,10 @@
             head_copy(j).start()
         go_ref[s] = gosend[s]
         tokens_out = jnp.concatenate([loaded[tok][t] for t in range(4)], axis=1)
-        grads[outw][...] = mm_tn(tokens_out, g_branch).astype(BF16).reshape(grads[outw].shape)
-        y_copy(l, outw).start()
+        for c in range(2):
+            osend[c] = mm_tn(tokens_out, g_branch[:, c * half: (c + 1) * half]).astype(BF16)
+        pair = rcopy(osend.at[1 - s % 2], orecv.at[l], o_s.at[0], o_r.at[l], {"seq": partner})
+        pair.start()
 
         @pl.when(l > 0)
         def _():
@@ -830,7 +947,13 @@
         @pl.when(step > 0)
         def _():
             z_finish(l + 1, qkvw)
-
+            vec_spread(l + 1)
+
+        pair.wait_recv()
+        out_sum = osend[s % 2].astype(F32) + orecv[l].astype(F32)
+        grads[outw][...] = out_sum.astype(BF16).reshape(grads[outw].shape)
+        y_copy(l, outw).start()
+        pair.wait_send()
         load(qh, l).wait()
         for j in range(3):
             t = relative(s, j)
@@ -888,7 +1011,7 @@
         load(attn, l).wait()
         grads[qkvw][...] = mm_tn(whole(loaded[attn]), whole(gqkv_ref)).astype(BF16).reshape(grads[qkvw].shape)
         y_copy(l, qkvw).start()
-        gqb_ref[l] = sums(whole(gqkv_ref).astype(F32))
+        cat_ref[l, 1:2, : 3 * hc] = sums(whole(gqkv_ref).astype(F32))
         z_start(l, outw)
         z_finish(l, down)
         z_finish(l, upw)
@@ -902,28 +1025,80 @@
 
         collect()
         g_ain = own_part[...]
-        dmod_ref[l, 1:2, :] = sums(g_ain * normed)
-        dmod_ref[l, 0:1, :] = sums(g_ain)
+        vec_ref[l, 1:2, :] = sums(g_ain * normed)
+        vec_ref[l, 0:1, :] = sums(g_ain)
         g_ref[...] = gmid_ref[...] + norm_back(g_ain * (1.0 + row(1)), normed, inverse)
+
+        @pl.when(l > 0)
+        def _():
+            vec_start(l)
+
         return carry
 
     lax.fori_loop(0, layers, layer, 0)
+    vec_start(0)
     z_start(0, qkvw)
     z_finish(0, outw)
-    z_finish(0, qkvw)
-    for l in reversed(range(layers)):
+    vec_spread(0)
+    for l in range(1, layers):
         for p in (down, upw, outw, qkvw):
             fin_arrived(l, p, 1)
             fin_copy(l, p, 2).start()
+    z_finish(0, qkvw)
+    for l in range(layers):
+        vec_arrived(l)
+        cat_all[l, s] = jnp.sum(cat_in[l], axis=0)
+    for j in range(3):
+        ref = cat_all.at[:, s]
+        rcopy(ref, ref, h_s.at[j], h_r.at[j], {"seq": relative(s, j)}).start()
+    g_cond = jnp.zeros((n, rows), F32)
+    for l in range(layers):
+        for r in range(6):
+            d = vec_all[l, :, r, :]
+            high = d.astype(BF16)
+            low = (d - high.astype(F32)).astype(BF16)
+            w = ada_ref[l, :, r * width: (r + 1) * width]
+            g_cond = g_cond + mm_nt(high, w) + mm_nt(low, w)
+    for i in range(n):
+        gc_send[i, 0:1, :rows] = g_cond[i: i + 1, :]
+
+    def cond_copy(k):
+        to = (f + k) % n
+        return rcopy(gc_send.at[to], gc_recv.at[f], i_s.at[k], i_r.at[k], {"fsdp": to})
+
+    gc_recv[f] = gc_send[f]
+    for k in range(1, n):
+        cond_copy(k).start()
+    for p in (down, upw, outw, qkvw):
+        fin_arrived(0, p, 1)
+        fin_copy(0, p, 2).start()
+    for k in range(1, n):
+        at = (f - k + n) % n
+        rcopy(gc_send.at[at], gc_recv.at[at], i_s.at[k], i_r.at[k], {"fsdp": at}).wait_recv()
+    gcond_ref[...] = jnp.concatenate([gc_recv[i, 0:1, :rows] for i in range(n)], axis=1)
+    for j in range(3):
+        ref = cat_all.at[:, relative(s, j)]
+        rcopy(ref, ref, h_s.at[j], h_r.at[j], {"seq": relative(s, j)}).wait_recv()
     for l in range(layers):
         for p in range(4):
             fin_arrived(l, p, 0)
             fin_arrived(l, p, 2)
             for i in range(3):
                 fin_copy(l, p, i).wait_send()
-
-
-def backward(n, cot, mod, stored):
+    for k in range(1, n):
+        cond_copy(k).wait_send()
+        to = {"fsdp": (f + k) % n}
+        for l in range(layers):
+            rcopy(vec_sum.at[l], vec_all.at[l, f], u_s.at[l, k], u_r.at[l, k], to).wait_send()
+            rcopy(cat_ref.at[l], cat_in.at[l, f], k_s.at[l, k], k_r.at[l, k], to).wait_send()
+    for j in range(3):
+        ref = cat_all.at[:, s]
+        rcopy(ref, ref, h_s.at[j], h_r.at[j], {"seq": relative(s, j)}).wait_send()
+        for l in range(layers):
+            vec_copy(l, j).wait_send()
+
+
+def backward(n, cot, mod, ada, stored):
     layers = mod.shape[0]
     block, width = cot.shape
     rows = width // n
@@ -934,14 +1109,12 @@
     nh = qc // HEAD_DIM
     sds = jax.ShapeDtypeStruct
     dma = pltpu.SemaphoreType.DMA
-    columns = (width, uc, width, qc)
+    columns = (width, uc, width // 2, qc)
     outs = [
         sds((block, width), F32),
-        sds((layers, 6, width), F32),
-        sds((layers, 1, width), F32),
-        sds((layers, 1, width), F32),
-        sds((layers, 1, uc), F32),
-        sds((layers, 1, qc), F32),
+        sds((layers, n, 8, width), F32),
+        sds((layers, 4, 2, uc), F32),
+        sds((1, width), F32),
     ] + [sds((layers, 4, rows, c), BF16) for c in columns]
     scratch = (
         [pltpu.VMEM(x.shape[1:], x.dtype) for x in stored]
@@ -962,12 +1135,25 @@
             pltpu.VMEM((2, block, width), F32),
             pltpu.VMEM((2, block, width), F32),
             pltpu.VMEM((block, width), F32),
+            pltpu.VMEM((block, width), BF16),
+            pltpu.VMEM((block, width), BF16),
             pltpu.VMEM((block, width), F32),
             pltpu.VMEM((block, width), F32),
-            pltpu.VMEM((block, width), F32),
+            pltpu.VMEM((2, width, width // 2), BF16),
+            pltpu.VMEM((layers, width, width // 2), BF16),
+            pltpu.VMEM((layers, 8, width), F32),
+            pltpu.VMEM((layers, 2, uc), F32),
+            pltpu.VMEM((layers, 4, 8, width), F32),
+            pltpu.VMEM((layers, 8, width), F32),
+            pltpu.VMEM((layers, n, 2, uc), F32),
+            pltpu.VMEM((n, 8, rows + -rows % 128), F32),
+            pltpu.VMEM((n, 8, rows + -rows % 128), F32),
+            dma((layers, 3)), dma((layers, 3)),
+            dma((layers, n)), dma((layers, n)), dma((layers, n)), dma((layers, n)),
+            dma((3,)), dma((3,)), dma((n,)), dma((n,)),
             pltpu.VMEM((4 * block, HEAD_DIM), F32),
             pltpu.VMEM((4 * block, HEAD_DIM), F32),
-            dma((13,)),
+            dma((13,)), dma((1,)), dma((layers,)),
             dma((4,)), dma((layers, 4)),
             dma((4, slow)), dma((layers, 4, slow)),
             dma((layers, 4, 3)), dma((layers, 4, 3)),
@@ -977,63 +1163,102 @@
     return pl.pallas_call(
         functools.partial(backward_kernel, n),
         out_shape=tuple(outs),
-        in_specs=vmem_specs(2) + [pl.BlockSpec(memory_space=pl.ANY)] * 13,
+        in_specs=vmem_specs(3) + [pl.BlockSpec(memory_space=pl.ANY)] * 13,
         out_specs=tuple(vmem_specs(len(outs))),
         scratch_shapes=scratch,
         compiler_params=pltpu.CompilerParams(
             collective_id=2, has_side_effects=True, vmem_limit_bytes=VMEM_LIMIT
         ),
-    )(cot, mod, *stored)
-
-
-def tail_kernel(n, sum_ref, cat_ref, sums_all, cats_all, s_in, c_all, s_tot,
-                a_s, a_r, b_s, b_r, c_s, c_r, d_s, d_r):
+    )(cot, mod, ada, *stored)
+
+
+def assemble_kernel(n, vec_ref, cat_ref, rows_ref, gcond_ref, cond_ref, fd_ref, fu_ref, fo_ref, fq_ref,
+                    gcondition, g_adab, g_qvb, g_ob, g_ub, g_db, g_ada, g_qkv, g_out, g_up, g_down,
+                    ada_buf, qkv_buf, out_buf, up_buf, down_buf, sem):
     f = lax.axis_index("fsdp")
-    s = lax.axis_index("seq")
-    entry_barrier([{"seq": relative(s, j)} for j in range(3)] + [{"fsdp": (f + k) % n} for k in range(1, n)])
-    sends = []
-    for j in range(3):
-        t = relative(s, j)
-        sends.append(rcopy(sum_ref, s_in.at[s], a_s.at[j], a_r.at[j], {"seq": t}))
-        sends[-1].start()
-        sends.append(rcopy(cat_ref, c_all.at[s], b_s.at[j], b_r.at[j], {"seq": t}))
-        sends[-1].start()
-    s_in[s] = sum_ref[...]
-    c_all[s] = cat_ref[...]
-    for j in range(3):
-        t = relative(s, j)
-        rcopy(sum_ref, s_in.at[t], a_s.at[j], a_r.at[j], {"seq": t}).wait_recv()
-        rcopy(cat_ref, c_all.at[t], b_s.at[j], b_r.at[j], {"seq": t}).wait_recv()
-    s_tot[...] = jnp.sum(s_in[...], axis=0)
-    sums_all[f] = s_tot[...]
-    cats_all[f] = c_all[...]
-    for k in range(1, n):
-        to = {"fsdp": (f + k) % n}
-        sends.append(rcopy(s_tot, sums_all.at[f], c_s.at[k], c_r.at[k], to))
-        sends[-1].start()
-        sends.append(rcopy(c_all, cats_all.at[f], d_s.at[k], d_r.at[k], to))
-        sends[-1].start()
-    for k in range(1, n):
-        at = (f - k + n) % n
-        rcopy(s_tot, sums_all.at[at], c_s.at[k], c_r.at[k], {"fsdp": at}).wait_recv()
-        rcopy(c_all, cats_all.at[at], d_s.at[k], d_r.at[k], {"fsdp": at}).wait_recv()
-    for copy in sends:
-        copy.wait_send()
-
-
-def tail(n, sums, cats):
+    layers, rows = fd_ref.shape[0], fd_ref.shape[2]
+    width = rows * n
+    hc = fq_ref.shape[3] // 3
+    fc = fu_ref.shape[3] // n
+    ac = g_adab.shape[1]
+    copies = []
+
+    def write(i, l, buf, out):
+        copies.append(pltpu.make_async_copy(buf.at[l], out.at[l], sem.at[i, l]))
+        copies[-1].start()
+
+    for l in range(layers):
+        for t in range(4):
+            down_buf[l, t * rows: (t + 1) * rows, :] = fd_ref[l, t].astype(F32)
+        write(0, l, down_buf, g_down)
+    for l in range(layers):
+        for j in range(n):
+            up_buf[l, :, 4 * j * fc: 4 * (j + 1) * fc] = jnp.concatenate(
+                [fu_ref[l, t, :, j * fc: (j + 1) * fc].astype(F32) for t in range(4)], axis=1
+            )
+        write(1, l, up_buf, g_up)
+    cond_rows = rows_ref[:, :rows].astype(BF16)
+    for l in range(layers):
+        for r in range(6):
+            d = vec_ref[l, :, r, :]
+            high = d.astype(BF16)
+            low = d - high.astype(F32)
+            mid = low.astype(BF16)
+            low = (low - mid.astype(F32)).astype(BF16)
+            ada_buf[l, :, r * width: (r + 1) * width] = (
+                mm_tn(cond_rows, high) + mm_tn(cond_rows, mid) + mm_tn(cond_rows, low)
+            )
+        write(2, l, ada_buf, g_ada)
+    for l in range(layers):
+        for j in range(3):
+            qkv_buf[l, :, j * width: (j + 1) * width] = jnp.concatenate(
+                [fq_ref[l, t, :, j * hc: (j + 1) * hc].astype(F32) for t in range(4)], axis=1
+            )
+        write(3, l, qkv_buf, g_qkv)
+    for l in range(layers):
+        for c in range(2):
+            out_buf[l, :, c * (width // 2): (c + 1) * (width // 2)] = (
+                fo_ref[l, c].astype(F32) + fo_ref[l, 2 + c].astype(F32)
+            )
+        write(4, l, out_buf, g_out)
+    cond = cond_ref[...].astype(F32)
+    gate = 1.0 / (1.0 + jnp.exp(-cond))
+    gcondition[...] = gcond_ref[...] * (gate * (1.0 + cond * (1.0 - gate)))
+    total = [jnp.sum(vec_ref[l], axis=0) for l in range(layers)]
+    for i in range(n):
+        @pl.when(f == i)
+        def _():
+            for l in range(layers):
+                at = slice(l, l + 1)
+                flat = jnp.concatenate([total[l][r: r + 1, :] for r in range(6)], axis=1)
+                g_adab[at, :] = flat[:, i * ac: (i + 1) * ac]
+                g_ob[at, :] = total[l][6:7, i * rows: (i + 1) * rows]
+                g_db[at, :] = total[l][7:8, i * rows: (i + 1) * rows]
+                g_ub[at, :] = jnp.concatenate(
+                    [cat_ref[l, t, 0:1, i * fc: (i + 1) * fc] for t in range(4)], axis=1
+                )
+                lo = (i // 4) * 2 * hc
+                g_qvb[at, :] = cat_ref[l, i % 4, 1:2, lo: lo + hc]
+    for copy in copies:
+        copy.wait()
+
+
+def assemble(n, vec_all, cat_all, cond_rows, g_cond, cond, fins):
+    layers, _, rows, width = fins[0].shape
+    uc, qc = fins[1].shape[3], fins[3].shape[3]
     sds = jax.ShapeDtypeStruct
-    dma = pltpu.SemaphoreType.DMA
+    big = [(layers, rows, 6 * width), (layers, rows, 4 * qc), (layers, rows, width),
+           (layers, rows, 4 * uc), (layers, 4 * rows, width)]
+    small = [(1, width), (layers, 6 * width // n), (layers, 2 * width // n), (layers, rows),
+             (layers, 4 * uc // n), (layers, rows)]
     return pl.pallas_call(
-        functools.partial(tail_kernel, n),
-        out_shape=(sds((n,) + sums.shape, F32), sds((n, 4) + cats.shape, F32)),
-        in_specs=vmem_specs(2),
-        out_specs=tuple(vmem_specs(2)),
-        scratch_shapes=[
-            pltpu.VMEM((4,) + sums.shape, F32), pltpu.VMEM((4,) + cats.shape, F32), pltpu.VMEM(sums.shape, F32),
-        ] + [dma((3,))] * 4 + [dma((n,))] * 4,
-        compiler_params=pltpu.CompilerParams(collective_id=3, has_side_effects=True),
-    )(sums, cats)
+        functools.partial(assemble_kernel, n),
+        out_shape=tuple(sds(x, F32) for x in small + big),
+        in_specs=vmem_specs(9),
+        out_specs=tuple(vmem_specs(6) + [pl.BlockSpec(memory_space=pl.ANY)] * 5),
+        scratch_shapes=[pltpu.VMEM(x, F32) for x in big] + [pltpu.SemaphoreType.DMA((5, layers))],
+        compiler_params=pltpu.CompilerParams(vmem_limit_bytes=VMEM_LIMIT),
+    )(vec_all, cat_all, cond_rows, g_cond, cond, *fins)
 
 
 def fused_device(
@@ -1041,94 +1266,14 @@
     up_weight, up_bias, down_weight, down_bias, cotangent,
 ):
     n = lax.axis_size("fsdp")
-    ns = lax.axis_size("seq")
-    f = lax.axis_index("fsdp")
-    s = lax.axis_index("seq")
-    layers, rows, width6 = ada_weight.shape
-    width = rows * n
-    ff = up_weight.shape[2]
-    hc = width // ns
-    fc = ff // (ns * n)
-
-    def take(x, axis):
-        return lax.dynamic_index_in_dim(x, s, axis, keepdims=False)
-
-    def own(x, axis, size):
-        return lax.dynamic_slice_in_dim(x, f * size, size, axis)
-
-    fw = n * fc
-    s_q = take(qkv_weight.reshape(layers, rows, 3, ns, hc), 3).reshape(layers, rows, 3 * hc)
-    s_u = take(up_weight.reshape(layers, rows, n, ns, fc), 3).reshape(layers, rows, fw)
-    s_d = take(down_weight.reshape(layers, ns, fc, width), 1)
-
-    cond_float = condition.astype(F32)
-    cond_act = jax.nn.silu(cond_float).astype(BF16)
-    cond_blocks = jnp.pad(cond_act.astype(F32).reshape(n, 1, rows), ((0, 0), (0, 7), (0, -rows % 128)))
-    small = jnp.concatenate(
-        [ada_bias.reshape(-1), qv_bias.reshape(-1), out_bias.reshape(-1), up_bias.reshape(-1),
-         down_bias.reshape(-1)]
-    ).astype(F32).reshape(8, -1)
-    cond_rows, small, mod = prep(n, cond_blocks, small, ada_weight)
-    cond_rows = cond_rows[:, :rows]
-    small = small.reshape(n, -1)
-    pos = 0
-
-    def unpack(per_layer):
-        nonlocal pos
-        part = small[:, pos: pos + layers * per_layer].reshape(n, layers, per_layer)
-        pos += layers * per_layer
-        return part.transpose(1, 0, 2).reshape(layers, n * per_layer)
-
-    ada_b = unpack(ada_bias.shape[1])
-    qv_b = unpack(qv_bias.shape[1])
-    out_b = unpack(out_bias.shape[1])
-    up_b = unpack(up_bias.shape[1])
-    down_b = unpack(down_bias.shape[1])
-    q_b = take(qv_b[:, :width].reshape(layers, ns, hc), 1)
-    v_b = take(qv_b[:, width:].reshape(layers, ns, hc), 1)
-    qkv_b = jnp.concatenate([q_b, jnp.zeros_like(q_b), v_b], axis=1)
-    up_bs = take(up_b.reshape(layers, n, ns, fc), 2).reshape(layers, fw)
-    mod = mod + ada_b
-
-    (block_out, w_q, w_o, w_u, w_d, xs, attn, qh, tok, branches, mids, mlp, ups, feeds) = forward(
-        n, tokens[0], mod.reshape(layers, 6, width), qkv_b[:, None], out_b[:, None], up_bs[:, None],
-        down_b[:, None], s_q, out_weight, s_u, s_d)
-    (g, d_mod, g_ob, g_db, g_ub, g_qb, grad_down, grad_up, grad_out, grad_qkv) = backward(
-        n, cotangent[0], mod.reshape(layers, 6, width),
-        (w_q, w_o, w_u, w_d, xs, attn, qh, tok, branches, mids, mlp, ups, feeds))
-    grad_up = grad_up.reshape(layers, ns, rows, n, fc).transpose(0, 2, 3, 1, 4).reshape(layers, rows, ff).astype(F32)
-    grad_down = grad_down.reshape(layers, ns * fc, width).astype(F32)
-    grad_qkv = grad_qkv.reshape(layers, ns, rows, 3, hc).transpose(0, 2, 3, 1, 4)
-    grad_qkv = grad_qkv.reshape(layers, rows, 3 * width).astype(F32)
-    grad_out = jnp.sum(grad_out.astype(F32), axis=1)
-
-    sums = jnp.concatenate([d_mod.reshape(-1), g_ob.reshape(-1), g_db.reshape(-1)])
-    g_qvb = jnp.concatenate([g_qb[:, 0, :hc], g_qb[:, 0, 2 * hc:]], axis=1)
-    cats = jnp.concatenate([g_ub.reshape(-1), g_qvb.reshape(-1)])
-    sums_all, cats_all = tail(n, sums.reshape(8, -1), cats.reshape(8, -1))
-    sums_all = sums_all.reshape(n, -1)
-    d_mod_all = sums_all[:, : layers * width6].reshape(n, layers, width6)
-    g_bias = jnp.sum(sums_all[:, layers * width6:], axis=0).reshape(2, layers, n, rows)
-    g_bias = lax.dynamic_index_in_dim(g_bias, f, 2, keepdims=False)
-    cats_all = jnp.sum(cats_all.reshape(n, ns, -1), axis=0)
-    g_ub = cats_all[:, : layers * fw].reshape(ns, layers, n, fc)
-    g_ub = lax.dynamic_index_in_dim(g_ub, f, 2, keepdims=False).transpose(1, 0, 2).reshape(layers, ns * fc)
-    g_qvb = cats_all[:, layers * fw:].reshape(ns, layers, 2, hc).transpose(1, 2, 0, 3).reshape(layers, -1)
-    g_qvb = own(g_qvb, 1, qv_bias.shape[1])
-
-    grad_ada = jnp.stack([
-        lax.dot_general(cond_rows, d_mod_all[:, l], (((0,), (0,)), ((), ())), precision=HIGHEST,
-                        preferred_element_type=F32) for l in range(layers)])
-    grad_ada_bias = own(jnp.sum(d_mod_all, axis=0), 1, width6 // n)
-    g_cond = sum(
-        lax.dot_general(d_mod_all[:, l], ada_weight[l].astype(F32), (((1,), (1,)), ((), ())),
-                        precision=HIGHEST, preferred_element_type=F32) for l in range(layers))
-    g_cond = lax.all_to_all(g_cond, "fsdp", split_axis=0, concat_axis=1, tiled=True)
-    _, silu_back = jax.vjp(jax.nn.silu, cond_float)
-    grad_condition = silu_back(g_cond)[0]
+    block_out, mod, cond_rows, *stored = forward(
+        n, tokens[0], condition,
+        (ada_weight, ada_bias, qkv_weight, qv_bias, out_weight, out_bias, up_weight, up_bias, down_weight, down_bias))
+    g, vec_all, cat_all, g_cond, *fins = backward(n, cotangent[0], mod, ada_weight, stored)
+    (g_condition, g_adab, g_qvb, g_ob, g_ub, g_db, g_ada, g_qkv, g_out, g_up, g_down) = assemble(
+        n, vec_all, cat_all, cond_rows, g_cond, condition, fins)
     return (
-        block_out[None], g[None], grad_condition, grad_ada, grad_ada_bias, grad_qkv, g_qvb,
-        grad_out, g_bias[0], grad_up, g_ub, grad_down, g_bias[1],
+        block_out[None], g[None], g_condition, g_ada, g_adab, g_qkv, g_qvb, g_out, g_ob, g_up, g_ub, g_down, g_db,
     )
 
 
@@ -1139,7 +1284,7 @@
 
     def per_device(*args):
         rows = args[2].shape[1]
-        fits = rows % 32 == 0 and mesh.shape["seq"] == 4 and args[0].shape[0] == 1
+        fits = rows % 32 == 0 and mesh.shape["seq"] == 4 and mesh.shape["fsdp"] == 8 and args[0].shape[0] == 1
         return (fused_device if fits else plain_device)(*args)
 
     return jax.shard_map(

time: 535 us -> 360 us (0.67)
  Pallas kernels: 432 us -> 356 us
  local copies, waits for them, and re-layouts: 63.4 us -> 2.65 us
  other arithmetic: 18 us -> 0 us
  starting transfers between devices: 9.81 us -> 0 us
  matrix products: 6.24 us -> 0 us
    pallas_call x2 -> x1, Pallas kernels: 44.4 us -> 9.04 us  [assemble(): pl.pallas_call(functools.partial(assemble_kernel, n), out_shape=tuple((sd...]
    pallas_call x1, Pallas kernels: 201 us -> 179 us  [backward(): pl.pallas_call(functools.partial(backward_kernel, n), out_shape=tuple(out...]
    convert_element_type x7 -> x0, local copies, waits for them, and re-layouts: 20.4 us -> none  [the longest x3 12 us: fused_device(): grad_up.reshape(layers, ns, rows, n, fc).transpose(0, 2, 3, 1, 4)]
    pallas_call x1, Pallas kernels: 186 us -> 168 us  [forward(): pl.pallas_call(functools.partial(forward_kernel, n), out_shape=outs, in_s...]
    reshape x33 -> x0, local copies, waits for them, and re-layouts: 17.8 us -> none  [the longest x2 2.21 us: fused_device(): cats_all[:, layers * fw:].reshape(ns, layers, 2, hc).transpose(1, 2, 0, 3)]
    all_to_all x1 -> x0, starting transfers between devices: 9.81 us -> none  [fused_device(): lax.all_to_all(g_cond, 'fsdp', split_axis=0, concat_axis=1, tiled=True)]
    dynamic_slice x7 -> x0, local copies, waits for them, and re-layouts: 6.61 us -> none  [the longest x4 3.16 us: take(): return lax.dynamic_index_in_dim(x, s, axis, keepdims=False)]
    dot_general x4 -> x0, matrix products: 6.24 us -> none  [the longest x2 4.05 us: fused_device(): lax.dot_general(cond_rows, d_mod_all[:, l], (((0,), (0,)), ((), ())), pre...]
  transfers between devices with their start and end apart: 1 -> 0, of which waited for: 0 -> 0; matrix products, arithmetic and copies ran while one was open for 9% -> 0% of each run, Pallas kernels for 0% -> 0%
where the time goes in v4:
time: 360 us
  Pallas kernels  356 us (99%)
    pallas_call x1, Pallas kernels, backward(): pl.pallas_call(functools.partial(backward_kernel, n), out_shape=tuple(out...  179 us
    pallas_call x1, Pallas kernels, forward(): pl.pallas_call(functools.partial(forward_kernel, n), out_shape=outs, in_s...  168 us
    pallas_call x1, Pallas kernels, assemble(): pl.pallas_call(functools.partial(assemble_kernel, n), out_shape=tuple((sd...  9.04 us

profile of v4, /device:TPU:0, one launch (start us, length us, event | category | flops | bytes accessed | tf_op | source)
XLA Modules:
  0.0 359.8 jit_solution(1601901316832661608)
XLA Ops:
  0.6 168.4 %shard_map.228 = (bf16[256,768]{1,0:T(8,128)(2,1)}, f32[2,6,768]{2,1,0:T(8,128)}, f32[8,128]{1,0:T(8,128)}, bf16[2,8,96,576]{3,2,1,0:T(8,128)(2,1)}, bf16[2,2,8,...) custom-call(bf16[256,768]{1,0:T(8,128)(2,1)} %bitcast.6, ...), custom_call_target="tpu_custom_call" | custom-call | tf_op jit(solution)/shard_map/pallas_call | solution.py:680
  169.1 179.0 %shard_map.229 = (f32[256,768]{1,0:T(8,128)}, f32[2,8,8,768]{3,2,1,0:T(8,128)}, f32[2,4,2,768]{3,2,1,0:T(2,128)}, f32[1,768]{1,0:T(1,128)}, bf16[2,4,96,768]{3,2...) custom-call(bf16[256,768]{1,0:T(8,128)(2,1)} %bitcast.5, ...), custom_call_target="tpu_custom_call" | custom-call | tf_op jit(solution)/shard_map/pallas_call | solution.py:1163
  348.1 0.0 copy-start
  348.1 9.0 %shard_map.230 = (f32[1,768]{1,0:T(1,128)}, f32[2,576]{1,0:T(2,128)}, f32[2,192]{1,0:T(2,128)}, f32[2,96]{1,0:T(2,128)}, f32[2,384]{1,0:T(2,128)}, /*index=5*/f3...) custom-call(f32[2,8,8,768]{3,2,1,0:T(8,128)} %get-tuple-element.64.v, ...), custom_call_target="tpu_custom_call" | custom-call | tf_op jit(solution)/shard_map/pallas_call | solution.py:1254
  357.1 1.8 copy.28
  358.9 0.0 copy-done
  358.9 0.9 copy.29
Async XLA Ops:
  348.1 10.8 %copy-start = (f32[256,768]{1,0:T(8,128)S(1)}, f32[256,768]{1,0:T(8,128)}, u32[]{:S(2)}) copy-start(f32[256,768]{1,0:T(8,128)} %get-tuple-element.63) | copy-start | bytes 2359300

commit v5 on v4

--- a/solution.py
+++ b/solution.py
@@ -245,7 +245,8 @@
 
 MESH = pl.DeviceIdType.MESH
 FAST = 2
-VMEM_LIMIT = 66_000_000
+VMEM_LIMIT = 67_043_328
+EXP2_SCALE = SCORE_SCALE * 1.4426950408889634
 
 
 def rcopy(src, dst, send, recv, device):
@@ -273,11 +274,12 @@
 def forward_kernel(n, *refs):
     (x_ref, cond_ref, ada_ref, adab_ref, qkvw_ref, qvb_ref, outw_ref, outb_ref, upw_ref, upb_ref,
      downw_ref, downb_ref,
-     out_ref, mod_ref, rows_ref, wq_ref, wo_ref, wu_ref, wd_ref, xs_ref, attn_ref, qh_ref, tok_ref, branch_ref,
-     mid_ref, mlp_ref, up_ref, feed_ref,
-     osend, psend, precv, xpart, xsend, xrecv, own_feed,
-     sq_ref, so_ref, su_ref, bq_ref, bo_ref, bu_ref, bd_ref, cblock, crecv, bsend, brecv, msend, mrecv,
-     c_s, c_r, b_s, b_r, m_s, m_r, w_s, w_r, z_s, z_r, y_s, y_r, a_s, a_r, t_s, t_r, g_s, g_r, r_s, r_r) = refs
+     out_ref, mod_ref, rows_ref), refs = refs[:15], refs[15:]
+    stored, held, refs = refs[:13], refs[13:26], refs[26:]
+    wq_ref, wo_ref, wu_ref, wd_ref, xs_ref, attn_ref, qh_ref, tok_ref, branch_ref, mid_ref, mlp_ref, up_ref, feed_ref = held
+    (osend, psend, precv, chip_sum, xsend, xrecv, xin,
+     sq_ref, so_ref, su_ref, bq_ref, bo_ref, bu_ref, bd_ref, cblock, crecv, bsend, brecv, msend, mrecv, mgath,
+     c_s, c_r, b_s, b_r, m_s, m_r, w_s, w_r, z_s, z_r, y_s, y_r, a_s, a_r, t_s, t_r, g_s, g_r, r_s, r_r, e_s, e_r, n_s, n_r, q_s, q_r, o_s) = refs
     f = lax.axis_index("fsdp")
     s = lax.axis_index("seq")
     slow = n // FAST
@@ -298,10 +300,29 @@
             return wo_ref.at[l, core, at]
         return (wq_ref, None, wu_ref, wd_ref)[p].at[l, at]
 
-    entry_barrier(
-        [{"fsdp": (f + k) % n} for k in range(1, n)] + [{"seq": across}, {"seq": diagonal}, {"seq": partner}]
-    )
-
+    peers = [{"fsdp": (f + k) % n} for k in range(1, n)] + [{"seq": across}, {"seq": diagonal}, {"seq": partner}]
+    barrier = pltpu.get_barrier_semaphore()
+    for device in peers:
+        pl.semaphore_signal(barrier, inc=1, device_id=device, device_id_type=MESH)
+
+    def cut_qkv(l, i):
+        sq_ref[l] = jnp.concatenate(
+            [qkvw_ref[l, :, j * width + i * hc: j * width + (i + 1) * hc] for j in range(3)], axis=1
+        )
+
+    def cut_rest(l, i):
+        so_ref[l] = outw_ref[l, :, (i % 2) * (width // 2): (i % 2 + 1) * (width // 2)]
+        su_ref[l] = jnp.concatenate(
+            [upw_ref[l, :, (4 * j + i) * fc: (4 * j + i + 1) * fc] for j in range(n)], axis=1
+        )
+
+    def by_member(work):
+        for i in range(4):
+            @pl.when(s == i)
+            def _():
+                work(i)
+
+    by_member(lambda i: cut_qkv(0, i))
     cond = cond_ref[...].astype(F32)
     act = cond / (1.0 + jnp.exp(-cond))
     act = act.astype(BF16).astype(F32)
@@ -309,9 +330,6 @@
     for i in range(n):
         cblock[i, 0:1, :rows] = act[:, i * rows: (i + 1) * rows]
     crecv[f] = cblock[f]
-    for k in range(1, n):
-        to = (f + k) % n
-        rcopy(cblock.at[to], crecv.at[f], c_s.at[k], c_r.at[k], {"fsdp": to}).start()
     for l in range(layers):
         bsend[l: l + 1, :] = jnp.concatenate(
             [r[l: l + 1, :].astype(F32) for r in (adab_ref, outb_ref, downb_ref)], axis=1
@@ -320,23 +338,17 @@
             [r[l: l + 1, :].astype(F32) for r in (qvb_ref, upb_ref)], axis=1
         )
     brecv[f] = bsend[...]
+    tokens_over = rcopy(x_ref, xin, n_s.at[0], n_r.at[0], {"seq": across})
 
     def shard(l, p):
         if p == 3:
             return downw_ref.at[l, pl.ds(pl.multiple_of(s * chunk, chunk), chunk)]
         return (sq_ref, so_ref, su_ref)[p].at[l]
 
-    for i in range(4):
-        @pl.when(s == i)
-        def _():
-            for l in range(layers):
-                sq_ref[l] = jnp.concatenate(
-                    [qkvw_ref[l, :, j * width + i * hc: j * width + (i + 1) * hc] for j in range(3)], axis=1
-                )
-                so_ref[l] = outw_ref[l, :, (i % 2) * (width // 2): (i % 2 + 1) * (width // 2)]
-                su_ref[l] = jnp.concatenate(
-                    [upw_ref[l, :, (4 * j + i) * fc: (4 * j + i + 1) * fc] for j in range(n)], axis=1
-                )
+    pl.semaphore_wait(barrier, len(peers))
+    for k in range(1, n):
+        to = (f + k) % n
+        rcopy(cblock.at[to], crecv.at[f], c_s.at[k], c_r.at[k], {"fsdp": to}).start()
 
     def z_copy(l, p, k, to):
         return rcopy(shard(l, p), place(l, p, f), z_s.at[l, p, k], z_r.at[l, p, k], {"fsdp": to})
@@ -352,10 +364,12 @@
             z_copy(l, p, k, ((a + k) % slow) * FAST + b).start()
 
     launch(0, 0)
+    tokens_over.start()
     for k in range(1, n):
         to = (f + k) % n
         rcopy(bsend, brecv.at[f], b_s.at[k], b_r.at[k], {"fsdp": to}).start()
 
+    by_member(lambda i: cut_rest(0, i))
     for k in range(1, n):
         at = (f - k + n) % n
         rcopy(cblock.at[at], crecv.at[at], c_s.at[k], c_r.at[k], {"fsdp": at}).wait_recv()
@@ -363,17 +377,21 @@
     rows_ref[...] = cond_rows
     cond_rows = cond_rows[:, :rows].astype(BF16)
     for l in range(layers):
-        part = mm(cond_rows, ada_ref[l])
+        quarter = msend.shape[2]
+        part = mm(cond_rows, ada_ref[l, :, pl.ds(pl.multiple_of(s * quarter, quarter), quarter)])
         for i in range(n):
             msend[i, l: l + 1, :] = part[i: i + 1, :]
     mrecv[f] = msend[f]
     for k in range(1, n):
         to = (f + k) % n
         rcopy(msend.at[to], mrecv.at[f], m_s.at[k], m_r.at[k], {"fsdp": to}).start()
-    for l in range(layers):
+    for p in range(1, 4):
+        launch(0, p)
+    for l in range(1, layers):
+        by_member(lambda i: cut_qkv(l, i))
+        by_member(lambda i: cut_rest(l, i))
         for p in range(4):
-            if l + p > 0:
-                launch(l, p)
+            launch(l, p)
 
     def forward_weights(l, p):
         for k in range(1, slow):
@@ -386,7 +404,6 @@
             at = ((a - k + slow) % slow) * FAST + 1 - b
             rcopy(shard(l, p), place(l, p, at), y_s.at[l, p, k], y_r.at[l, p, k], y_dev).wait_recv()
 
-    xs_ref[0] = x_ref[...].astype(F32)
     for k in range(1, n):
         at = (f - k + n) % n
         rcopy(bsend, brecv.at[at], b_s.at[k], b_r.at[k], {"fsdp": at}).wait_recv()
@@ -408,14 +425,32 @@
     for k in range(1, n):
         at = (f - k + n) % n
         rcopy(msend.at[at], mrecv.at[at], m_s.at[k], m_r.at[k], {"fsdp": at}).wait_recv()
-    mod = jnp.sum(mrecv[...], axis=0)
-    for l in range(layers):
-        full = mod[l: l + 1] + jnp.concatenate([brecv[i, l: l + 1, :ac] for i in range(n)], axis=1)
+    mgath[s] = jnp.sum(mrecv[...], axis=0)
+    for j in range(3):
+        rcopy(mgath.at[s], mgath.at[s], q_s.at[j], q_r.at[j], {"seq": relative(s, j)}).start()
+    for j in range(3):
+        ref = mgath.at[relative(s, j)]
+        rcopy(ref, ref, q_s.at[j], q_r.at[j], {"seq": relative(s, j)}).wait_recv()
+    for l in range(layers):
+        full = jnp.concatenate([mgath[i, l: l + 1, :] for i in range(4)], axis=1) + jnp.concatenate([brecv[i, l: l + 1, :ac] for i in range(n)], axis=1)
         for r in range(6):
             mod_ref[l, r: r + 1, :] = full[:, r * width: (r + 1) * width]
     for l in range(layers):
         for p in range(4):
             place(l, p, f)[...] = shard(l, p)[...]
+
+    core, side = s % 2, s // 2
+    xs_ref[0, side] = x_ref[...].astype(F32)
+    tokens_over.wait_recv()
+    xs_ref[0, 1 - side] = xin[...].astype(F32)
+
+    def save(l, *members):
+        for i in members:
+            save_copy(l, i).start()
+
+    def save_copy(l, i):
+        src = held[i].at[l, side] if i in (7, 8) else held[i].at[l]
+        return pltpu.make_async_copy(src, stored[i].at[l], o_s.at[l, i])
 
     def matrix(ref, l):
         return ref[l].reshape(n * rows, ref.shape[3])
@@ -428,122 +463,142 @@
         ref = wo_ref.at[l, 1 - core]
         rcopy(ref, ref, w_s.at[l], w_r.at[l], {"seq": partner}).wait_recv()
 
-    def gather(buf, l, send, recv, visit):
-        mine = buf.at[l, s]
-        to_partner = rcopy(mine, mine, send.at[0], recv.at[0], {"seq": partner})
-        to_across = rcopy(mine, mine, send.at[1], recv.at[1], {"seq": across})
-        to_across.start()
-        to_partner.start()
-        theirs = buf.at[l, across]
-        relay = rcopy(theirs, theirs, send.at[2], recv.at[2], {"seq": partner})
-
-        def step(i, carry):
-            @pl.when(i == 1)
-            def _():
-                ref = buf.at[l, partner]
-                rcopy(ref, ref, send.at[0], recv.at[0], {"seq": partner}).wait_recv()
-
-            @pl.when(i == 2)
-            def _():
-                rcopy(theirs, theirs, send.at[1], recv.at[1], {"seq": across}).wait_recv()
-                relay.start()
-
-            @pl.when(i == 3)
-            def _():
-                ref = buf.at[l, diagonal]
-                rcopy(ref, ref, send.at[2], recv.at[2], {"seq": partner}).wait_recv()
-
-            visit(i, relative(s, pick(i)))
-            return carry
-
-        lax.fori_loop(0, 4, step, 0)
-        for copy in (to_partner, to_across, relay):
-            copy.wait_send()
-
-    def pick(i):
-        return (3 - i) * (1 - i // 2) + (i - 2) * (i // 2)
+    def share(buf, l, i, send, recv):
+        ref = buf.at[l, 2 * i + core]
+        return rcopy(ref, ref, send.at[i], recv.at[i], {"seq": partner})
+
+    def shared(buf, l, i, send, recv):
+        ref = buf.at[l, 2 * i + 1 - core]
+        rcopy(ref, ref, send.at[i], recv.at[i], {"seq": partner}).wait_recv()
+
+    def part_copy(i):
+        return rcopy(psend.at[i], precv.at[i], r_s.at[i], r_r.at[i], {"seq": partner})
+
+    def over(i):
+        return rcopy(xsend.at[i], xrecv.at[i], e_s.at[i], e_r.at[i], {"seq": across})
+
+    def out_copy(l, j, i, t):
+        return rcopy(osend.at[t], tok_ref.at[l, i, s], t_s.at[j, i], t_r.at[j, i], {"seq": relative(s, j)})
 
     def layer(l, carry):
         row = lambda i: mod_ref[l, i: i + 1, :]
-        x = xs_ref[l]
-        normed, _ = normalize(x)
-        attn_ref[l, s] = (normed * (1.0 + row(1)) + row(0)).astype(BF16)
-
-        @pl.when(l == 0)
-        def _():
-            forward_weights(0, 0)
-
-        def qkv_block(i, t):
-            @pl.when(i == 0)
-            def _():
-                ready(l, 0)
-
+
+        def qkv_block(t):
             val = (mm(attn_ref[l, t], matrix(wq_ref, l)) + bq_ref[l]).astype(BF16)
             for h in range(3 * heads):
                 qh_ref[l, h, pl.ds(pl.multiple_of(t * block, block), block), :] = (
                     val[:, h * HEAD_DIM: (h + 1) * HEAD_DIM]
                 )
 
-        gather(attn_ref, l, a_s, a_r, qkv_block)
-
-        @pl.when(l == 0)
-        def _():
-            forward_weights(0, 1)
+        def enter(i, carry):
+            @pl.when(l > 0)
+            def _():
+                over(i).wait_recv()
+                feed = chip_sum[i] + xrecv[i].astype(F32) + bd_ref[l - 1]
+                xs_ref[l, i] = mid_ref[l - 1, i] + mod_ref[l - 1, 5:6, :] * feed
+
+                @pl.when(i == side)
+                def _():
+                    feed_ref[l - 1] = feed
+
+                over(i).wait_send()
+
+            normed, _ = normalize(xs_ref[l, i])
+            attn_ref[l, 2 * i + core] = (normed * (1.0 + row(1)) + row(0)).astype(BF16)
+            share(attn_ref, l, i, a_s, a_r).start()
+
+            @pl.when((l == 0) & (i == 0))
+            def _():
+                forward_weights(0, 0)
+
+            @pl.when(i == 0)
+            def _():
+                ready(l, 0)
+
+            def both(w, carry):
+                @pl.when(w == 1)
+                def _():
+                    shared(attn_ref, l, i, a_s, a_r)
+
+                qkv_block(2 * i + (core + w) % 2)
+                return carry
+
+            lax.fori_loop(0, 2, both, 0)
+            return carry
+
+        lax.fori_loop(0, 2, enter, 0)
 
         @pl.when(l > 0)
         def _():
+            save(l - 1, 12)
             forward_weights(l, 2)
 
-        def attend_block(j, carry):
-            t = relative(s, j)
+        def attend_block(t, carry):
             outs = []
             for h in range(heads):
                 q = qh_ref[l, h, pl.ds(pl.multiple_of(t * block, block), block), :]
-                scores = mm_nt(q, qh_ref[l, heads + h]) * SCORE_SCALE
-                e = jnp.exp(scores)
+                e = jnp.exp2(mm_nt(q, qh_ref[l, heads + h]) * EXP2_SCALE)
                 inverse = 1.0 / jnp.sum(e, axis=-1, keepdims=True)
                 prob = (e * inverse).astype(BF16)
                 outs.append(mm(prob, qh_ref[l, 2 * heads + h]))
-            osend[j] = jnp.concatenate(outs, axis=1).astype(BF16)
-
-            @pl.when(j < 3)
-            def _():
-                rcopy(osend.at[j], tok_ref.at[l, s], t_s.at[j], t_r.at[j], {"seq": t}).start()
-
-            @pl.when((j == 1) & (l == 0))
+            val = jnp.concatenate(outs, axis=1).astype(BF16)
+            osend[t] = val
+            i = t // 2
+
+            @pl.when(t % 2 == core)
+            def _():
+                tok_ref[l, i, s] = val
+                out_copy(l, 0, i, t).start()
+
+            @pl.when(t % 2 != core)
+            def _():
+                out_copy(l, 1, i, t).start()
+                out_copy(l, 2, i, t).start()
+
+            @pl.when((t == 2) & (l == 0))
+            def _():
+                forward_weights(0, 1)
+
+            return carry
+
+        lax.fori_loop(0, 4, attend_block, 0)
+        save(l, 0, 4, 5, 6)
+        ready(l, 1)
+        half_copy(l).start()
+
+        @pl.when(l > 0)
+        def _():
+            forward_weights(l, 3)
+
+        half_arrived(l)
+
+        def exchange(i):
+            part_copy(i).wait_recv()
+            chip_sum[i] = chip_sum[i] + precv[i]
+
+            @pl.when((l + 1 < layers) | (i != side))
+            def _():
+                xsend[i] = chip_sum[i].astype(BF16)
+                over(i).start()
+
+        def mlp(i, carry):
+            for j in range(3):
+                ref = tok_ref.at[l, i, relative(s, j)]
+                rcopy(ref, ref, t_s.at[j, i], t_r.at[j, i], {"seq": relative(s, j)}).wait_recv()
+            tokens_out = jnp.concatenate([tok_ref[l, i, t] for t in range(4)], axis=1)
+            branch = jnp.concatenate(
+                [mm(tokens_out, wo_ref[l, c].reshape(n * rows, width // 2)) for c in range(2)], axis=1
+            ) + bo_ref[l]
+            branch_ref[l, i] = branch
+            middle = xs_ref[l, i] + row(2) * branch
+            mid_ref[l, i] = middle
+            normed, _ = normalize(middle)
+            mlp_ref[l, 2 * i + core] = (normed * (1.0 + row(4)) + row(3)).astype(BF16)
+            share(mlp_ref, l, i, g_s, g_r).start()
+
+            @pl.when((i == 0) & (l == 0))
             def _():
                 forward_weights(0, 2)
-
-            @pl.when((j == 1) & (l > 0))
-            def _():
-                forward_weights(l, 3)
-
-            @pl.when(j == 2)
-            def _():
-                ready(l, 1)
-                half_copy(l).start()
-
-            return carry
-
-        lax.fori_loop(0, 4, attend_block, 0)
-        tok_ref[l, s] = osend[3]
-        for j in range(3):
-            t = relative(s, j)
-            rcopy(osend.at[j], tok_ref.at[l, t], t_s.at[j], t_r.at[j], {"seq": t}).wait_recv()
-        tokens_out = jnp.concatenate([tok_ref[l, t] for t in range(4)], axis=1)
-        half_arrived(l)
-        branch = jnp.concatenate(
-            [mm(tokens_out, wo_ref[l, c].reshape(n * rows, width // 2)) for c in range(2)], axis=1
-        ) + bo_ref[l]
-        branch_ref[l] = branch
-        middle = xs_ref[l] + row(2) * branch
-        mid_ref[l] = middle
-        normed, _ = normalize(middle)
-        mlp_ref[l, s] = (normed * (1.0 + row(4)) + row(3)).astype(BF16)
-
-        def mlp_block(i, t):
-            @pl.when((i == 0) & (l == 0))
-            def _():
                 forward_weights(0, 3)
 
             @pl.when(i == 0)
@@ -551,67 +606,67 @@
                 ready(l, 2)
                 ready(l, 3)
 
-            up = mm(mlp_ref[l, t], matrix(wu_ref, l)) + bu_ref[l]
-            up_ref[l, t] = up
-            act = gelu_parts(up)[0].astype(BF16)
-            part = mm(act, matrix(wd_ref, l))
-
-            @pl.when(i == 0)
-            def _():
-                own_feed[...] = part
-
-            @pl.when(i == 1)
-            def _():
-                psend[0] = part
-                rcopy(psend.at[0], precv.at[0], r_s.at[0], r_r.at[0], {"seq": partner}).start()
-
-            @pl.when(i == 2)
-            def _():
-                xpart[...] = part
-
-            @pl.when(i == 3)
-            def _():
-                psend[1] = part
-                rcopy(psend.at[1], precv.at[1], r_s.at[1], r_r.at[1], {"seq": partner}).start()
-
-            @pl.when((i == 2) & (l + 1 < layers))
-            def _():
-                forward_weights(1, 0)
-
-        gather(mlp_ref, l, g_s, g_r, mlp_block)
-        rcopy(psend.at[1], precv.at[1], r_s.at[1], r_r.at[1], {"seq": partner}).wait_recv()
-        xsend[...] = (xpart[...] + precv[1]).astype(BF16)
-        over = rcopy(xsend, xrecv, r_s.at[2], r_r.at[2], {"seq": across})
-        over.start()
+            def both(w, carry):
+                @pl.when(w == 1)
+                def _():
+                    shared(mlp_ref, l, i, g_s, g_r)
+
+                t = 2 * i + (core + w) % 2
+                up = mm(mlp_ref[l, t], matrix(wu_ref, l)) + bu_ref[l]
+                up_ref[l, t] = up
+                act = gelu_parts(up)[0].astype(BF16)
+                part = mm(act, matrix(wd_ref, l))
+
+                @pl.when(w == 0)
+                def _():
+                    chip_sum[i] = part
+
+                @pl.when(w == 1)
+                def _():
+                    psend[i] = part
+                    part_copy(i).start()
+
+                @pl.when((w == 0) & (i == 1))
+                def _():
+                    exchange(0)
+
+                return carry
+
+            lax.fori_loop(0, 2, both, 0)
+            return carry
+
+        lax.fori_loop(0, 2, mlp, 0)
+        exchange(1)
+        save(l, 1, 2, 3, 7, 8, 9, 10, 11)
 
         @pl.when(l + 1 < layers)
         def _():
+            forward_weights(1, 0)
             forward_weights(1, 1)
 
-        rcopy(psend.at[0], precv.at[0], r_s.at[0], r_r.at[0], {"seq": partner}).wait_recv()
-        own_feed[...] = own_feed[...] + precv[0] + bd_ref[l]
-        over.wait_recv()
-        feed = own_feed[...] + xrecv[...].astype(F32)
-        feed_ref[l] = feed
-        nxt = mid_ref[l] + row(5) * feed
-
-        @pl.when(l + 1 < layers)
-        def _():
-            xs_ref[1] = nxt
-
-        @pl.when(l + 1 == layers)
-        def _():
-            out_ref[...] = nxt.astype(BF16)
-
-        over.wait_send()
         half_copy(l).wait_send()
         for i in range(2):
-            rcopy(psend.at[i], precv.at[i], r_s.at[i], r_r.at[i], {"seq": partner}).wait_send()
-        for j in range(3):
-            rcopy(osend.at[j], tok_ref.at[l, s], t_s.at[j], t_r.at[j], {"seq": relative(s, j)}).wait_send()
+            share(attn_ref, l, i, a_s, a_r).wait_send()
+            share(mlp_ref, l, i, g_s, g_r).wait_send()
+            part_copy(i).wait_send()
+            for j in range(3):
+                out_copy(l, j, i, 2 * i).wait_send()
         return carry
 
     lax.fori_loop(0, layers, layer, 0)
+    last = layers - 1
+    over(side).wait_recv()
+    feed = chip_sum[side] + xrecv[side].astype(F32) + bd_ref[last]
+    feed_ref[last] = feed
+    save(last, 12)
+    out_ref[...] = (mid_ref[last, side] + mod_ref[last, 5:6, :] * feed).astype(BF16)
+    over(1 - side).wait_send()
+    tokens_over.wait_send()
+    for j in range(3):
+        rcopy(mgath.at[s], mgath.at[s], q_s.at[j], q_r.at[j], {"seq": relative(s, j)}).wait_send()
+    for l in range(layers):
+        for i in range(13):
+            save_copy(l, i).wait()
     for l in range(layers):
         for p in range(4):
             y_copy(l, p, 0).wait_send()
@@ -643,26 +698,29 @@
         sds((layers, 2, n, rows, width // 2), BF16),
         sds((layers, n, rows, uc), BF16),
         sds((layers, n, rows, width), BF16),
-        sds((layers, block, width), F32),
+        sds((layers, 2, block, width), F32),
         sds((layers, 4, block, width), BF16),
         sds((layers, nh, total, HEAD_DIM), BF16),
         sds((layers, 4, block, hc), BF16),
         sds((layers, block, width), F32),
-        sds((layers, block, width), F32),
+        sds((layers, 2, block, width), F32),
         sds((layers, 4, block, width), BF16),
         sds((layers, 4, block, uc), F32),
         sds((layers, block, width), F32),
     )
     slow = n // FAST
     dma = pltpu.SemaphoreType.DMA
-    scratch = [
+    kept = [list(x.shape) for x in outs[3:]]
+    for i in (7, 8):
+        kept[i].insert(1, 2)
+    scratch = [pltpu.VMEM(tuple(shape), x.dtype) for shape, x in zip(kept, outs[3:])] + [
         pltpu.VMEM((4, block, hc), BF16),
         pltpu.VMEM((2, block, width), F32),
         pltpu.VMEM((2, block, width), F32),
-        pltpu.VMEM((block, width), F32),
+        pltpu.VMEM((2, block, width), F32),
+        pltpu.VMEM((2, block, width), BF16),
+        pltpu.VMEM((2, block, width), BF16),
         pltpu.VMEM((block, width), BF16),
-        pltpu.VMEM((block, width), BF16),
-        pltpu.VMEM((block, width), F32),
         pltpu.VMEM((layers, rows, qc), BF16),
         pltpu.VMEM((layers, rows, width // 2), BF16),
         pltpu.VMEM((layers, rows, uc), BF16),
@@ -674,14 +732,15 @@
         pltpu.VMEM((n, 8, lanes), F32),
         pltpu.VMEM((2 * layers, width), F32),
         pltpu.VMEM((n, 2 * layers, width), F32),
-        pltpu.VMEM((n, layers, width6), F32),
-        pltpu.VMEM((n, layers, width6), F32),
-    ] + [dma((n,))] * 6 + [dma((layers,))] * 2 + [dma((layers, 4, slow))] * 4 + [dma((3,))] * 8
+        pltpu.VMEM((n, layers, width6 // 4), F32),
+        pltpu.VMEM((n, layers, width6 // 4), F32),
+        pltpu.VMEM((4, layers, width6 // 4), F32),
+    ] + [dma((n,))] * 6 + [dma((layers,))] * 2 + [dma((layers, 4, slow))] * 4 + [dma((2,))] * 2 + [dma((3, 2))] * 2 + [dma((2,))] * 6 + [dma((1,))] * 2 + [dma((3,))] * 2 + [dma((layers, 13))]
     return pl.pallas_call(
         functools.partial(forward_kernel, n),
         out_shape=outs,
         in_specs=vmem_specs(12),
-        out_specs=tuple(vmem_specs(len(outs))),
+        out_specs=tuple(vmem_specs(3) + [pl.BlockSpec(memory_space=pl.ANY)] * 13),
         scratch_shapes=scratch,
         compiler_params=pltpu.CompilerParams(
             collective_id=1, has_side_effects=True, vmem_limit_bytes=VMEM_LIMIT
@@ -694,16 +753,18 @@
     stored, rest = rest[:13], rest[13:]
     (g_ref, vec_all, cat_all, gcond_ref), rest = rest[:4], rest[4:]
     fin, rest = rest[:4], rest[4:]
-    loaded, rest = rest[:13], rest[13:]
+    loaded, rest = list(rest[:11]), rest[11:]
+    loaded.insert(5, loaded[8])
+    loaded.insert(8, loaded[11])
     grads, rest = rest[:4], rest[4:]
     y_in, rest = rest[:4], rest[4:]
     z_out, rest = rest[:4], rest[4:]
     z_in, rest = rest[:4], rest[4:]
     kept, rest = rest[:4], rest[4:]
-    (gf_ref, act_ref, gup_ref, gosend, go_ref, goh_ref, gqh_ref, gqkv_ref, psend, precv, xpart, xsend, xrecv,
-     own_part, gmid_ref, osend, orecv,
-     vec_ref, cat_ref, vec_in, vec_sum, cat_in, gc_send, gc_recv, v_s, v_r, u_s, u_r, k_s, k_r, h_s, h_r, i_s, i_r, dk_acc, dv_acc,
-     l_s, o_s, o_r, y_s, y_r, z_s, z_r, f_s, f_r, g_s, g_r, t_s, t_r, r_s, r_r) = rest
+    (gf_ref, gb_ref, act_ref, gup_ref, gqkv_ref, psend, precv, chip_sum, xsend, xrecv,
+     gx_ref, gmid_ref, dk_acc, dv_acc, orecv,
+     vec_ref, cat_ref, vec_in, vec_sum, cat_in, gc_send, gc_recv, v_s, v_r, u_s, u_r, k_s, k_r, h_s, h_r, i_s, i_r,
+     l_s, o_s, o_r, y_s, y_r, z_s, z_r, f_s, f_r, g_s, g_r, t_s, t_r, r_s, r_r, e_s, e_r, n_s, n_r, ada_s) = rest
     wq, wo, wu, wd, xs, attn, qh, tok, branch, mid, mlp, up, feed = range(13)
     down, upw, outw, qkvw = range(4)
     f = lax.axis_index("fsdp")
@@ -713,7 +774,9 @@
     layers = mod_ref.shape[0]
     block, width = cot_ref.shape
     rows = width // n
-    hc = gosend.shape[2]
+    hc = gqkv_ref.shape[2] // 3
+    half = width // 2
+    core, side = s % 2, s // 2
     heads = hc // HEAD_DIM
     across, diagonal, partner = relative(s, 0), relative(s, 1), relative(s, 2)
     y_dev = {"fsdp": a * FAST + (1 - b)}
@@ -721,7 +784,7 @@
     def load(i, l):
         return pltpu.make_async_copy(stored[i].at[l], loaded[i], l_s.at[i])
 
-    for i in (feed, wd, up, wu, mlp, mid, branch, wo, tok, qh, wq, attn, xs):
+    for i in (feed, wd, up, wu, mlp, mid, wo, tok, qh, wq, xs):
         load(i, layers - 1).start()
 
     entry_barrier(
@@ -765,46 +828,49 @@
         ref = fin[p].at[l, (partner, across, diagonal)[i]]
         rcopy(ref, ref, f_s.at[l, p, i], f_r.at[l, p, i], {"seq": partner}).wait_recv()
 
+    def ada_load(q):
+        l, r = q // 6, q % 6
+        dst = loaded[(wd, wu)[q // n]].at[q % n]
+        return pltpu.make_async_copy(ada_ref.at[l, :, pl.ds(r * width, width)], dst, ada_s.at[q])
+
     def matrix(i):
         return loaded[i][...].reshape(width, loaded[i].shape[2])
 
     def part_copy(i):
-        return rcopy(psend.at[i], precv.at[i], r_s.at[i], r_r.at[i], {"seq": partner})
-
-    over = rcopy(xsend, xrecv, r_s.at[2], r_r.at[2], {"seq": across})
-
-    def place(j, part):
-        @pl.when(j == 3)
-        def _():
-            own_part[...] = part
-
-        @pl.when(j == 2)
+        return rcopy(psend.at[0], precv.at[i], r_s.at[i], r_r.at[i], {"seq": partner})
+
+    def over(kind, i):
+        at = 2 * kind + i
+        return rcopy(xsend.at[i], xrecv.at[at], e_s.at[at], e_r.at[at], {"seq": across})
+
+    def share(buf, i, send, recv):
+        ref = buf.at[2 * i + core]
+        return rcopy(ref, ref, send.at[i], recv.at[i], {"seq": partner})
+
+    def shared(buf, i, send, recv):
+        ref = buf.at[2 * i + 1 - core]
+        rcopy(ref, ref, send.at[i], recv.at[i], {"seq": partner}).wait_recv()
+
+    def place(w, i, part):
+        @pl.when(w == 0)
+        def _():
+            chip_sum[i] = part
+
+        @pl.when(w == 1)
         def _():
             psend[0] = part
-            part_copy(0).start()
-
-        @pl.when(j == 0)
-        def _():
-            xpart[...] = part
-
-        @pl.when(j == 1)
-        def _():
-            psend[1] = part
-            part_copy(1).start()
-
-    def send_across():
-        part_copy(1).wait_recv()
-        xsend[...] = (xpart[...] + precv[1]).astype(BF16)
-        over.start()
-
-    def collect():
-        part_copy(0).wait_recv()
-        own_part[...] = own_part[...] + precv[0]
-        over.wait_recv()
-        own_part[...] = own_part[...] + xrecv[...].astype(F32)
-        over.wait_send()
-        part_copy(0).wait_send()
-        part_copy(1).wait_send()
+            part_copy(i).start()
+
+    def exchange(kind, i, wanted):
+        part_copy(i).wait_recv()
+        chip_sum[i] = chip_sum[i] + precv[i]
+
+        @pl.when(wanted)
+        def _():
+            xsend[i] = chip_sum[i].astype(BF16)
+            over(kind, i).start()
+
+        part_copy(i).wait_send()
 
     def vec_copy(l, j):
         return rcopy(vec_ref.at[l], vec_in.at[l, s], v_s.at[l, j], v_r.at[l, j], {"seq": relative(s, j)})
@@ -835,229 +901,275 @@
     def sums(value):
         return jnp.sum(value, axis=0, keepdims=True)
 
+    def leave(l, i):
+        g_ain = chip_sum[i] + xrecv[2 + i].astype(F32)
+        normed, inverse = normalize(loaded[xs][i])
+
+        @pl.when(i == side)
+        def _():
+            vec_ref[l, 1:2, :] = sums(g_ain * normed)
+            vec_ref[l, 0:1, :] = sums(g_ain)
+
+        return gmid_ref[i] + norm_back(g_ain * (1.0 + mod_ref[l, 1:2, :]), normed, inverse)
+
+    cot_over = rcopy(cot_ref, xrecv.at[2 + side], n_s.at[0], n_r.at[0], {"seq": across})
+    cot_over.start()
+    gx_ref[side] = cot_ref[...].astype(F32)
+
     def layer(step, carry):
         l = layers - 1 - step
         row = lambda i: mod_ref[l, i: i + 1, :]
-
-        @pl.when(step == 0)
-        def _():
-            g_ref[...] = cot_ref[...].astype(F32)
-
-        load(feed, l).wait()
-        g = g_ref[...]
-        g_feed = (row(5) * g).astype(BF16)
-        gf_ref[s] = g_feed
-        mine, theirs = gf_ref.at[s], gf_ref.at[across]
-        to_partner = rcopy(mine, mine, g_s.at[0], g_r.at[0], {"seq": partner})
-        to_across = rcopy(mine, mine, g_s.at[1], g_r.at[1], {"seq": across})
-        relay = rcopy(theirs, theirs, g_s.at[2], g_r.at[2], {"seq": partner})
-        to_across.start()
-        to_partner.start()
-        vec_ref[l, 5:6, :] = sums(g * loaded[feed][...])
-        vec_ref[l, 7:8, :] = sums(g_feed.astype(F32))
         cat_ref[l] = jnp.zeros_like(cat_ref[l])
-        for i in (wd, up, wu, mlp):
+        for i in (feed, wd, up, wu, mlp):
             load(i, l).wait()
 
-        def mlp_block(i, carry):
-            @pl.when(i == 1)
-            def _():
-                ref = gf_ref.at[partner]
-                rcopy(ref, ref, g_s.at[0], g_r.at[0], {"seq": partner}).wait_recv()
-
-            @pl.when(i == 2)
-            def _():
-                rcopy(theirs, theirs, g_s.at[1], g_r.at[1], {"seq": across}).wait_recv()
-                relay.start()
-
-            @pl.when(i == 3)
-            def _():
-                ref = gf_ref.at[diagonal]
-                rcopy(ref, ref, g_s.at[2], g_r.at[2], {"seq": partner}).wait_recv()
-
-            j = (3 - i) * (1 - i // 2) + (i - 2) * (i // 2)
-            t = relative(s, j)
-            value, slope = gelu_parts(loaded[up][t])
-            act_ref[t] = value.astype(BF16)
-            g_up = (mm_nt(gf_ref[t], matrix(wd)) * slope).astype(BF16)
-            gup_ref[t] = g_up
-            cat_ref[l, 0:1, :] = cat_ref[l, 0:1, :] + sums(g_up.astype(F32))
-            place(j, mm_nt(g_up, matrix(wu)))
+        @pl.when(step > 0)
+        def _():
+            load(xs, l + 1).wait()
+
+        def enter(turn, carry):
+            i = (turn + side * (1 - (step + layers - 1) // layers)) % 2
+
+            @pl.when((step == 0) & (turn == 1))
+            def _():
+                theirs = xrecv.at[3 - side]
+                rcopy(cot_ref, theirs, n_s.at[0], n_r.at[0], {"seq": across}).wait_recv()
+                gx_ref[1 - side] = theirs[...].astype(F32)
+
+            @pl.when(step > 0)
+            def _():
+                over(1, i).wait_recv()
+                over(1, i).wait_send()
+                gx_ref[i] = leave(l + 1, i)
+
+            g = gx_ref[i]
+            g_feed = (row(5) * g).astype(BF16)
+            gf_ref[2 * i + core] = g_feed
+            share(gf_ref, i, g_s, g_r).start()
+
+            @pl.when(i == side)
+            def _():
+                vec_ref[l, 5:6, :] = sums(g * loaded[feed][...])
+                vec_ref[l, 7:8, :] = sums(g_feed.astype(F32))
+
+            def both(w, carry):
+                @pl.when(w == 1)
+                def _():
+                    shared(gf_ref, i, g_s, g_r)
+
+                t = 2 * i + (core + w) % 2
+                value, slope = gelu_parts(loaded[up][t])
+                act_ref[pl.ds(pl.multiple_of(t * block, block), block), :] = value.astype(BF16)
+                g_up = (mm_nt(gf_ref[t], matrix(wd)) * slope).astype(BF16)
+                gup_ref[t] = g_up
+                cat_ref[l, 0:1, :] = cat_ref[l, 0:1, :] + sums(g_up.astype(F32))
+                place(w, i, mm_nt(g_up, matrix(wu)))
+                return carry
+
+            lax.fori_loop(0, 2, both, 0)
+            exchange(0, i, l >= 0)
             return carry
 
-        lax.fori_loop(0, 4, mlp_block, 0)
-        for copy in (to_partner, to_across, relay):
-            copy.wait_send()
-        send_across()
+        lax.fori_loop(0, 2, enter, 0)
+
+        load(branch, l).start()
 
         @pl.when(step > 0)
         def _():
-            z_start(l + 1, qkvw)
-            z_finish(l + 1, outw)
+            load(xs, l).start()
+            vec_start(l + 1)
 
         whole = lambda ref: ref[...].reshape(4 * block, ref.shape[2])
-        grads[down][...] = mm_tn(whole(act_ref), whole(gf_ref)).astype(BF16).reshape(grads[down].shape)
+        grads[down][...] = mm_tn(act_ref[...], whole(gf_ref)).astype(BF16).reshape(grads[down].shape)
         y_copy(l, down).start()
         grads[upw][...] = mm_tn(whole(loaded[mlp]), whole(gup_ref)).astype(BF16).reshape(grads[upw].shape)
         y_copy(l, upw).start()
 
+        load(attn, l).start()
+
+        @pl.when(step > 0)
+        def _():
+            z_start(l + 1, outw)
+            z_start(l + 1, qkvw)
+
         @pl.when(l > 0)
         def _():
-            for i in (feed, wd, up, wu, mlp):
+            for i in (wd, up, wu):
                 load(i, l - 1).start()
 
-        load(mid, l).wait()
-        normed, inverse = normalize(loaded[mid][...])
-        for i in (branch, wo, tok):
+        @pl.when(l == 0)
+        def _():
+            for q in range(6 * layers):
+                ada_load(q).start()
+
+        for i in (mid, branch, wo, tok, qh):
             load(i, l).wait()
-        collect()
-        g_min = own_part[...]
-        vec_ref[l, 4:5, :] = sums(g_min * normed)
-        vec_ref[l, 3:4, :] = sums(g_min)
-        g_mid = g_ref[...] + norm_back(g_min * (1.0 + row(4)), normed, inverse)
-        gmid_ref[...] = g_mid
-        g_branch = (row(2) * g_mid).astype(BF16)
-        vec_ref[l, 2:3, :] = sums(g_mid * loaded[branch][...])
-        vec_ref[l, 6:7, :] = sums(g_branch.astype(F32))
-        half = width // 2
-        g_o = sum(
-            mm_nt(g_branch[:, c * half: (c + 1) * half], loaded[wo][c].reshape(width, half)) for c in range(2)
-        ).astype(BF16)
-        for t in range(4):
-            gosend[t] = g_o[:, t * hc: (t + 1) * hc]
-
-        def head_copy(j):
-            t = relative(s, j)
-            return rcopy(gosend.at[t], go_ref.at[s], t_s.at[j], t_r.at[j], {"seq": t})
-
-        for j in range(3):
-            head_copy(j).start()
-        go_ref[s] = gosend[s]
-        tokens_out = jnp.concatenate([loaded[tok][t] for t in range(4)], axis=1)
+        dk_acc[...] = jnp.zeros_like(dk_acc)
+        dv_acc[...] = jnp.zeros_like(dv_acc)
+
+        def pair(c):
+            src = act_ref.at[pl.ds(0, width), pl.ds(c * half, half)]
+            return rcopy(src, orecv.at[l], o_s.at[0], o_r.at[l], {"seq": partner})
+
+        def inner(i, carry):
+            over(0, i).wait_recv()
+            over(0, i).wait_send()
+            g_min = chip_sum[i] + xrecv[i].astype(F32)
+            normed, inverse = normalize(loaded[mid][i])
+            g_mid = gx_ref[i] + norm_back(g_min * (1.0 + row(4)), normed, inverse)
+            gmid_ref[i] = g_mid
+            g_branch = (row(2) * g_mid).astype(BF16)
+            gb_ref[2 * i + core] = g_branch
+            share(gb_ref, i, t_s, t_r).start()
+
+            @pl.when(i == side)
+            def _():
+                vec_ref[l, 4:5, :] = sums(g_min * normed)
+                vec_ref[l, 3:4, :] = sums(g_min)
+                vec_ref[l, 2:3, :] = sums(g_mid * loaded[branch][...])
+                vec_ref[l, 6:7, :] = sums(g_branch.astype(F32))
+
+            @pl.when(i == 1)
+            def _():
+                tokens_out = jnp.concatenate([loaded[tok][t] for t in range(4)], axis=1)
+                for c in range(2):
+                    act_ref[:width, c * half: (c + 1) * half] = mm_tn(
+                        tokens_out, gb_ref[s, :, c * half: (c + 1) * half]
+                    ).astype(BF16)
+                for c in range(2):
+                    @pl.when(core != c)
+                    def _():
+                        pair(c).start()
+
+            def tile(w, carry):
+                @pl.when(w == 1)
+                def _():
+                    shared(gb_ref, i, t_s, t_r)
+
+                t = 2 * i + (core + w) % 2
+                at = pl.ds(pl.multiple_of(t * block, block), block)
+                lines = hc // rows
+                g_o = sum(
+                    mm_nt(
+                        gb_ref[t, :, c * half: (c + 1) * half],
+                        loaded[wo][c, pl.ds(s * lines, lines)].reshape(hc, half),
+                    )
+                    for c in range(2)
+                ).astype(BF16)
+                for h in range(heads):
+                    q = loaded[qh][h, at, :]
+                    k = loaded[qh][heads + h]
+                    g_out = g_o[:, h * HEAD_DIM: (h + 1) * HEAD_DIM]
+                    e = jnp.exp2(mm_nt(k, q) * EXP2_SCALE)
+                    prob = e * (1.0 / jnp.sum(e, axis=0, keepdims=True))
+                    dv_acc[h] = dv_acc[h] + mm(prob.astype(BF16), g_out)
+                    dp = mm_nt(loaded[qh][2 * heads + h], g_out)
+                    inner_sum = jnp.sum(prob * dp, axis=0, keepdims=True)
+                    ds = (prob * (dp - inner_sum)).astype(BF16)
+                    gqkv_ref[t, :, h * HEAD_DIM: (h + 1) * HEAD_DIM] = (mm_tn(ds, k) * SCORE_SCALE).astype(BF16)
+                    dk_acc[h] = dk_acc[h] + mm(ds, q)
+                return carry
+
+            lax.fori_loop(0, 2, tile, 0)
+
+            return carry
+
+        lax.fori_loop(0, 2, inner, 0)
+        pair(0).wait_recv()
         for c in range(2):
-            osend[c] = mm_tn(tokens_out, g_branch[:, c * half: (c + 1) * half]).astype(BF16)
-        pair = rcopy(osend.at[1 - s % 2], orecv.at[l], o_s.at[0], o_r.at[l], {"seq": partner})
-        pair.start()
+            @pl.when(core == c)
+            def _():
+                out_sum = act_ref[:width, c * half: (c + 1) * half].astype(F32) + orecv[l].astype(F32)
+                grads[outw][...] = out_sum.astype(BF16).reshape(grads[outw].shape)
+        y_copy(l, outw).start()
+        pair(0).wait_send()
+
+        @pl.when(step > 0)
+        def _():
+            z_finish(l + 1, down)
+            z_finish(l + 1, upw)
+            z_finish(l + 1, outw)
+
+        z_start(l, down)
+        for h in range(heads):
+            for j, acc, scale in ((1, dk_acc, SCORE_SCALE), (2, dv_acc, 1.0)):
+                lo = (j * heads + h) * HEAD_DIM
+                value = (acc[h] * scale).astype(BF16)
+                for t in range(4):
+                    gqkv_ref[t, :, lo: lo + HEAD_DIM] = value[t * block: (t + 1) * block]
 
         @pl.when(l > 0)
         def _():
-            for i in (mid, branch, wo, tok):
+            for i in (feed, mid, wo, tok, qh):
                 load(i, l - 1).start()
 
-        @pl.when(step > 0)
-        def _():
-            z_finish(l + 1, qkvw)
-            vec_spread(l + 1)
-
-        pair.wait_recv()
-        out_sum = osend[s % 2].astype(F32) + orecv[l].astype(F32)
-        grads[outw][...] = out_sum.astype(BF16).reshape(grads[outw].shape)
-        y_copy(l, outw).start()
-        pair.wait_send()
-        load(qh, l).wait()
-        for j in range(3):
-            t = relative(s, j)
-            rcopy(gosend.at[t], go_ref.at[t], t_s.at[j], t_r.at[j], {"seq": t}).wait_recv()
-        for t in range(4):
-            part = go_ref[t]
-            for h in range(heads):
-                goh_ref[h, t * block: (t + 1) * block, :] = part[:, h * HEAD_DIM: (h + 1) * HEAD_DIM]
-
-        for h in range(heads):
-            dk_acc[...] = jnp.zeros_like(dk_acc)
-            dv_acc[...] = jnp.zeros_like(dv_acc)
-
-            def tile(t, carry):
-                at = pl.ds(pl.multiple_of(t * block, block), block)
-                q = loaded[qh][h, at, :]
-                k = loaded[qh][heads + h]
-                g_out = goh_ref[h, at, :]
-                e = jnp.exp(mm_nt(q, k) * SCORE_SCALE)
-                prob = e * (1.0 / jnp.sum(e, axis=-1, keepdims=True))
-                dv_acc[...] = dv_acc[...] + mm_tn(prob.astype(BF16), g_out)
-                dp = mm_nt(g_out, loaded[qh][2 * heads + h])
-                inner = jnp.sum(prob * dp, axis=-1, keepdims=True)
-                ds = (prob * (dp - inner)).astype(BF16)
-                gqh_ref[h, at, :] = (mm(ds, k) * SCORE_SCALE).astype(BF16)
-                dk_acc[...] = dk_acc[...] + mm_tn(ds, q)
+        load(wq, l).wait()
+
+        def back(i, carry):
+            def both(w, carry):
+                place(1 - w, i, mm_nt(gqkv_ref[2 * i + (core + 1 - w) % 2], matrix(wq)))
                 return carry
 
-            lax.fori_loop(0, 4, tile, 0)
-            gqh_ref[heads + h] = (dk_acc[...] * SCORE_SCALE).astype(BF16)
-            gqh_ref[2 * heads + h] = dv_acc[...].astype(BF16)
-            if h < 2:
-                z_start(l, h)
-
-        for j in range(3):
-            head_copy(j).wait_send()
-
-        @pl.when(l > 0)
-        def _():
-            load(qh, l - 1).start()
-
-        for t in range(4):
-            gqkv_ref[t] = jnp.concatenate(
-                [gqh_ref[i, t * block: (t + 1) * block, :] for i in range(3 * heads)], axis=1
-            )
-        load(wq, l).wait()
-
-        def back_block(i, carry):
-            j = (1 - i) * (1 - i // 2) + i * (i // 2)
-            place(j, mm_nt(gqkv_ref[relative(s, j)], matrix(wq)))
+            lax.fori_loop(0, 2, both, 0)
+            exchange(1, i, (l > 0) | (i != side))
             return carry
 
-        lax.fori_loop(0, 4, back_block, 0)
-        send_across()
+        lax.fori_loop(0, 2, back, 0)
         load(attn, l).wait()
         grads[qkvw][...] = mm_tn(whole(loaded[attn]), whole(gqkv_ref)).astype(BF16).reshape(grads[qkvw].shape)
         y_copy(l, qkvw).start()
         cat_ref[l, 1:2, : 3 * hc] = sums(whole(gqkv_ref).astype(F32))
-        z_start(l, outw)
-        z_finish(l, down)
-        z_finish(l, upw)
-        load(xs, l).wait()
-        normed, inverse = normalize(loaded[xs][...])
 
         @pl.when(l > 0)
         def _():
-            for i in (wq, attn, xs):
+            for i in (wq, mlp):
                 load(i, l - 1).start()
 
-        collect()
-        g_ain = own_part[...]
-        vec_ref[l, 1:2, :] = sums(g_ain * normed)
-        vec_ref[l, 0:1, :] = sums(g_ain)
-        g_ref[...] = gmid_ref[...] + norm_back(g_ain * (1.0 + row(1)), normed, inverse)
-
-        @pl.when(l > 0)
-        def _():
-            vec_start(l)
+        for i in range(2):
+            share(gf_ref, i, g_s, g_r).wait_send()
+            share(gb_ref, i, t_s, t_r).wait_send()
+        z_start(l, upw)
+
+        @pl.when(step > 0)
+        def _():
+            z_finish(l + 1, qkvw)
+            vec_spread(l + 1)
 
         return carry
 
     lax.fori_loop(0, layers, layer, 0)
+    load(xs, 0).wait()
+    z_start(0, outw)
+    over(1, side).wait_recv()
+    g_ref[...] = leave(0, side)
     vec_start(0)
     z_start(0, qkvw)
+    vec_spread(0)
+    over(1, 1 - side).wait_send()
+    cot_over.wait_send()
+    z_finish(0, down)
+    z_finish(0, upw)
     z_finish(0, outw)
-    vec_spread(0)
     for l in range(1, layers):
         for p in (down, upw, outw, qkvw):
             fin_arrived(l, p, 1)
             fin_copy(l, p, 2).start()
-    z_finish(0, qkvw)
     for l in range(layers):
         vec_arrived(l)
         cat_all[l, s] = jnp.sum(cat_in[l], axis=0)
     for j in range(3):
         ref = cat_all.at[:, s]
         rcopy(ref, ref, h_s.at[j], h_r.at[j], {"seq": relative(s, j)}).start()
+    for q in range(6 * layers):
+        ada_load(q).wait()
     g_cond = jnp.zeros((n, rows), F32)
     for l in range(layers):
         for r in range(6):
             d = vec_all[l, :, r, :]
             high = d.astype(BF16)
             low = (d - high.astype(F32)).astype(BF16)
-            w = ada_ref[l, :, r * width: (r + 1) * width]
+            q = 6 * l + r
+            w = loaded[(wd, wu)[q // n]][q % n]
             g_cond = g_cond + mm_nt(high, w) + mm_nt(low, w)
     for i in range(n):
         gc_send[i, 0:1, :rows] = g_cond[i: i + 1, :]
@@ -1069,6 +1181,7 @@
     gc_recv[f] = gc_send[f]
     for k in range(1, n):
         cond_copy(k).start()
+    z_finish(0, qkvw)
     for p in (down, upw, outw, qkvw):
         fin_arrived(0, p, 1)
         fin_copy(0, p, 2).start()
@@ -1117,7 +1230,7 @@
         sds((1, width), F32),
     ] + [sds((layers, 4, rows, c), BF16) for c in columns]
     scratch = (
-        [pltpu.VMEM(x.shape[1:], x.dtype) for x in stored]
+        [pltpu.VMEM(x.shape[1:], x.dtype) for i, x in enumerate(stored) if i not in (5, 8)]
         + [pltpu.VMEM((slow, FAST, rows, c), BF16) for c in columns]
         + [pltpu.VMEM((layers, slow, rows, c), BF16) for c in columns]
         + [pltpu.VMEM((slow, rows, c), BF16) for c in columns]
@@ -1125,21 +1238,19 @@
         + [pltpu.VMEM((rows, c), F32) for c in columns]
         + [
             pltpu.VMEM((4, block, width), BF16),
+            pltpu.VMEM((4, block, width), BF16),
+            pltpu.VMEM((4 * block, uc), BF16),
             pltpu.VMEM((4, block, uc), BF16),
-            pltpu.VMEM((4, block, uc), BF16),
-            pltpu.VMEM((4, block, hc), BF16),
-            pltpu.VMEM((4, block, hc), BF16),
-            pltpu.VMEM((nh // 3, 4 * block, HEAD_DIM), BF16),
-            pltpu.VMEM((nh, 4 * block, HEAD_DIM), BF16),
             pltpu.VMEM((4, block, qc), BF16),
+            pltpu.VMEM((1, block, width), F32),
             pltpu.VMEM((2, block, width), F32),
             pltpu.VMEM((2, block, width), F32),
-            pltpu.VMEM((block, width), F32),
-            pltpu.VMEM((block, width), BF16),
-            pltpu.VMEM((block, width), BF16),
-            pltpu.VMEM((block, width), F32),
-            pltpu.VMEM((block, width), F32),
-            pltpu.VMEM((2, width, width // 2), BF16),
+            pltpu.VMEM((2, block, width), BF16),
+            pltpu.VMEM((4, block, width), BF16),
+            pltpu.VMEM((2, block, width), F32),
+            pltpu.VMEM((2, block, width), F32),
+            pltpu.VMEM((nh // 3, 4 * block, HEAD_DIM), F32),
+            pltpu.VMEM((nh // 3, 4 * block, HEAD_DIM), F32),
             pltpu.VMEM((layers, width, width // 2), BF16),
             pltpu.VMEM((layers, 8, width), F32),
             pltpu.VMEM((layers, 2, uc), F32),
@@ -1151,19 +1262,17 @@
             dma((layers, 3)), dma((layers, 3)),
             dma((layers, n)), dma((layers, n)), dma((layers, n)), dma((layers, n)),
             dma((3,)), dma((3,)), dma((n,)), dma((n,)),
-            pltpu.VMEM((4 * block, HEAD_DIM), F32),
-            pltpu.VMEM((4 * block, HEAD_DIM), F32),
             dma((13,)), dma((1,)), dma((layers,)),
             dma((4,)), dma((layers, 4)),
             dma((4, slow)), dma((layers, 4, slow)),
             dma((layers, 4, 3)), dma((layers, 4, 3)),
         ]
-        + [dma((3,))] * 6
+        + [dma((2,))] * 6 + [dma((4,))] * 2 + [dma((1,))] * 2 + [dma((6 * layers,))]
     )
     return pl.pallas_call(
         functools.partial(backward_kernel, n),
         out_shape=tuple(outs),
-        in_specs=vmem_specs(3) + [pl.BlockSpec(memory_space=pl.ANY)] * 13,
+        in_specs=vmem_specs(2) + [pl.BlockSpec(memory_space=pl.ANY)] * 14,
         out_specs=tuple(vmem_specs(len(outs))),
         scratch_shapes=scratch,
         compiler_params=pltpu.CompilerParams(

time: 360 us -> 327 us (0.908)
  Pallas kernels: 356 us -> 323 us
    pallas_call x1, Pallas kernels: 179 us -> 162 us  [backward(): pl.pallas_call(functools.partial(backward_kernel, n), out_shape=tuple(out...]
    pallas_call x1, Pallas kernels: 168 us -> 152 us  [forward(): pl.pallas_call(functools.partial(forward_kernel, n), out_shape=outs, in_s...]
where the time goes in v5:
time: 327 us
  Pallas kernels  323 us (99%)
  local copies, waits for them, and re-layouts  3.83 us (1%)
    pallas_call x1, Pallas kernels, backward(): pl.pallas_call(functools.partial(backward_kernel, n), out_shape=tuple(out...  162 us
    pallas_call x1, Pallas kernels, forward(): pl.pallas_call(functools.partial(forward_kernel, n), out_shape=outs, in_s...  152 us
    pallas_call x1, Pallas kernels, assemble(): pl.pallas_call(functools.partial(assemble_kernel, n), out_shape=tuple((sd...  8.97 us

profile of v5, /device:TPU:0, one launch (start us, length us, event | category | flops | bytes accessed | tf_op | source)
XLA Modules:
  0.0 327.2 jit_solution(13914107129468289872)
XLA Ops:
  0.6 152.1 %shard_map.228 = (bf16[256,768]{1,0:T(8,128)(2,1)}, f32[2,6,768]{2,1,0:T(8,128)}, f32[8,128]{1,0:T(8,128)}, bf16[2,8,96,576]{3,2,1,0:T(8,128)(2,1)}, bf16[2,2,8,...) custom-call(bf16[256,768]{1,0:T(8,128)(2,1)} %bitcast.6, ...), custom_call_target="tpu_custom_call" | custom-call | tf_op jit(solution)/shard_map/pallas_call | solution.py:739
  152.8 161.6 %shard_map.229 = (f32[256,768]{1,0:T(8,128)}, f32[2,8,8,768]{3,2,1,0:T(8,128)}, f32[2,4,2,768]{3,2,1,0:T(2,128)}, f32[1,768]{1,0:T(1,128)}, bf16[2,4,96,768]{3,2...) custom-call(bf16[256,768]{1,0:T(8,128)(2,1)} %bitcast.5, ...), custom_call_target="tpu_custom_call" | custom-call | tf_op jit(solution)/shard_map/pallas_call | solution.py:1272
  314.4 9.0 %shard_map.230 = (f32[1,768]{1,0:T(1,128)}, f32[2,576]{1,0:T(2,128)}, f32[2,192]{1,0:T(2,128)}, f32[2,96]{1,0:T(2,128)}, f32[2,384]{1,0:T(2,128)}, /*index=5*/f3...) custom-call(f32[2,8,8,768]{3,2,1,0:T(8,128)} %get-tuple-element.64.v, ...), custom_call_target="tpu_custom_call" | custom-call | tf_op jit(solution)/shard_map/pallas_call | solution.py:1363
  323.4 1.8 copy.28
  325.1 2.1 copy.29

commit v6 on v5

--- a/solution.py
+++ b/solution.py
@@ -272,14 +272,23 @@
 
 
 def forward_kernel(n, *refs):
-    (x_ref, cond_ref, ada_ref, adab_ref, qkvw_ref, qvb_ref, outw_ref, outb_ref, upw_ref, upb_ref,
-     downw_ref, downb_ref,
+    (x_ref, cond_ref, ada_in, adab_ref, qkvw_ref, qvb_ref, outw_in, outb_ref, upw_in, upb_ref,
+     downw_in, downb_ref,
      out_ref, mod_ref, rows_ref), refs = refs[:15], refs[15:]
     stored, held, refs = refs[:13], refs[13:26], refs[26:]
     wq_ref, wo_ref, wu_ref, wd_ref, xs_ref, attn_ref, qh_ref, tok_ref, branch_ref, mid_ref, mlp_ref, up_ref, feed_ref = held
     (osend, psend, precv, chip_sum, xsend, xrecv, xin,
      sq_ref, so_ref, su_ref, bq_ref, bo_ref, bu_ref, bd_ref, cblock, crecv, bsend, brecv, msend, mrecv, mgath,
-     c_s, c_r, b_s, b_r, m_s, m_r, w_s, w_r, z_s, z_r, y_s, y_r, a_s, a_r, t_s, t_r, g_s, g_r, r_s, r_r, e_s, e_r, n_s, n_r, q_s, q_r, o_s) = refs
+     c_s, c_r, b_s, b_r, m_s, m_r, w_s, w_r, z_s, z_r, y_s, y_r, a_s, a_r, t_s, t_r, g_s, g_r, r_s, r_r, e_s, e_r, n_s, n_r, q_s, q_r, o_s,
+     upw_ref, outw_ref, ada_ref, downw_ref, i_s) = refs
+    loads = [
+        pltpu.make_async_copy(src, dst, i_s.at[i])
+        for i, (src, dst) in enumerate(
+            ((upw_in, upw_ref), (outw_in, outw_ref), (ada_in, ada_ref), (downw_in, downw_ref))
+        )
+    ]
+    for load in loads:
+        load.start()
     f = lax.axis_index("fsdp")
     s = lax.axis_index("seq")
     slow = n // FAST
@@ -369,7 +378,11 @@
         to = (f + k) % n
         rcopy(bsend, brecv.at[f], b_s.at[k], b_r.at[k], {"fsdp": to}).start()
 
+    loads[0].wait()
+    loads[1].wait()
     by_member(lambda i: cut_rest(0, i))
+    loads[2].wait()
+    loads[3].wait()
     for k in range(1, n):
         at = (f - k + n) % n
         rcopy(cblock.at[at], crecv.at[at], c_s.at[k], c_r.at[k], {"fsdp": at}).wait_recv()
@@ -581,7 +594,10 @@
                 xsend[i] = chip_sum[i].astype(BF16)
                 over(i).start()
 
-        def mlp(i, carry):
+        flip = (1 - side) * ((l + 1) // layers)
+
+        def mlp(turn, carry):
+            i = (turn + flip) % 2
             for j in range(3):
                 ref = tok_ref.at[l, i, relative(s, j)]
                 rcopy(ref, ref, t_s.at[j, i], t_r.at[j, i], {"seq": relative(s, j)}).wait_recv()
@@ -596,15 +612,13 @@
             mlp_ref[l, 2 * i + core] = (normed * (1.0 + row(4)) + row(3)).astype(BF16)
             share(mlp_ref, l, i, g_s, g_r).start()
 
-            @pl.when((i == 0) & (l == 0))
+            @pl.when((turn == 0) & (l == 0))
             def _():
                 forward_weights(0, 2)
-                forward_weights(0, 3)
-
-            @pl.when(i == 0)
+
+            @pl.when(turn == 0)
             def _():
                 ready(l, 2)
-                ready(l, 3)
 
             def both(w, carry):
                 @pl.when(w == 1)
@@ -615,6 +629,15 @@
                 up = mm(mlp_ref[l, t], matrix(wu_ref, l)) + bu_ref[l]
                 up_ref[l, t] = up
                 act = gelu_parts(up)[0].astype(BF16)
+
+                @pl.when((turn == 0) & (w == 0) & (l == 0))
+                def _():
+                    forward_weights(0, 3)
+
+                @pl.when((turn == 0) & (w == 0))
+                def _():
+                    ready(l, 3)
+
                 part = mm(act, matrix(wd_ref, l))
 
                 @pl.when(w == 0)
@@ -626,9 +649,9 @@
                     psend[i] = part
                     part_copy(i).start()
 
-                @pl.when((w == 0) & (i == 1))
+                @pl.when((w == 0) & (turn == 1))
                 def _():
-                    exchange(0)
+                    exchange(1 - i)
 
                 return carry
 
@@ -636,7 +659,7 @@
             return carry
 
         lax.fori_loop(0, 2, mlp, 0)
-        exchange(1)
+        exchange((1 + flip) % 2)
         save(l, 1, 2, 3, 7, 8, 9, 10, 11)
 
         @pl.when(l + 1 < layers)
@@ -735,11 +758,15 @@
         pltpu.VMEM((n, layers, width6 // 4), F32),
         pltpu.VMEM((n, layers, width6 // 4), F32),
         pltpu.VMEM((4, layers, width6 // 4), F32),
-    ] + [dma((n,))] * 6 + [dma((layers,))] * 2 + [dma((layers, 4, slow))] * 4 + [dma((2,))] * 2 + [dma((3, 2))] * 2 + [dma((2,))] * 6 + [dma((1,))] * 2 + [dma((3,))] * 2 + [dma((layers, 13))]
+    ] + [dma((n,))] * 6 + [dma((layers,))] * 2 + [dma((layers, 4, slow))] * 4 + [dma((2,))] * 2 + [dma((3, 2))] * 2 + [dma((2,))] * 6 + [dma((1,))] * 2 + [dma((3,))] * 2 + [dma((layers, 13))] + [
+        pltpu.VMEM(weights[i].shape, BF16) for i in (6, 4, 0, 8)
+    ] + [dma((4,))]
     return pl.pallas_call(
         functools.partial(forward_kernel, n),
         out_shape=outs,
-        in_specs=vmem_specs(12),
+        in_specs=[
+            pl.BlockSpec(memory_space=pl.ANY if i in (2, 6, 8, 10) else pltpu.VMEM) for i in range(12)
+        ],
         out_specs=tuple(vmem_specs(3) + [pl.BlockSpec(memory_space=pl.ANY)] * 13),
         scratch_shapes=scratch,
         compiler_params=pltpu.CompilerParams(
@@ -1029,6 +1056,11 @@
                 vec_ref[l, 2:3, :] = sums(g_mid * loaded[branch][...])
                 vec_ref[l, 6:7, :] = sums(g_branch.astype(F32))
 
+            @pl.when((step > 0) & (i == 1))
+            def _():
+                z_finish(l + 1, down)
+                z_finish(l + 1, upw)
+
             @pl.when(i == 1)
             def _():
                 tokens_out = jnp.concatenate([loaded[tok][t] for t in range(4)], axis=1)
@@ -1084,12 +1116,6 @@
         y_copy(l, outw).start()
         pair(0).wait_send()
 
-        @pl.when(step > 0)
-        def _():
-            z_finish(l + 1, down)
-            z_finish(l + 1, upw)
-            z_finish(l + 1, outw)
-
         z_start(l, down)
         for h in range(heads):
             for j, acc, scale in ((1, dk_acc, SCORE_SCALE), (2, dv_acc, 1.0)):
@@ -1105,7 +1131,11 @@
 
         load(wq, l).wait()
 
-        def back(i, carry):
+        flip = (1 - side) * ((step + 1) // layers)
+
+        def back(turn, carry):
+            i = (turn + flip) % 2
+
             def both(w, carry):
                 place(1 - w, i, mm_nt(gqkv_ref[2 * i + (core + 1 - w) % 2], matrix(wq)))
                 return carry
@@ -1132,6 +1162,7 @@
 
         @pl.when(step > 0)
         def _():
+            z_finish(l + 1, outw)
             z_finish(l + 1, qkvw)
             vec_spread(l + 1)
 
@@ -1311,12 +1342,8 @@
         for r in range(6):
             d = vec_ref[l, :, r, :]
             high = d.astype(BF16)
-            low = d - high.astype(F32)
-            mid = low.astype(BF16)
-            low = (low - mid.astype(F32)).astype(BF16)
-            ada_buf[l, :, r * width: (r + 1) * width] = (
-                mm_tn(cond_rows, high) + mm_tn(cond_rows, mid) + mm_tn(cond_rows, low)
-            )
+            low = (d - high.astype(F32)).astype(BF16)
+            ada_buf[l, :, r * width: (r + 1) * width] = mm_tn(cond_rows, high) + mm_tn(cond_rows, low)
         write(2, l, ada_buf, g_ada)
     for l in range(layers):
         for j in range(3):

time: 327 us -> 324 us (level)
  Pallas kernels: 323 us -> 319 us
where the time goes in v6:
time: 324 us
  Pallas kernels  319 us (98%)
  local copies, waits for them, and re-layouts  3.83 us (1%)
    pallas_call x1, Pallas kernels, backward(): pl.pallas_call(functools.partial(backward_kernel, n), out_shape=tuple(out...  160 us
    pallas_call x1, Pallas kernels, forward(): pl.pallas_call(functools.partial(forward_kernel, n), out_shape=outs, in_s...  151 us
    pallas_call x1, Pallas kernels, assemble(): pl.pallas_call(functools.partial(assemble_kernel, n), out_shape=tuple((sd...  8.42 us

profile of v6, /device:TPU:0, one launch (start us, length us, event | category | flops | bytes accessed | tf_op | source)
XLA Modules:
  0.0 323.9 jit_solution(1049549781251804154)
XLA Ops:
  0.6 151.4 %shard_map.228 = (bf16[256,768]{1,0:T(8,128)(2,1)}, f32[2,6,768]{2,1,0:T(8,128)}, f32[8,128]{1,0:T(8,128)}, bf16[2,8,96,576]{3,2,1,0:T(8,128)(2,1)}, bf16[2,2,8,...) custom-call(bf16[256,768]{1,0:T(8,128)(2,1)} %bitcast.6, ...), custom_call_target="tpu_custom_call" | custom-call | tf_op jit(solution)/shard_map/pallas_call | solution.py:764
  152.0 159.6 %shard_map.229 = (f32[256,768]{1,0:T(8,128)}, f32[2,8,8,768]{3,2,1,0:T(8,128)}, f32[2,4,2,768]{3,2,1,0:T(2,128)}, f32[1,768]{1,0:T(1,128)}, bf16[2,4,96,768]{3,2...) custom-call(bf16[256,768]{1,0:T(8,128)(2,1)} %bitcast.5, ...), custom_call_target="tpu_custom_call" | custom-call | tf_op jit(solution)/shard_map/pallas_call | solution.py:1303
  311.7 8.4 %shard_map.230 = (f32[1,768]{1,0:T(1,128)}, f32[2,576]{1,0:T(2,128)}, f32[2,192]{1,0:T(2,128)}, f32[2,96]{1,0:T(2,128)}, f32[2,384]{1,0:T(2,128)}, /*index=5*/f3...) custom-call(f32[2,8,8,768]{3,2,1,0:T(8,128)} %get-tuple-element.64.v, ...), custom_call_target="tpu_custom_call" | custom-call | tf_op jit(solution)/shard_map/pallas_call | solution.py:1390
  320.1 1.8 copy.28
  321.9 2.1 copy.29

commit v7 on v6

--- a/solution.py
+++ b/solution.py
@@ -504,6 +504,10 @@
                 )
 
         def enter(i, carry):
+            @pl.when((l > 0) & (i == 1))
+            def _():
+                forward_weights(l, 2)
+
             @pl.when(l > 0)
             def _():
                 over(i).wait_recv()
@@ -544,7 +548,6 @@
         @pl.when(l > 0)
         def _():
             save(l - 1, 12)
-            forward_weights(l, 2)
 
         def attend_block(t, carry):
             outs = []
@@ -572,16 +575,16 @@
             def _():
                 forward_weights(0, 1)
 
+            @pl.when((t == 3) & (l > 0))
+            def _():
+                forward_weights(l, 3)
+
             return carry
 
         lax.fori_loop(0, 4, attend_block, 0)
         save(l, 0, 4, 5, 6)
         ready(l, 1)
         half_copy(l).start()
-
-        @pl.when(l > 0)
-        def _():
-            forward_weights(l, 3)
 
         half_arrived(l)
 
@@ -653,6 +656,10 @@
                 def _():
                     exchange(1 - i)
 
+                @pl.when((w == 0) & (turn == 1) & (l + 1 < layers))
+                def _():
+                    forward_weights(1, 0)
+
                 return carry
 
             lax.fori_loop(0, 2, both, 0)
@@ -664,7 +671,6 @@
 
         @pl.when(l + 1 < layers)
         def _():
-            forward_weights(1, 0)
             forward_weights(1, 1)
 
         half_copy(l).wait_send()
@@ -1005,6 +1011,8 @@
         def _():
             load(xs, l).start()
             vec_start(l + 1)
+            z_start(l + 1, outw)
+            z_start(l + 1, qkvw)
 
         whole = lambda ref: ref[...].reshape(4 * block, ref.shape[2])
         grads[down][...] = mm_tn(act_ref[...], whole(gf_ref)).astype(BF16).reshape(grads[down].shape)
@@ -1013,11 +1021,6 @@
         y_copy(l, upw).start()
 
         load(attn, l).start()
-
-        @pl.when(step > 0)
-        def _():
-            z_start(l + 1, outw)
-            z_start(l + 1, qkvw)
 
         @pl.when(l > 0)
         def _():
@@ -1060,6 +1063,7 @@
             def _():
                 z_finish(l + 1, down)
                 z_finish(l + 1, upw)
+                vec_spread(l + 1)
 
             @pl.when(i == 1)
             def _():
@@ -1164,7 +1168,6 @@
         def _():
             z_finish(l + 1, outw)
             z_finish(l + 1, qkvw)
-            vec_spread(l + 1)
 
         return carry
 

time: 324 us -> 317 us (0.978)
  Pallas kernels: 319 us -> 312 us
    pallas_call x1, Pallas kernels: 160 us -> 156 us  [backward(): pl.pallas_call(functools.partial(backward_kernel, n), out_shape=tuple(out...]
    pallas_call x1, Pallas kernels: 151 us -> 148 us  [forward(): pl.pallas_call(functools.partial(forward_kernel, n), out_shape=outs, in_s...]
where the time goes in v7:
time: 317 us
  Pallas kernels  312 us (98%)
  local copies, waits for them, and re-layouts  3.83 us (1%)
    pallas_call x1, Pallas kernels, backward(): pl.pallas_call(functools.partial(backward_kernel, n), out_shape=tuple(out...  156 us
    pallas_call x1, Pallas kernels, forward(): pl.pallas_call(functools.partial(forward_kernel, n), out_shape=outs, in_s...  148 us
    pallas_call x1, Pallas kernels, assemble(): pl.pallas_call(functools.partial(assemble_kernel, n), out_shape=tuple((sd...  8.42 us

profile of v7, /device:TPU:0, one launch (start us, length us, event | category | flops | bytes accessed | tf_op | source)
XLA Modules:
  0.0 316.7 jit_solution(7417577102351014990)
XLA Ops:
  0.6 148.1 %shard_map.228 = (bf16[256,768]{1,0:T(8,128)(2,1)}, f32[2,6,768]{2,1,0:T(8,128)}, f32[8,128]{1,0:T(8,128)}, bf16[2,8,96,576]{3,2,1,0:T(8,128)(2,1)}, bf16[2,2,8,...) custom-call(bf16[256,768]{1,0:T(8,128)(2,1)} %bitcast.6, ...), custom_call_target="tpu_custom_call" | custom-call | tf_op jit(solution)/shard_map/pallas_call | solution.py:770
  148.7 155.7 %shard_map.229 = (f32[256,768]{1,0:T(8,128)}, f32[2,8,8,768]{3,2,1,0:T(8,128)}, f32[2,4,2,768]{3,2,1,0:T(2,128)}, f32[1,768]{1,0:T(1,128)}, bf16[2,4,96,768]{3,2...) custom-call(bf16[256,768]{1,0:T(8,128)(2,1)} %bitcast.5, ...), custom_call_target="tpu_custom_call" | custom-call | tf_op jit(solution)/shard_map/pallas_call | solution.py:1306
  304.5 8.4 %shard_map.230 = (f32[1,768]{1,0:T(1,128)}, f32[2,576]{1,0:T(2,128)}, f32[2,192]{1,0:T(2,128)}, f32[2,96]{1,0:T(2,128)}, f32[2,384]{1,0:T(2,128)}, /*index=5*/f3...) custom-call(f32[2,8,8,768]{3,2,1,0:T(8,128)} %get-tuple-element.64.v, ...), custom_call_target="tpu_custom_call" | custom-call | tf_op jit(solution)/shard_map/pallas_call | solution.py:1393
  312.9 1.8 copy.28
  314.7 2.1 copy.29
